TPU v7x, 8 devices: a whole 2x2x1 slice. The times are simulated.
8 devices in a mesh: dp: 1 (over z), ep: 8 (over y, x, core).
Axes of the slice: x: 2, y: 2, z: 1, core: 2. Of those that a mesh axis runs over, the one named last changes fastest.
Arguments:
- x_in: bfloat16 [512, 1536], P(('dp', 'ep'))
- expert_ids: int32 [512, 8], P(('dp', 'ep'))
- gate_val: float32 [512, 8], P(('dp', 'ep'))
- w_gate: bfloat16 [128, 1536, 512], P('ep')
- w_up: bfloat16 [128, 1536, 512], P('ep')
- w_down: bfloat16 [128, 512, 1536], P('ep')
- old_map: int32 [128], replicated
- mig_src: int32 [2], replicated
- mig_dst: int32 [2], replicated
Outputs:
- output 1: bfloat16 [512, 1536], P(('dp', 'ep'))
- output 2: bfloat16 [128, 1536, 512], P('ep')
- output 3: bfloat16 [128, 1536, 512], P('ep')
- output 4: bfloat16 [128, 512, 1536], P('ep')
All inputs are finite; a program needn't handle non-finite values.
Results may differ from a plain program's by a relative error of at most 0.001.
Values are sent between devices in bfloat16 or wider.
A program may use at most 1 GiB of HBM per device.

v0:
```python
import jax
import jax.numpy as jnp
from jax import lax
from jax.sharding import PartitionSpec as P


def solution(mesh):
    groups = mesh.shape['ep']

    def migrate(w_gate, w_up, w_down, mig_src, mig_dst):
        num_slots = w_gate.shape[0]
        my_index = lax.axis_index('ep')
        is_source = (mig_src // num_slots) == my_index
        src_local = mig_src % num_slots

        def pack_src(weights):
            gathered = jnp.take(weights, src_local, axis=0)
            return jnp.where(is_source[:, None, None], gathered, jnp.zeros_like(gathered))

        moved_w = lax.psum((pack_src(w_gate), pack_src(w_up), pack_src(w_down)), 'ep')
        slot_ids = my_index * num_slots + jnp.arange(num_slots)
        dst_match = slot_ids[:, None] == mig_dst[None, :]
        incoming = jnp.any(dst_match, axis=1)
        move_pick = jnp.sum(jnp.where(dst_match, jnp.arange(mig_dst.shape[0])[None, :], 0), axis=1)

        def place_dst(weights, arrived):
            return jnp.where(incoming[:, None, None], jnp.take(arrived, move_pick, axis=0), weights)

        return place_dst(w_gate, moved_w[0]), place_dst(w_up, moved_w[1]), place_dst(w_down, moved_w[2])

    def moe_local(x_loc, expert_ids, gate_val, w_gate, w_up, w_down, slot_map):
        tokens, top_k = expert_ids.shape
        num_slots = w_gate.shape[0]
        model = x_loc.shape[1]
        experts = groups * num_slots
        capacity = 2 * tokens * top_k // experts
        buf_width = experts * capacity
        slot_of = jnp.argsort(slot_map)
        target = slot_of[expert_ids]
        hit_mask = (target.reshape(-1)[:, None] == jnp.arange(experts)[None, :]).astype(jnp.int32)
        rank_in = jnp.sum(jnp.cumsum(hit_mask, axis=0) * hit_mask, axis=1) - 1
        slot_pos = target * capacity + rank_in.reshape(tokens, top_k)
        chosen = slot_pos[:, :, None] == jnp.arange(buf_width)[None, None, :]
        spread = jnp.any(chosen, axis=1).astype(jnp.bfloat16)
        gate_rows = jnp.sum(jnp.where(chosen, gate_val[:, :, None], 0.0), axis=(0, 1))
        send_rows = jnp.einsum('tp,td->pd', spread, x_loc, preferred_element_type=jnp.float32).astype(jnp.bfloat16)
        recv_rows = lax.all_to_all(send_rows.reshape(groups, num_slots, capacity, model), 'ep', 0, 2, tiled=True)
        recv_rows = recv_rows.reshape(num_slots, groups * capacity, model)
        recv_gate = lax.all_to_all(gate_rows.reshape(groups, num_slots, capacity), 'ep', 0, 2, tiled=True)
        recv_gate = recv_gate.reshape(num_slots, groups * capacity)
        act_g = jnp.einsum('srd,sdf->srf', recv_rows, w_gate, preferred_element_type=jnp.float32)
        act_u = jnp.einsum('srd,sdf->srf', recv_rows, w_up, preferred_element_type=jnp.float32)
        hidden = (jax.nn.silu(act_g) * act_u).astype(jnp.bfloat16)
        expert_out = jnp.einsum('srf,sfd->srd', hidden, w_down, preferred_element_type=jnp.float32)
        scaled = (expert_out * recv_gate[:, :, None]).astype(jnp.bfloat16)
        back_rows = lax.all_to_all(scaled.reshape(1, num_slots, groups * capacity, model), 'ep', 2, 0, tiled=True)
        back_rows = back_rows.reshape(buf_width, model)
        expert_sum = jnp.einsum('tp,pd->td', spread, back_rows, preferred_element_type=jnp.float32)
        return (x_loc.astype(jnp.float32) + expert_sum).astype(jnp.bfloat16)

    def local_step(x_loc, expert_ids, gate_val, w_gate, w_up, w_down, old_map, mig_src, mig_dst):
        new_gate, new_up, new_down = migrate(w_gate, w_up, w_down, mig_src, mig_dst)
        new_map = old_map.at[mig_dst].set(old_map[mig_src])
        y_out = moe_local(x_loc, expert_ids, gate_val, new_gate, new_up, new_down, new_map)
        return y_out, new_gate, new_up, new_down

    row_spec = P(('dp', 'ep'), None)
    slot_spec = P('ep', None, None)
    return jax.shard_map(local_step, mesh=mesh, in_specs=(row_spec, row_spec, row_spec, slot_spec, slot_spec, slot_spec, P(), P(), P()), out_specs=(row_spec, slot_spec, slot_spec, slot_spec), check_vma=False)
```

profile of v0, /device:TPU:0, one launch (start us, length us, event | category | flops | bytes accessed | tf_op | source)
XLA Modules:
  0.0 408.8 jit_solution(17286185961304590614)
XLA Ops:
  7.2 0.0 all-reduce.3.cloned.1.call-start
  7.2 0.7 copy.70
  7.9 0.7 compare_and_fusion.1
  8.6 10.6 %gather_fusion.2 = bf16[2,512,1536]{2,1,0:T(8,128)(2,1)} fusion(bf16[16,512,1536]{2,1,0:T(8,128)(2,1)} %param.18, s32[1024]{0:T(1024)S(1)} %pad_clamp_fusion.2), kind=kCustom, calls=%fused_computation.6 | custom fusion | bytes 6291464 | tf_op jit(solution)/shard_map/jit(_take)/gather | solution.py:17
  19.1 8.9 %gather_fusion.6 = bf16[2,1536,512]{2,1,0:T(8,128)(2,1)S(1)} fusion(bf16[16,1536,512]{2,1,0:T(8,128)(2,1)} %param.17, s32[1024]{0:T(1024)S(1)} %pad_clamp_fusion.2), kind=kCustom, calls=%fused_computation.2.clone | custom fusion | bytes 6291464 | tf_op jit(solution)/shard_map/jit(_take)/gather | solution.py:17
  28.0 10.6 %gather_fusion.4 = bf16[2,1536,512]{2,1,0:T(8,128)(2,1)} fusion(bf16[16,1536,512]{2,1,0:T(8,128)(2,1)} %param.16, s32[1024]{0:T(1024)S(1)} %pad_clamp_fusion.2), kind=kCustom, calls=%fused_computation.clone | custom fusion | bytes 6291464 | tf_op jit(solution)/shard_map/jit(_take)/gather | solution.py:17
  38.6 0.0 copy-start.1
  38.6 4.1 %select_select_fusion.5 = bf16[2,512,1536]{2,1,0:T(8,128)(2,1)} fusion(bf16[2,512,1536]{2,1,0:T(8,128)(2,1)} %gather_fusion.2, pred[2]{0:T(512)(128)(4,1)S(1)} %get-tuple-element.11, pred[2]{0:T(512)(128)(4,1)S(1)} %get-tuple-element.17), kind=kLoop, calls=%fused_computation.22 | loop fusion | flops 3145728 | bytes 6291460 | tf_op jit(solution)/shard_map/jit(_where)/select_n | solution.py:18
  42.7 0.0 copy-done.1
  42.7 3.4 select_select_fusion.3
  46.2 0.0 copy-start.4
  46.2 0.0 copy-start.3
  46.2 0.0 copy-start.5
  46.2 0.0 copy-start.6
  46.2 0.0 all-reduce.3.cloned.1.call-update
  46.2 0.7 copy-done.4
  46.9 0.1 copy.41
  46.9 0.1 reshape.146
  47.0 0.0 copy-done.3
  47.0 0.1 copy.45
  47.1 0.0 copy-done.5
  47.2 0.6 gather_fusion
  47.8 0.0 copy-done.6
  47.8 0.6 scatter_fusion
  48.4 2.5 sort.17
  50.9 0.0 copy-start.2
  50.9 3.3 gather_fusion.1
  54.3 0.1 copy.42
  54.4 0.2 fusion.15
  54.7 0.2 fusion.14
  55.0 0.1 reshape.189
  55.1 0.3 select_reduce_fusion
  55.4 0.1 reshape.101
  55.4 0.1 copy.46
  55.5 0.7 reshape.198
  56.2 4.3 %all-to-all-start.1 = ((f32[8,1,128]{2,1,0:T(1,128)}), f32[8,1,128]{2,1,0:T(1,128)S(1)}, u32[]{:S(2)}, u32[]{:S(2)}) async-start(f32[8,1,128]{2,1,0:T(1,128)} %reshape.198), calls=%async_computation.1 | async-start | bytes 8192 | tf_op jit(solution)/shard_map/all_to_all | solution.py:49
  60.5 0.1 fusion.18
  60.6 0.1 compare_reduce_fusion
  60.7 0.7 fusion.8
  61.4 0.0 copy-done.2
  61.4 2.7 convolution_convert_fusion
  64.2 1.0 all-to-all-done.1
  65.1 3.4 all-to-all-start
  68.5 0.5 broadcast.219
  69.0 0.7 reduce
  69.7 0.1 reshape.199
  69.8 0.1 copy.47
  69.8 139.3 %all-reduce.3.cloned.1.call-done = (bf16[2,512,1536]{2,1,0:T(8,128)(2,1)}, bf16[2,1536,512]{2,1,0:T(8,128)(2,1)}, bf16[2,1536,512]{2,1,0:T(8,128)(2,1)}) async-done(((bf16[2,512,1536]{2,1,0:T(8,128)(2,1)}, bf16[2,1536,512]{2,1,0:T(8,128)(2,1)}, bf16[2,1536,512]{2,1,0:T(8,128)(2,1)}), (bf16[2,512,1536]{2,1,0:T(8,128)(2,1)}, bf16[2,1536,512]{2,1,0:T(8,128)(2,1)}, ...) | async-done | bytes 9437200 | tf_op jit(solution)/shard_map/psum | solution.py:20
  209.2 11.9 %gather_fusion.5 = bf16[16,1536,512]{2,1,0:T(8,128)(2,1)} fusion(bf16[2,1536,512]{2,1,0:T(8,128)(2,1)} %get-tuple-element.9, s32[1024]{0:T(1024)S(1)} %pad_clamp_fusion.1), kind=kCustom, calls=%fused_computation.1.clone | custom fusion | bytes 50331712 | tf_op jit(solution)/shard_map/jit(_take)/gather | solution.py:27
  221.1 0.0 copy-start
  221.1 12.0 %gather_fusion.7 = bf16[16,1536,512]{2,1,0:T(8,128)(2,1)} fusion(bf16[2,1536,512]{2,1,0:T(8,128)(2,1)} %get-tuple-element.10, s32[1024]{0:T(1024)S(1)} %pad_clamp_fusion.1), kind=kCustom, calls=%fused_computation.3.clone | custom fusion | bytes 50331712 | tf_op jit(solution)/shard_map/jit(_take)/gather | solution.py:27
  233.1 0.0 copy-done
  233.1 10.0 %gather_fusion.3 = bf16[16,512,1536]{2,1,0:T(8,128)(2,1)} fusion(bf16[2,512,1536]{2,1,0:T(8,128)(2,1)S(1)} %copy-done, s32[1024]{0:T(1024)S(1)} %pad_clamp_fusion), kind=kCustom, calls=%fused_computation.7 | custom fusion | bytes 50331712 | tf_op jit(solution)/shard_map/jit(_take)/gather | solution.py:27
  243.1 49.1 %select_select_fusion = (bf16[16,1536,512]{2,1,0:T(8,128)(2,1)}, bf16[16,1536,512]{2,1,0:T(8,128)(2,1)}) fusion(bf16[16,1536,512]{2,1,0:T(8,128)(2,1)} %param.17, bf16[16,1536,512]{2,1,0:T(8,128)(2,1)} %gather_fusion.7, pred[16]{0:T(512)(128)(4,1)S(1)} %compare_and_fusion, pred[16]{0:T(512)(128)(4,1)S(1)} %compare_reduce_fusion, ...), kind=kLoop, calls=%fused_computation.9 | loop fusion | flops 50331648 | bytes 150994976 | tf_op jit(solution)/shard_map/jit(_where)/select_n | solution.py:27
  292.3 26.0 %select_select_fusion.2 = bf16[16,512,1536]{2,1,0:T(8,128)(2,1)} fusion(bf16[16,512,1536]{2,1,0:T(8,128)(2,1)} %param.18, bf16[16,512,1536]{2,1,0:T(8,128)(2,1)} %gather_fusion.3, pred[16]{0:T(512)(128)(4,1)S(1)} %compare_and_fusion, pred[16]{0:T(512)(128)(4,1)S(1)} %compare_reduce_fusion), kind=kLoop, calls=%fused_computation.11 | loop fusion | flops 25165824 | bytes 75497504 | tf_op jit(solution)/shard_map/jit(_where)/select_n | solution.py:27
  318.3 0.0 all-to-all-done
  318.3 15.0 %fusion.3 = f32[16,64,512]{2,1,0:T(8,128)} fusion(bf16[16,1536,512]{2,1,0:T(8,128)(2,1)} %get-tuple-element.14, bf16[8,16,8,1536]{3,2,1,0:T(8,128)(2,1)} %all-to-all-done), kind=kOutput, calls=%fused_computation.17 | convolution fusion | flops 1610612736 | bytes 30408704 | tf_op jit(solution)/shard_map/srd,sdf->srf/dot_general | solution.py:51
  333.2 24.4 %fusion = bf16[1,16,64,1536]{3,2,1,0:T(8,128)(2,1)S(1)} fusion(bf16[16,512,1536]{2,1,0:T(8,128)(2,1)} %select_select_fusion.2, f32[16,64]{1,0:T(8,128)S(1)} %copy.47, f32[16,64,512]{2,1,0:T(8,128)} %fusion.3, bf16[16,1536,512]{2,1,0:T(8,128)(2,1)} %get-tuple-element.13, bf16[8,16,8,1536]{3,2,1,0:T(8,128)(2,1)} %all-to-all-done), kind=kOutput, calls=%fused_computation.14 | convolution fusion | flops 3227516928 | bytes 58724352 | tf_op jit(solution)/shard_map/srf,sfd->srd/dot_general | solution.py:54
  357.7 1.7 copy.48
  359.4 39.1 %all_to_all.45 = bf16[1,16,64,1536]{3,1,0,2:T(8,128)(2,1)S(1)} all-to-all(bf16[1,16,64,1536]{3,1,0,2:T(8,128)(2,1)S(1)} %copy.48), channel_id=1, replica_groups=mesh['dp'=1,'ep'=8] {'ep'}, dimensions={2} | all-to-all | bytes 6291456 | tf_op jit(solution)/shard_map/all_to_all | solution.py:56
  398.6 1.7 copy.64
  400.3 0.3 copy.50
  400.6 1.3 fusion.7
  (21 shorter events, 0.2 us)
Async XLA Ops:
  7.2 202.0 %all-reduce.3.cloned.1.call-start = ((), (), s32[]{:S(2)}) async-start(), calls=%async_computation.3 | async-start | bytes 18874368 | tf_op jit(solution)/shard_map/psum | solution.py:20
  38.6 4.1 %copy-start.1 = (bf16[2,1536,512]{2,1,0:T(8,128)(2,1)S(1)}, bf16[2,1536,512]{2,1,0:T(8,128)(2,1)}, u32[]{:S(2)}) copy-start(bf16[2,1536,512]{2,1,0:T(8,128)(2,1)} %gather_fusion.4) | copy-start | bytes 9437188
  46.2 0.7 copy-start.4
  46.2 0.9 copy-start.3
  46.2 1.0 copy-start.5
  46.2 1.6 copy-start.6
  50.9 10.5 %copy-start.2 = (bf16[64,1536]{1,0:T(8,128)(2,1)S(1)}, bf16[64,1536]{1,0:T(8,128)(2,1)}, u32[]{:S(2)}) copy-start(bf16[64,1536]{1,0:T(8,128)(2,1)} %param.13) | copy-start | bytes 589828
  56.2 8.9 %all-to-all-start.1 = ((f32[8,1,128]{2,1,0:T(1,128)}), f32[8,1,128]{2,1,0:T(1,128)S(1)}, u32[]{:S(2)}, u32[]{:S(2)}) async-start(f32[8,1,128]{2,1,0:T(1,128)} %reshape.198), calls=%async_computation.1 | async-start | bytes 8192 | tf_op jit(solution)/shard_map/all_to_all | solution.py:49
  65.1 253.1 %all-to-all-start = ((bf16[8,16,8,1536]{3,2,1,0:T(8,128)(2,1)}), bf16[8,16,8,1536]{3,2,1,0:T(8,128)(2,1)}, u32[]{:S(2)}, u32[]{:S(2)}) async-start(bf16[8,16,8,1536]{3,2,1,0:T(8,128)(2,1)} %bitcast.4), calls=%async_computation | async-start | bytes 6291456 | tf_op jit(solution)/shard_map/all_to_all | solution.py:47
  221.1 12.0 %copy-start = (bf16[2,512,1536]{2,1,0:T(8,128)(2,1)S(1)}, bf16[2,512,1536]{2,1,0:T(8,128)(2,1)}, u32[]{:S(2)}) copy-start(bf16[2,512,1536]{2,1,0:T(8,128)(2,1)} %get-tuple-element.8) | copy-start | bytes 9437188
Sparse Core Ops, SparseCore 0:
  46.3 162.7 all-reduce.2
where the time goes:
time: 409 us
  waiting for transfers between devices  140 us (34%)
  other arithmetic  88.3 us (22%)
  local copies, waits for them, and re-layouts  75.6 us (18%)
  matrix products  43.4 us (11%)
  blocking collectives  39.1 us (10%)
  between operations  14.2 us (3%)
  starting transfers between devices  7.69 us (2%)
    psum x1, waiting for transfers between devices, migrate(): lax.psum((pack_src(w_gate), pack_src(w_up), pack_src(w_down)), 'ep')  139 us
    select_n x2, other arithmetic, place_dst(): jnp.where(incoming[:, None, None], jnp.take(arrived, move_pick, axis=0),...  75.2 us
    all_to_all x1, blocking collectives, moe_local(): lax.all_to_all(scaled.reshape(1, num_slots, groups * capacity, model), 'e...  39.1 us
    gather x3, local copies, waits for them, and re-layouts, place_dst(): jnp.take(arrived, move_pick, axis=0)  33.9 us
    gather x3, local copies, waits for them, and re-layouts, pack_src(): gathered = jnp.take(weights, src_local, axis=0)  30 us
    dot_general x1, matrix products, moe_local(): jnp.einsum('srf,sfd->srd', hidden, w_down, preferred_element_type=jnp.flo...  24.4 us
    dot_general x1, matrix products, moe_local(): jnp.einsum('srd,sdf->srf', recv_rows, w_gate, preferred_element_type=jnp....  15 us
  transfers between devices with their start and end apart: 3, of which 2 were waited for; matrix products, arithmetic and copies ran while one was open for 30% of the time, Pallas kernels for 0%

commit v1 on v0

v1 whole, which is shorter than its diff:
```python
import functools

import jax
import jax.numpy as jnp
from jax import lax
from jax.experimental import pallas as pl
from jax.experimental.pallas import tpu as pltpu
from jax.sharding import PartitionSpec as P

MESH = pl.DeviceIdType.MESH
BF16, F32 = jnp.bfloat16, jnp.float32
ANY = pl.BlockSpec(memory_space=pl.ANY)
VMEM = pl.BlockSpec(memory_space=pltpu.VMEM)
SMEM = pl.BlockSpec(memory_space=pltpu.SMEM)
LIMIT = 62 * 1024 * 1024
RING = 12
LAG = 4


def places():
    me = lax.axis_index('ep')
    core, chip = me % 2, me // 2
    x, y = chip % 2, chip // 2
    sib = chip * 2 + 1 - core
    chips = ((1 - y) * 2 + 1 - x, y * 2 + 1 - x, (1 - y) * 2 + x)
    return me, core, chip, sib, chips


def enter(partners):
    barrier = pltpu.get_barrier_semaphore()
    for dev in partners:
        pl.semaphore_signal(barrier, inc=1, device_id={'ep': dev}, device_id_type=MESH)
    pl.semaphore_wait(barrier, len(partners))


def remote(src, dst, send, recv, dev):
    return pltpu.make_async_remote_copy(src, dst, send, recv, device_id={'ep': dev}, device_id_type=MESH)


def dispatch_kernel(x_ref, meta_ref, xall, mall, send, recv):
    me, core, chip, sib, chips = places()
    peers = [c * 2 + core for c in chips]
    enter(peers + [sib])

    def pair(k, src_x, src_m, block, dev):
        return (remote(src_x, xall.at[block], send.at[2 * k], recv.at[2 * k], dev),
                remote(src_m, mall.at[block], send.at[2 * k + 1], recv.at[2 * k + 1], dev))

    first = [pair(k, x_ref, meta_ref, me, peers[k]) for k in range(3)]
    first.append(pair(3, x_ref, meta_ref, me, sib))
    for group in first:
        for copy in group:
            copy.start()
    xall[pl.ds(me, 1)] = x_ref[...][None]
    mall[pl.ds(me, 1)] = meta_ref[...][None]
    second = []
    for k in (1, 2, 0):
        for copy in first[k]:
            copy.wait_recv()
        fwd = pair(4 + k, xall.at[peers[k]], mall.at[peers[k]], peers[k], sib)
        for copy in fwd:
            copy.start()
        second.append(fwd)
    for copy in first[3]:
        copy.wait_recv()
    for group in first:
        for copy in group:
            copy.wait_send()
    for group in second:
        for copy in group:
            copy.wait()


def gate_up_kernel(old_map, x_ref, mall, wg, wu, wg_new, wu_new, z_ref, at_ref, gr_ref,
                   bg, bu, xg, a_ref, pos, gsc, meta, sem_in, sem_out):
    me = lax.axis_index('ep')
    slots = wg.shape[0]
    devs, tok = x_ref.shape[0] // 64, 64
    total = devs * tok
    cap = 8
    rows = devs * cap

    def load(s):
        b = lax.rem(s, RING)
        return (pltpu.make_async_copy(wg.at[s], bg.at[b], sem_in.at[0, b]),
                pltpu.make_async_copy(wu.at[s], bu.at[b], sem_in.at[1, b]))

    def drain(s):
        b = lax.rem(s, RING)
        return (pltpu.make_async_copy(bg.at[b], wg_new.at[s], sem_out.at[0, b]),
                pltpu.make_async_copy(bu.at[b], wu_new.at[s], sem_out.at[1, b]))

    for s in range(RING):
        for copy in load(s):
            copy.start()

    lane = lax.broadcasted_iota(jnp.int32, (16, 128), 1)
    for p in range(devs // 2):
        other = pltpu.roll(mall[2 * p + 1], 64, axis=1)
        meta[:, pl.ds(128 * p, 128)] = jnp.where(lane < 64, mall[2 * p], other)
    ids = meta[0:8, :]
    gates = meta[8:16, :]
    hits, gs = [], []
    for j in range(slots):
        same = ids == old_map[me * slots + j].astype(F32)
        hits.append(jnp.sum(jnp.where(same, 1.0, 0.0), axis=0, keepdims=True))
        gs.append(jnp.sum(jnp.where(same, gates, 0.0), axis=0, keepdims=True))
    hit = jnp.concatenate(hits, axis=0)
    gsc[...] = jnp.concatenate(gs, axis=0)
    t_row = lax.broadcasted_iota(jnp.int32, (total, total), 0)
    t_col = lax.broadcasted_iota(jnp.int32, (total, total), 1)
    before = jnp.where((t_row < t_col) & (t_row // tok == t_col // tok), 1.0, 0.0).astype(BF16)
    rank = jnp.dot(hit.astype(BF16), before, preferred_element_type=F32)
    owner = (lax.broadcasted_iota(jnp.int32, (slots, total), 1) // tok * cap).astype(F32)
    pos[...] = jnp.where(hit > 0.5, rank + owner, -1.0)
    post = jnp.transpose(jnp.concatenate([pos[...], jnp.full((128 - slots, total), -1.0, F32)], axis=0))
    wide = lax.broadcasted_iota(jnp.int32, (total, 128), 1)
    for p in range(slots // 2):
        want = jnp.where(wide < rows, post[:, 2 * p:2 * p + 1], post[:, 2 * p + 1:2 * p + 2])
        at_ref[:, pl.ds(128 * p, 128)] = jnp.where(want == (wide % rows).astype(F32), 1.0, 0.0).astype(BF16)

    row_id = lax.broadcasted_iota(jnp.int32, (rows, total), 0).astype(F32)

    @pl.loop(0, slots)
    def _(j):
        r0 = pl.multiple_of(j * rows, rows)
        chosen = row_id == pos[pl.ds(j, 1), :]
        a_ref[pl.ds(r0, rows), :] = jnp.where(chosen, 1.0, 0.0).astype(BF16)
        g = jnp.sum(jnp.where(chosen, gsc[pl.ds(j, 1), :], 0.0), axis=1, keepdims=True)
        gr_ref[pl.ds(r0, rows), :] = jnp.broadcast_to(g, (rows, 128))

    @pl.loop(0, slots // 4)
    def _(q):
        r0 = pl.multiple_of(q * 4 * rows, 4 * rows)
        picked = jnp.dot(a_ref[pl.ds(r0, 4 * rows), :], x_ref[...], preferred_element_type=F32)
        xg[pl.ds(r0, 4 * rows), :] = picked.astype(BF16)

    @pl.loop(0, slots)
    def _(s):
        b = lax.rem(s, RING)
        for copy in load(s):
            copy.wait()
        for copy in drain(s):
            copy.start()
        r0 = pl.multiple_of(s * rows, rows)
        xs = xg[pl.ds(r0, rows), :]
        act_g = jnp.dot(xs, bg[b], preferred_element_type=F32)
        act_u = jnp.dot(xs, bu[b], preferred_element_type=F32)
        z_ref[pl.ds(r0, rows), :] = (jax.nn.silu(act_g) * act_u).astype(BF16)

        @pl.when((s >= LAG) & (s - LAG + RING < slots))
        def _():
            for copy in drain(s - LAG):
                copy.wait()
            for copy in load(s - LAG + RING):
                copy.start()

    for s in range(max(slots - RING, 0), slots):
        for copy in drain(s):
            copy.wait()


def down_kernel(z_ref, at_ref, gr_ref, wd, wd_new, out_ref, bd, c_ref, sem_in, sem_out):
    slots = wd.shape[0]
    rows = z_ref.shape[0] // slots

    def load(s):
        return pltpu.make_async_copy(wd.at[s], bd.at[s], sem_in.at[s])

    def drain(s):
        return pltpu.make_async_copy(bd.at[s], wd_new.at[s], sem_out.at[s])

    for s in range(slots):
        load(s).start()

    @pl.loop(0, slots)
    def _(s):
        load(s).wait()
        drain(s).start()
        r0 = pl.multiple_of(s * rows, rows)
        o = jnp.dot(z_ref[pl.ds(r0, rows), :], bd[s], preferred_element_type=F32)
        c_ref[pl.ds(r0, rows), :] = (o * gr_ref[pl.ds(r0, rows), 0:1]).astype(BF16)

    cols = 256

    @pl.loop(0, out_ref.shape[1] // cols)
    def _(n):
        c0 = pl.multiple_of(n * cols, cols)
        out_ref[:, pl.ds(c0, cols)] = jnp.dot(at_ref[...], c_ref[:, pl.ds(c0, cols)], preferred_element_type=F32)

    @pl.loop(0, slots)
    def _(s):
        drain(s).wait()


def combine_kernel(part, x_ref, y_ref, near, summed, far, send, recv):
    me, core, chip, sib, chips = places()
    peers = [c * 2 + core for c in chips]
    order = list(chips) + [chip]
    enter(peers + [sib])
    across = [remote(part.at[c * 2 + 1 - core], near.at[k], send.at[k], recv.at[k], sib) for k, c in enumerate(order)]
    for copy in across:
        copy.start()
    out = [remote(summed.at[k], far.at[k], send.at[4 + k], recv.at[4 + k], peers[k]) for k in range(3)]
    for k in range(4):
        across[k].wait_recv()
        summed[k] = part[order[k] * 2 + core] + near[k]
        if k >= 1:
            out[k - 1].start()
    acc = x_ref[...].astype(F32) + summed[3]
    for k in (1, 2, 0):
        out[k].wait_recv()
        acc = acc + far[k]
    y_ref[...] = acc.astype(BF16)
    for copy in across + out:
        copy.wait_send()


def patch_kernel(src, dst, half, other, wg, wu, wd, wg_old, wu_old, wd_old, wg_new, wu_new, wd_new, buf, sem):
    me = lax.axis_index('ep')
    core = me % 2
    slots = wg.shape[0]
    depth, width = wg.shape[1:]
    part = half.shape[0] * half.shape[1]
    here = [dst[i] // slots == me for i in range(2)]
    local = here[0] & here[1]

    def run(copies):
        for copy in copies:
            copy.start()
        for copy in copies:
            copy.wait()

    def put(slot):
        copies = [pltpu.make_async_copy(buf.at[pl.ds(0, depth)], wg_new.at[slot], sem.at[0]),
                  pltpu.make_async_copy(buf.at[pl.ds(depth, depth)], wu_new.at[slot], sem.at[1])]
        for b in range(depth // width):
            copies.append(pltpu.make_async_copy(buf.at[pl.ds(2 * depth + width * b, width)],
                                                wd_new.at[slot, :, pl.ds(width * b, width)], sem.at[2 + b]))
        run(copies)

    @pl.when((here[0] | here[1]) & jnp.logical_not(local))
    def _():
        slot = jnp.where(here[0], dst[0], dst[1]) % slots
        size = half.shape[1]
        copies = []
        for p in range(2):
            copies.append(pltpu.make_async_copy(
                half.at[p], buf.at[pl.ds(pl.multiple_of(core * part + p * size, 128), size)], sem.at[p]))
            copies.append(pltpu.make_async_copy(
                other.at[p], buf.at[pl.ds(pl.multiple_of((1 - core) * part + p * size, 128), size)], sem.at[2 + p]))
        run(copies)
        put(slot)

    @pl.when(local)
    def _():
        for i in range(2):
            s = src[i] % slots
            copies = [pltpu.make_async_copy(wg.at[s], buf.at[pl.ds(0, depth)], sem.at[0]),
                      pltpu.make_async_copy(wu.at[s], buf.at[pl.ds(depth, depth)], sem.at[1])]
            for b in range(depth // width):
                copies.append(pltpu.make_async_copy(wd.at[s, :, pl.ds(width * b, width)],
                                                    buf.at[pl.ds(2 * depth + width * b, width)], sem.at[2 + b]))
            run(copies)
            put(dst[i] % slots)


def solution(mesh):
    groups = mesh.shape['ep']
    chips = groups // 2
    to_sib = [(d, d + 1 - 2 * (d % 2)) for d in range(groups)]

    def flip(bit):
        return [(d, d + bit - 2 * bit * ((d // bit) % 2)) for d in range(groups)]

    to_x, to_y = flip(2), flip(4)

    def migrate(w_gate, w_up, w_down, mig_src, mig_dst):
        slots, depth, width = w_gate.shape
        me = lax.axis_index('ep')
        core, chip = me % 2, me // 2
        owner = mig_src // slots
        oc = owner // 2
        i_own = (owner[0] == me) | (owner[1] == me)
        chip_own = (oc[0] == chip) | (oc[1] == chip)
        loc = jnp.where(owner[0] == me, mig_src[0], mig_src[1]) % slots
        same_chip = oc[0] == oc[1]
        same_x, same_y = oc[0] % 2 == oc[1] % 2, oc[0] // 2 == oc[1] // 2
        down = lax.dynamic_index_in_dim(w_down, loc, 0, keepdims=False)
        mine = jnp.concatenate(
            [lax.dynamic_index_in_dim(w_gate, loc, 0, keepdims=False),
             lax.dynamic_index_in_dim(w_up, loc, 0, keepdims=False)]
            + [down[:, width * b:width * (b + 1)] for b in range(depth // width)], axis=0)
        mine = mine.reshape(4, 3 * depth // 4, width)
        near = lax.ppermute(lax.dynamic_slice_in_dim(mine, 2 - 2 * core, 2, 0), 'ep', to_sib)
        own = lax.dynamic_slice_in_dim(mine, 2 * core, 2, 0)
        held = jnp.where(i_own, own, near)
        rx1 = lax.ppermute(held[0], 'ep', to_x)
        ry1 = lax.ppermute(jnp.where(same_x, held[0], held[1]), 'ep', to_y)

        def second():
            rx2 = lax.ppermute(jnp.where(chip_own, held[1], ry1), 'ep', to_x)
            ry2 = lax.ppermute(jnp.where(chip_own, held[1], rx1), 'ep', to_y)
            along = jnp.where(same_y, jnp.stack([rx1, rx2]), jnp.where(same_x, jnp.stack([ry1, ry2]), jnp.stack([ry2, rx2])))
            other = lax.ppermute(jnp.where(same_chip, own, along), 'ep', to_sib)
            return jnp.where(same_chip, near, along), other

        return second()

    def local_step(x_loc, expert_ids, gate_val, w_gate, w_up, w_down, old_map, mig_src, mig_dst):
        tok, model = x_loc.shape
        slots, depth, width = w_gate.shape
        total = groups * tok
        rows = slots * groups * 8
        half, other = migrate(w_gate, w_up, w_down, mig_src, mig_dst)

        meta = jnp.concatenate([expert_ids.astype(F32).T, gate_val.T], axis=0)
        meta = jnp.pad(meta, ((0, 0), (0, 128 - tok)))
        xall, mall = pl.pallas_call(
            dispatch_kernel,
            out_shape=(jax.ShapeDtypeStruct((groups, tok, model), BF16), jax.ShapeDtypeStruct((groups, 16, 128), F32)),
            in_specs=[VMEM, VMEM], out_specs=(VMEM, VMEM),
            scratch_shapes=[pltpu.SemaphoreType.DMA((14,)), pltpu.SemaphoreType.DMA((14,))],
            compiler_params=pltpu.CompilerParams(collective_id=0, has_side_effects=True),
            cost_estimate=pl.CostEstimate(flops=8_000_000_000, bytes_accessed=2_000_000, transcendentals=0),
            name='dispatch',
        )(x_loc, meta)

        bytes_gu = 4 * 2 * slots * depth * width
        wg_new, wu_new, z, at, gr = pl.pallas_call(
            gate_up_kernel,
            out_shape=(jax.ShapeDtypeStruct(w_gate.shape, BF16), jax.ShapeDtypeStruct(w_up.shape, BF16),
                       jax.ShapeDtypeStruct((rows, width), BF16), jax.ShapeDtypeStruct((total, rows), BF16),
                       jax.ShapeDtypeStruct((rows, 128), F32)),
            in_specs=[SMEM, VMEM, VMEM, ANY, ANY], out_specs=(ANY, ANY, VMEM, VMEM, VMEM),
            scratch_shapes=[pltpu.VMEM((RING, depth, width), BF16), pltpu.VMEM((RING, depth, width), BF16),
                            pltpu.VMEM((rows, model), BF16), pltpu.VMEM((rows, total), BF16),
                            pltpu.VMEM((slots, total), F32), pltpu.VMEM((slots, total), F32),
                            pltpu.VMEM((16, total), F32),
                            pltpu.SemaphoreType.DMA((2, RING)), pltpu.SemaphoreType.DMA((2, RING))],
            compiler_params=pltpu.CompilerParams(vmem_limit_bytes=LIMIT),
            cost_estimate=pl.CostEstimate(flops=30_000_000_000, bytes_accessed=bytes_gu, transcendentals=0),
            name='gate_up',
        )(old_map, xall.reshape(total, model), mall, w_gate, w_up)

        wd_new, part = pl.pallas_call(
            down_kernel,
            out_shape=(jax.ShapeDtypeStruct(w_down.shape, BF16), jax.ShapeDtypeStruct((total, model), F32)),
            in_specs=[VMEM, VMEM, VMEM, ANY], out_specs=(ANY, VMEM),
            scratch_shapes=[pltpu.VMEM((slots, width, depth), BF16), pltpu.VMEM((rows, model), BF16),
                            pltpu.SemaphoreType.DMA((slots,)), pltpu.SemaphoreType.DMA((slots,))],
            compiler_params=pltpu.CompilerParams(vmem_limit_bytes=LIMIT),
            cost_estimate=pl.CostEstimate(flops=15_000_000_000, bytes_accessed=bytes_gu // 2, transcendentals=0),
            name='down',
        )(z, at, gr, w_down)

        y_out = pl.pallas_call(
            combine_kernel,
            out_shape=jax.ShapeDtypeStruct((tok, model), BF16),
            in_specs=[VMEM, VMEM], out_specs=VMEM,
            scratch_shapes=[pltpu.VMEM((4, tok, model), F32), pltpu.VMEM((4, tok, model), F32),
                            pltpu.VMEM((3, tok, model), F32),
                            pltpu.SemaphoreType.DMA((7,)), pltpu.SemaphoreType.DMA((7,))],
            compiler_params=pltpu.CompilerParams(collective_id=1, has_side_effects=True, vmem_limit_bytes=40 * 1024 * 1024),
            cost_estimate=pl.CostEstimate(flops=16_000_000_000, bytes_accessed=4_000_000, transcendentals=0),
            name='combine',
        )(part.reshape(groups, tok, model), x_loc)

        wg_new, wu_new, wd_new = pl.pallas_call(
            patch_kernel,
            out_shape=tuple(jax.ShapeDtypeStruct(w.shape, BF16) for w in (w_gate, w_up, w_down)),
            in_specs=[SMEM, SMEM] + [ANY] * 8, out_specs=(ANY, ANY, ANY),
            input_output_aliases={7: 0, 8: 1, 9: 2},
            scratch_shapes=[pltpu.VMEM((3 * depth, width), BF16), pltpu.SemaphoreType.DMA((5,))],
            cost_estimate=pl.CostEstimate(flops=3_000_000_000, bytes_accessed=9_000_000, transcendentals=0),
            name='patch',
        )(mig_src, mig_dst, half, other, w_gate, w_up, w_down, wg_new, wu_new, wd_new)
        return y_out, wg_new, wu_new, wd_new

    row_spec = P(('dp', 'ep'), None)
    slot_spec = P('ep', None, None)
    return jax.shard_map(local_step, mesh=mesh, in_specs=(row_spec, row_spec, row_spec, slot_spec, slot_spec, slot_spec, P(), P(), P()), out_specs=(row_spec, slot_spec, slot_spec, slot_spec), check_vma=False)
```

time: 409 us -> 171 us (0.42)
  waiting for transfers between devices: 140 us -> 0.02 us
  Pallas kernels: 0 us -> 119 us
  other arithmetic: 88.3 us -> 14.1 us
  local copies, waits for them, and re-layouts: 75.6 us -> 16.8 us
  matrix products: 43.4 us -> 0 us
  blocking collectives: 39.1 us -> 0 us
    psum x1 -> x0, waiting for transfers between devices: 139 us -> none  [migrate(): lax.psum((pack_src(w_gate), pack_src(w_up), pack_src(w_down)), 'ep')]
    pallas_call x0 -> x5, Pallas kernels: none -> 119 us  [the longest x1 36.3 us: local_step(): pl.pallas_call(gate_up_kernel, out_shape=(jax.ShapeDtypeStruct(w_gate.sha...]
    select_n x9 -> x5, other arithmetic: 82.7 us -> 13.5 us  [the longest x1 6.06 us: second(): other = lax.ppermute(jnp.where(same_chip, own, along), 'ep', to_sib)]
    gather x8 -> x0, local copies, waits for them, and re-layouts: 68 us -> none  [the longest x3 33.9 us: place_dst(): jnp.take(arrived, move_pick, axis=0)]
    dot_general x4 -> x0, matrix products: 43.4 us -> none  [the longest x1 24.4 us: moe_local(): jnp.einsum('srf,sfd->srd', hidden, w_down, preferred_element_type=jnp.flo...]
    all_to_all x1 -> x0, blocking collectives: 39.1 us -> none  [moe_local(): lax.all_to_all(scaled.reshape(1, num_slots, groups * capacity, model), 'e...]
    all_to_all x2 -> x0, starting transfers between devices: 7.65 us -> none  [the longest x1 4.3 us: moe_local(): lax.all_to_all(gate_rows.reshape(groups, num_slots, capacity), 'ep', 0, 2...]
    unnamed x19 -> x13, local copies, waits for them, and re-layouts: 2.18 us -> 9.54 us
  transfers between devices with their start and end apart: 3 -> 6, of which waited for: 2 -> 0; matrix products, arithmetic and copies ran while one was open for 30% -> 0% of each run, Pallas kernels for 0% -> 70%
where the time goes in v1:
time: 171 us; the launch traced here: 168 us
  Pallas kernels  119 us (70%)
  local copies, waits for them, and re-layouts  16.8 us (10%)
  other arithmetic  14.1 us (8%)
  between operations  11.5 us (7%)
  starting transfers between devices  7 us (4%)
    pallas_call x1, Pallas kernels, local_step(): pl.pallas_call(gate_up_kernel, out_shape=(jax.ShapeDtypeStruct(w_gate.sha...  36.3 us
    pallas_call x1, Pallas kernels, local_step(): pl.pallas_call(dispatch_kernel, out_shape=(jax.ShapeDtypeStruct((groups,...  36.2 us
    pallas_call x1, Pallas kernels, local_step(): pl.pallas_call(combine_kernel, out_shape=jax.ShapeDtypeStruct((tok, model...  23.1 us
    pallas_call x1, Pallas kernels, local_step(): pl.pallas_call(down_kernel, out_shape=(jax.ShapeDtypeStruct(w_down.shape,...  22.6 us
    unnamed x13, local copies, waits for them, and re-layouts  9.54 us
    select_n x1, other arithmetic, second(): other = lax.ppermute(jnp.where(same_chip, own, along), 'ep', to_sib)  6.06 us
  transfers between devices with their start and end apart: 6, of which 0 were waited for; matrix products, arithmetic and copies ran while one was open for 0% of the time, Pallas kernels for 70%

profile of v1, /device:TPU:0, one launch (start us, length us, event | category | flops | bytes accessed | tf_op | source)
XLA Modules:
  0.0 168.4 jit_solution(3765383706057220247)
XLA Ops:
  0.6 0.7 and_select_fusion
  1.3 1.3 fusion.4
  2.6 0.7 fusion.2
  5.3 1.5 dynamic-slice_bitcast_fusion
  6.8 2.7 %bitcast_dynamic-update-slice_fusion.1 = bf16[4608,512]{1,0:T(8,128)(2,1)} fusion(bf16[16,1536,512]{2,1,0:T(8,128)(2,1)} %wg.3, s32[]{:T(128)S(6)} %select_n.106), kind=kLoop, calls=%fused_computation.8 | loop fusion | bytes 3145732
  9.4 2.7 %bitcast_dynamic-update-slice_fusion = bf16[4608,512]{1,0:T(8,128)(2,1)} fusion(bf16[4608,512]{1,0:T(8,128)(2,1)} %bitcast_dynamic-update-slice_fusion.1, bf16[16,1536,512]{2,1,0:T(8,128)(2,1)} %wu.3, s32[]{:T(128)S(6)} %select_n.106), kind=kLoop, calls=%fused_computation.7 | loop fusion | bytes 3145732
  12.1 0.8 slice_dynamic-update-slice_fusion.2
  12.9 0.8 slice_dynamic-update-slice_fusion.1
  13.7 0.8 slice_dynamic-update-slice_fusion
  14.6 1.8 %constant_dynamic-slice_fusion = bf16[2,1152,512]{2,1,0:T(8,128)(2,1)S(1)} fusion(bf16[4,1152,512]{2,1,0:T(8,128)(2,1)} %bitcast.12, s32[]{:T(128)S(6)} %select_n.108), kind=kLoop, calls=%fused_computation.23 | loop fusion | bytes 4718596 | tf_op jit(solution)/shard_map/dynamic_slice | solution.py:295
  16.4 0.9 collective-permute-start
  21.9 0.0 collective-permute-done
  22.0 2.6 %broadcast_select_fusion = bf16[2,1152,512]{2,1,0:T(8,128)(2,1)S(1)} fusion(bf16[2,1152,512]{2,1,0:T(8,128)(2,1)} %collective-permute-done, pred[]{:T(512)S(6)} %or.6, bf16[4,1152,512]{2,1,0:T(8,128)(2,1)} %bitcast.12, s32[]{:T(128)S(6)} %select_n.113), kind=kLoop, calls=%fused_computation.4 | loop fusion | flops 1179648 | bytes 7077893 | tf_op jit(solution)/shard_map/jit(_where)/select_n | solution.py:297
  24.6 1.1 slice_bitcast_fusion.1
  25.7 0.0 copy-start.2
  25.7 0.0 copy-start.3
  25.7 1.1 broadcast_select_fusion.3
  26.8 2.5 %collective-permute-start.1 = (bf16[1152,512]{1,0:T(8,128)(2,1)}, bf16[1152,512]{1,0:T(8,128)(2,1)S(1)}, u32[]{:S(2)}, u32[]{:S(2)}) collective-permute-start(bf16[1152,512]{1,0:T(8,128)(2,1)} %slice_bitcast_fusion.1), channel_id=1, source_target_pairs={{0,2},{1,3},{2,0},{3,1},{4,6},{5,7},{6,4},{7,5}} | collective-permute-start | bytes 3538952 | tf_op jit(solution)/shard_map/ppermute | solution.py:298
  29.3 1.5 collective-permute-start.2
  32.2 0.0 copy-done.2
  32.2 0.0 copy-done.3
  32.2 0.6 select_maximum_fusion.meta_ref
  32.8 36.2 %dispatch.1 = (bf16[8,64,1536]{2,1,0:T(8,128)(2,1)}, f32[8,16,128]{2,1,0:T(8,128)}) custom-call(bf16[64,1536]{1,0:T(8,128)(2,1)} %x_ref.3, f32[16,128]{1,0:T(8,128)} %select_maximum_fusion.meta_ref), custom_call_target="tpu_custom_call" | custom-call | flops 8000000000 | bytes 2000000 | tf_op jit(solution)/shard_map/dispatch/pallas_call | solution.py:319
  69.0 0.0 collective-permute-done.1
  69.0 0.0 collective-permute-done.2
  69.0 3.0 %broadcast_select_fusion.5 = (bf16[1152,512]{1,0:T(8,128)(2,1)}, bf16[1152,512]{1,0:T(8,128)(2,1)}) fusion(bf16[1152,512]{1,0:T(8,128)(2,1)} %collective-permute-done.2, pred[]{:T(512)S(6)} %or.7, bf16[2,1152,512]{2,1,0:T(8,128)(2,1)S(1)} %broadcast_select_fusion, bf16[1152,512]{1,0:T(8,128)(2,1)S(1)} %collective-permute-done.1), kind=kLoop, calls=%fused_computation.14 | loop fusion | flops 1179648 | bytes 5898241 | tf_op jit(solution)/shard_map/jit(_where)/select_n | solution.py:302
  72.0 0.6 collective-permute-start.3
  72.6 1.5 collective-permute-start.4
  74.1 36.3 %gate_up.1 = (bf16[16,1536,512]{2,1,0:T(8,128)(2,1)}, bf16[16,1536,512]{2,1,0:T(8,128)(2,1)}, bf16[1024,512]{1,0:T(8,128)(2,1)}, bf16[512,1024]{1,0:T(8,128)(2,1)}, f32[1024,128]{1,0:T(8,128)}) custom-call(s32[128]{0:T(128)} %old_map.1, bf16[512,1536]{1,0:T(8,128)(2,1)} %bitcast.37, f32[8,16,128]{2,1,0:T(8,128)} %get-tuple-element.17.mall, ...), custom_call_target="tpu_custom_call" | custom-call | flops 30000001024 | bytes 100663296 | tf_op jit(solution)/shard_map/gate_up/pallas_call | solution.py:330
  113.1 0.0 collective-permute-done.3
  113.1 0.0 collective-permute-done.4
  113.1 6.1 %broadcast_select_fusion.1 = (bf16[2,1152,512]{2,1,0:T(8,128)(2,1)}, bf16[2,1152,512]{2,1,0:T(8,128)(2,1)}) fusion(pred[]{:T(512)S(6)} %eq.27, bf16[4,1152,512]{2,1,0:T(8,128)(2,1)} %bitcast.12, s32[]{:T(128)S(6)} %select_n.113, bf16[1,1152,512]{2,1,0:T(8,128)(2,1)} %bitcast.19, bf16[1,1152,512]{2,1,0:T(8,128)(2,1)} %bitcast.18, pred[]{:T(512)S(6)} %eq.33, ...), kind=kLoop, calls=%fused_computation.5 | loop fusion | flops 8257536 | bytes 14155783 | tf_op jit(solution)/shard_map/jit(_where)/select_n | solution.py:305
  119.2 0.0 collective-permute-start.5
  119.2 0.0 copy-start
  119.2 22.6 %down.1 = (bf16[16,512,1536]{2,1,0:T(8,128)(2,1)}, f32[512,1536]{1,0:T(8,128)}) custom-call(bf16[1024,512]{1,0:T(8,128)(2,1)} %get-tuple-element.18.z_ref, bf16[512,1024]{1,0:T(8,128)(2,1)} %get-tuple-element.19.at_ref, f32[1024,128]{1,0:T(8,128)} %get-tuple-element.20.gr_ref, bf16[16,512,1536]{2,1,0:T(8,128)(2,1)} %wd.3), custom_call_target="tpu_custom_call" | custom-call | flops 15000000512 | bytes 50331648 | tf_op jit(solution)/shard_map/down/pallas_call | solution.py:346
  141.8 0.0 copy-done
  141.9 0.0 copy-start.1
  141.9 1.9 %copy-done.1 = f32[512,1536]{1,0:T(8,128)S(1)} copy-done((f32[512,1536]{1,0:T(8,128)S(1)}, f32[512,1536]{1,0:T(8,128)}, u32[]{:S(2)}) %copy-start.1) | copy-done | bytes 3145752
  143.7 23.1 %combine.1 = bf16[64,1536]{1,0:T(8,128)(2,1)S(1)} custom-call(f32[8,64,1536]{2,1,0:T(8,128)S(1)} %bitcast.34, bf16[64,1536]{1,0:T(8,128)(2,1)S(1)} %copy-done), custom_call_target="tpu_custom_call" | custom-call | flops 16000000000 | bytes 4000000 | tf_op jit(solution)/shard_map/combine/pallas_call | solution.py:357
  166.8 0.0 collective-permute-done.5.other
  166.8 0.8 patch.1
  167.7 0.7 copy.24
  (1 shorter events, 0.0 us)
Async XLA Ops:
  16.4 5.6 %collective-permute-start = (bf16[2,1152,512]{2,1,0:T(8,128)(2,1)S(1)}, bf16[2,1152,512]{2,1,0:T(8,128)(2,1)}, u32[]{:S(2)}, u32[]{:S(2)}) collective-permute-start(bf16[2,1152,512]{2,1,0:T(8,128)(2,1)S(1)} %constant_dynamic-slice_fusion), channel_id=1, source_target_pairs={{0,1},{1,0},{2,3},{3,2},{4,5},{5,4},{6,7},{7,6}} | collective-permute-start | bytes 7077896 | tf_op jit(solution)/shard_map/ppermute | solution.py:295
  25.7 6.5 %copy-start.2 = (s32[64,8]{0,1:T(8,128)S(1)}, s32[64,8]{0,1:T(8,128)}, u32[]{:S(2)}) copy-start(s32[64,8]{0,1:T(8,128)} %param.10) | copy-start | bytes 6148
  25.7 6.5 %copy-start.3 = (f32[64,8]{0,1:T(8,128)S(1)}, f32[64,8]{0,1:T(8,128)}, u32[]{:S(2)}) copy-start(f32[64,8]{0,1:T(8,128)} %param.11) | copy-start | bytes 6148
  26.8 42.2 %collective-permute-start.1 = (bf16[1152,512]{1,0:T(8,128)(2,1)}, bf16[1152,512]{1,0:T(8,128)(2,1)S(1)}, u32[]{:S(2)}, u32[]{:S(2)}) collective-permute-start(bf16[1152,512]{1,0:T(8,128)(2,1)} %slice_bitcast_fusion.1), channel_id=1, source_target_pairs={{0,2},{1,3},{2,0},{3,1},{4,6},{5,7},{6,4},{7,5}} | collective-permute-start | bytes 3538952 | tf_op jit(solution)/shard_map/ppermute | solution.py:298
  29.3 39.7 %collective-permute-start.2 = (bf16[1152,512]{1,0:T(8,128)(2,1)}, bf16[1152,512]{1,0:T(8,128)(2,1)}, u32[]{:S(2)}, u32[]{:S(2)}) collective-permute-start(bf16[1152,512]{1,0:T(8,128)(2,1)} %broadcast_select_fusion.3), channel_id=1, source_target_pairs={{0,4},{1,5},{2,6},{3,7},{4,0},{5,1},{6,2},{7,3}} | collective-permute-start | bytes 3538952 | tf_op jit(solution)/shard_map/ppermute | solution.py:299
  72.0 41.1 %collective-permute-start.3 = (bf16[1152,512]{1,0:T(8,128)(2,1)}, bf16[1152,512]{1,0:T(8,128)(2,1)}, u32[]{:S(2)}, u32[]{:S(2)}) collective-permute-start(bf16[1152,512]{1,0:T(8,128)(2,1)} %get-tuple-element.32), channel_id=1, source_target_pairs={{0,2},{1,3},{2,0},{3,1},{4,6},{5,7},{6,4},{7,5}} | collective-permute-start | bytes 3538952 | tf_op jit(solution)/shard_map/ppermute | solution.py:302
  72.6 40.5 %collective-permute-start.4 = (bf16[1152,512]{1,0:T(8,128)(2,1)}, bf16[1152,512]{1,0:T(8,128)(2,1)}, u32[]{:S(2)}, u32[]{:S(2)}) collective-permute-start(bf16[1152,512]{1,0:T(8,128)(2,1)} %get-tuple-element.33), channel_id=1, source_target_pairs={{0,4},{1,5},{2,6},{3,7},{4,0},{5,1},{6,2},{7,3}} | collective-permute-start | bytes 3538952 | tf_op jit(solution)/shard_map/ppermute | solution.py:303
  119.2 47.6 %collective-permute-start.5 = (bf16[2,1152,512]{2,1,0:T(8,128)(2,1)}, bf16[2,1152,512]{2,1,0:T(8,128)(2,1)}, u32[]{:S(2)}, u32[]{:S(2)}) collective-permute-start(bf16[2,1152,512]{2,1,0:T(8,128)(2,1)} %get-tuple-element.30), channel_id=1, source_target_pairs={{0,1},{1,0},{2,3},{3,2},{4,5},{5,4},{6,7},{7,6}} | collective-permute-start | bytes 7077896 | tf_op jit(solution)/shard_map/ppermute | solution.py:305
  119.2 22.6 %copy-start = (bf16[64,1536]{1,0:T(8,128)(2,1)S(1)}, bf16[64,1536]{1,0:T(8,128)(2,1)}, u32[]{:S(2)}) copy-start(bf16[64,1536]{1,0:T(8,128)(2,1)} %x_ref.3) | copy-start | bytes 589828
  141.9 1.9 %copy-start.1 = (f32[512,1536]{1,0:T(8,128)S(1)}, f32[512,1536]{1,0:T(8,128)}, u32[]{:S(2)}) copy-start(f32[512,1536]{1,0:T(8,128)} %get-tuple-element.21) | copy-start | bytes 9437188

commit v2 on v1

v2 whole, which is shorter than its diff:
```python
import functools

import jax
import jax.numpy as jnp
from jax import lax
from jax.experimental import pallas as pl
from jax.experimental.pallas import tpu as pltpu
from jax.sharding import PartitionSpec as P

MESH = pl.DeviceIdType.MESH
BF16, F32 = jnp.bfloat16, jnp.float32
ANY = pl.BlockSpec(memory_space=pl.ANY)
VMEM = pl.BlockSpec(memory_space=pltpu.VMEM)
SMEM = pl.BlockSpec(memory_space=pltpu.SMEM)
LIMIT = 62 * 1024 * 1024
HALF = 8


def places():
    me = lax.axis_index('ep')
    core, chip = me % 2, me // 2
    x, y = chip % 2, chip // 2
    sib = chip * 2 + 1 - core
    chips = ((1 - y) * 2 + 1 - x, y * 2 + 1 - x, (1 - y) * 2 + x)
    return me, core, chip, sib, chips


def enter(partners):
    barrier = pltpu.get_barrier_semaphore()
    for dev in partners:
        pl.semaphore_signal(barrier, inc=1, device_id={'ep': dev}, device_id_type=MESH)
    pl.semaphore_wait(barrier, len(partners))


def remote(src, dst, send, recv, dev):
    return pltpu.make_async_remote_copy(src, dst, send, recv, device_id={'ep': dev}, device_id_type=MESH)


def pack_kernel(src, wg, wu, wd, send_ref, own_ref, sem):
    me = lax.axis_index('ep')
    slots, depth, width = wg.shape
    half = 3 * depth // 2
    slot = jnp.where(src[0] // slots == me, src[0], src[1]) % slots

    def first(ref, k):
        return [pltpu.make_async_copy(wg.at[slot], ref.at[pl.ds(0, depth)], sem.at[k]),
                pltpu.make_async_copy(wu.at[slot, pl.ds(0, half - depth)], ref.at[pl.ds(depth, half - depth)], sem.at[k + 1])]

    def second(ref, k):
        rest = 2 * depth - half
        copies = [pltpu.make_async_copy(wu.at[slot, pl.ds(half - depth, rest)], ref.at[pl.ds(0, rest)], sem.at[k])]
        for b in range(depth // width):
            copies.append(pltpu.make_async_copy(wd.at[slot, :, pl.ds(width * b, width)],
                                                ref.at[pl.ds(rest + width * b, width)], sem.at[k + 1 + b]))
        return copies

    def run(copies):
        for copy in copies:
            copy.start()
        for copy in copies:
            copy.wait()

    @pl.when(me % 2 == 0)
    def _():
        run(second(send_ref, 2) + first(own_ref, 0))

    @pl.when(me % 2 == 1)
    def _():
        run(first(send_ref, 0) + second(own_ref, 2))


def dispatch_kernel(x_ref, meta_ref, slot_ref, xall, mall, near, send, recv):
    me, core, chip, sib, chips = places()
    peers = [c * 2 + core for c in chips]
    enter(peers + [sib])

    def pair(k, src_x, src_m, block, dev):
        return (remote(src_x, xall.at[block], send.at[2 * k], recv.at[2 * k], dev),
                remote(src_m, mall.at[block], send.at[2 * k + 1], recv.at[2 * k + 1], dev))

    first = [pair(k, x_ref, meta_ref, me, peers[k]) for k in range(3)]
    first.append(pair(3, x_ref, meta_ref, me, sib))
    for group in first:
        for copy in group:
            copy.start()
    slot = remote(slot_ref, near, send.at[14], recv.at[14], sib)
    slot.start()
    xall[pl.ds(me, 1)] = x_ref[...][None]
    mall[pl.ds(me, 1)] = meta_ref[...][None]
    second = []
    for k in (1, 2, 0):
        for copy in first[k]:
            copy.wait_recv()
        fwd = pair(4 + k, xall.at[peers[k]], mall.at[peers[k]], peers[k], sib)
        for copy in fwd:
            copy.start()
        second.append(fwd)
    for copy in first[3]:
        copy.wait_recv()
    for group in first:
        for copy in group:
            copy.wait_send()
    for group in second:
        for copy in group:
            copy.wait()
    slot.wait()


def stream(slots0, count, w, w_new, bufs, sem_in, sem_out):
    def load(i):
        return [pltpu.make_async_copy(w[k].at[slots0 + i], bufs[k].at[i], sem_in.at[k, i]) for k in range(3)]

    def drain(i):
        return [pltpu.make_async_copy(bufs[k].at[i], w_new[k].at[slots0 + i], sem_out.at[k, i]) for k in range(3)]

    return load, drain


def experts(i, xs, gate, bufs):
    act_g = jnp.dot(xs, bufs[0][i], preferred_element_type=F32)
    act_u = jnp.dot(xs, bufs[1][i], preferred_element_type=F32)
    z = (jax.nn.silu(act_g) * act_u).astype(BF16)
    o = jnp.dot(z, bufs[2][i], preferred_element_type=F32)
    return (o * gate).astype(BF16)


def first_kernel(old_map, x_hbm, m_hbm, wg, wu, wd, wg_new, wu_new, wd_new, xg_out, at_out, gr_out, c_out,
                 bg, bu, bd, x_ref, mall, xg, a_ref, at_ref, gr_ref, c_ref, pos, gsc, meta, sem_in, sem_out, sem):
    me = lax.axis_index('ep')
    slots, tok, cap = wg.shape[0], 64, 8
    total = x_ref.shape[0]
    devs = total // tok
    rows = devs * cap
    bufs = (bg, bu, bd)
    load, drain = stream(0, HALF, (wg, wu, wd), (wg_new, wu_new, wd_new), bufs, sem_in, sem_out)
    get_m = pltpu.make_async_copy(m_hbm, mall, sem.at[0])
    get_x = pltpu.make_async_copy(x_hbm, x_ref, sem.at[1])
    get_m.start()
    get_x.start()
    for i in range(HALF):
        for copy in load(i):
            copy.start()
    get_m.wait()

    lane = lax.broadcasted_iota(jnp.int32, (16, 128), 1)
    for p in range(devs // 2):
        other = pltpu.roll(mall[2 * p + 1], 64, axis=1)
        meta[:, pl.ds(128 * p, 128)] = jnp.where(lane < 64, mall[2 * p], other)
    ids = meta[0:8, :]
    gates = meta[8:16, :]
    hits, gs = [], []
    for j in range(slots):
        same = ids == old_map[me * slots + j].astype(F32)
        hits.append(jnp.sum(jnp.where(same, 1.0, 0.0), axis=0, keepdims=True))
        gs.append(jnp.sum(jnp.where(same, gates, 0.0), axis=0, keepdims=True))
    hit = jnp.concatenate(hits, axis=0)
    gsc[...] = jnp.concatenate(gs, axis=0)
    t_row = lax.broadcasted_iota(jnp.int32, (total, total), 0)
    t_col = lax.broadcasted_iota(jnp.int32, (total, total), 1)
    before = jnp.where((t_row < t_col) & (t_row // tok == t_col // tok), 1.0, 0.0).astype(BF16)
    rank = jnp.dot(hit.astype(BF16), before, preferred_element_type=F32)
    owner = (lax.broadcasted_iota(jnp.int32, (slots, total), 1) // tok * cap).astype(F32)
    pos[...] = jnp.where(hit > 0.5, rank + owner, -1.0)
    post = jnp.transpose(jnp.concatenate([pos[...], jnp.full((128 - slots, total), -1.0, F32)], axis=0))
    wide = lax.broadcasted_iota(jnp.int32, (total, 128), 1)
    for p in range(slots // 2):
        want = jnp.where(wide < rows, post[:, 2 * p:2 * p + 1], post[:, 2 * p + 1:2 * p + 2])
        at_ref[:, pl.ds(128 * p, 128)] = jnp.where(want == (wide % rows).astype(F32), 1.0, 0.0).astype(BF16)

    row_id = lax.broadcasted_iota(jnp.int32, (rows, total), 0).astype(F32)

    @pl.loop(0, slots)
    def _(j):
        r0 = pl.multiple_of(j * rows, rows)
        chosen = row_id == pos[pl.ds(j, 1), :]
        a_ref[pl.ds(r0, rows), :] = jnp.where(chosen, 1.0, 0.0).astype(BF16)
        g = jnp.sum(jnp.where(chosen, gsc[pl.ds(j, 1), :], 0.0), axis=1, keepdims=True)
        gr_ref[pl.ds(r0, rows), :] = jnp.broadcast_to(g, (rows, 128))

    get_x.wait()

    @pl.loop(0, slots // 4)
    def _(q):
        r0 = pl.multiple_of(q * 4 * rows, 4 * rows)
        picked = jnp.dot(a_ref[pl.ds(r0, 4 * rows), :], x_ref[...], preferred_element_type=F32)
        xg[pl.ds(r0, 4 * rows), :] = picked.astype(BF16)

    @pl.loop(0, HALF)
    def _(i):
        for copy in load(i):
            copy.wait()
        for copy in drain(i):
            copy.start()
        r0 = pl.multiple_of(i * rows, rows)
        c_ref[pl.ds(r0, rows), :] = experts(i, xg[pl.ds(r0, rows), :], gr_ref[pl.ds(r0, rows), 0:1], bufs)

    done = HALF * rows
    puts = [pltpu.make_async_copy(xg.at[pl.ds(done, slots * rows - done)], xg_out, sem.at[0]),
            pltpu.make_async_copy(at_ref, at_out, sem.at[1]),
            pltpu.make_async_copy(gr_ref.at[pl.ds(done, slots * rows - done)], gr_out, sem.at[2]),
            pltpu.make_async_copy(c_ref, c_out, sem.at[3])]
    for copy in puts:
        copy.start()
    for i in range(HALF):
        for copy in drain(i):
            copy.wait()
    for copy in puts:
        copy.wait()


def second_kernel(xg_hbm, at_hbm, gr_hbm, c_hbm, wg, wu, wd, wg_old, wu_old, wd_old, wg_new, wu_new, wd_new, out_hbm,
                  bg, bu, bd, xg, at_ref, gr_ref, c_ref, out_ref, sem_in, sem_out, sem):
    slots = wg.shape[0]
    count = slots - HALF
    rows = xg.shape[0] // count
    bufs = (bg, bu, bd)
    load, drain = stream(HALF, count, (wg, wu, wd), (wg_new, wu_new, wd_new), bufs, sem_in, sem_out)
    done = HALF * rows
    gets = [pltpu.make_async_copy(xg_hbm, xg, sem.at[0]), pltpu.make_async_copy(gr_hbm, gr_ref, sem.at[1]),
            pltpu.make_async_copy(c_hbm, c_ref.at[pl.ds(0, done)], sem.at[2]), pltpu.make_async_copy(at_hbm, at_ref, sem.at[3])]
    for copy in gets[:2]:
        copy.start()
    for i in range(count):
        for copy in load(i):
            copy.start()
    for copy in gets[2:]:
        copy.start()
    for copy in gets[:2]:
        copy.wait()

    @pl.loop(0, count)
    def _(i):
        for copy in load(i):
            copy.wait()
        for copy in drain(i):
            copy.start()
        r0 = pl.multiple_of(i * rows, rows)
        c = experts(i, xg[pl.ds(r0, rows), :], gr_ref[pl.ds(r0, rows), 0:1], bufs)
        c_ref[pl.ds(pl.multiple_of(done + i * rows, rows), rows), :] = c

    for copy in gets[2:]:
        copy.wait()
    cols = 256

    @pl.loop(0, out_ref.shape[1] // cols)
    def _(n):
        c0 = pl.multiple_of(n * cols, cols)
        out_ref[:, pl.ds(c0, cols)] = jnp.dot(at_ref[...], c_ref[:, pl.ds(c0, cols)], preferred_element_type=F32)

    put = pltpu.make_async_copy(out_ref, out_hbm, sem.at[0])
    put.start()
    for i in range(count):
        for copy in drain(i):
            copy.wait()
    put.wait()


def combine_kernel(part, x_ref, rx1, ry1, rx2, ry2, own, y_ref, got, gown, here, near, summed, far, sem, send, recv):
    me, core, chip, sib, chips = places()
    peers = [c * 2 + core for c in chips]
    order = list(chips) + [chip]
    mine = [pltpu.make_async_copy(part.at[c * 2 + core], here.at[k], sem.at[k]) for k, c in enumerate(order)]
    for copy in mine:
        copy.start()
    enter(peers + [sib])
    across = [remote(part.at[c * 2 + 1 - core], near.at[k], send.at[k], recv.at[k], sib) for k, c in enumerate(order)]
    for copy in across:
        copy.start()
    out = [remote(summed.at[k], far.at[k], send.at[4 + k], recv.at[4 + k], peers[k]) for k in range(3)]
    moved = [remote(r, got.at[k], send.at[7 + k], recv.at[7 + k], sib) for k, r in enumerate((rx1, ry1, rx2, ry2))]
    moved.append(remote(own, gown, send.at[11], recv.at[11], sib))
    for copy in moved:
        copy.start()
    for k in range(4):
        mine[k].wait()
        across[k].wait_recv()
        summed[k] = here[k] + near[k]
        if k >= 1:
            out[k - 1].start()
    acc = x_ref[...].astype(F32) + summed[3]
    for k in (1, 2, 0):
        out[k].wait_recv()
        acc = acc + far[k]
    y_ref[...] = acc.astype(BF16)
    for copy in moved:
        copy.wait_recv()
    for copy in across + out + moved:
        copy.wait_send()


def patch_kernel(src, dst, rx1, ry1, rx2, ry2, got, near, gown, wg, wu, wd, wg_old, wu_old, wd_old,
                 wg_new, wu_new, wd_new, buf, sem):
    me = lax.axis_index('ep')
    core = me % 2
    slots, depth, width = wg.shape
    part = rx1.shape[0]
    owner = [dst[i] // slots for i in range(2)]
    here = [owner[i] == me for i in range(2)]
    chip = [owner[i] // 2 for i in range(2)]
    local = here[0] & here[1]
    comes = (here[0] | here[1]) & jnp.logical_not(local)
    same_x, same_y = chip[0] % 2 == chip[1] % 2, chip[0] // 2 == chip[1] // 2

    def run(copies):
        for copy in copies:
            copy.start()
        for copy in copies:
            copy.wait()

    def put(slot):
        copies = [pltpu.make_async_copy(buf.at[pl.ds(0, depth)], wg_new.at[slot], sem.at[0]),
                  pltpu.make_async_copy(buf.at[pl.ds(depth, depth)], wu_new.at[slot], sem.at[1])]
        for b in range(depth // width):
            copies.append(pltpu.make_async_copy(buf.at[pl.ds(2 * depth + width * b, width)],
                                                wd_new.at[slot, :, pl.ds(width * b, width)], sem.at[2 + b]))
        run(copies)

    def receive(case, a0, a1, b0, b1):
        @pl.when(comes & case)
        def _():
            copies = []
            for p, (a, b) in enumerate(((a0, b0), (a1, b1))):
                at = pl.multiple_of(core * 2 * part + p * part, 128)
                copies.append(pltpu.make_async_copy(a, buf.at[pl.ds(at, part)], sem.at[p]))
                at = pl.multiple_of((1 - core) * 2 * part + p * part, 128)
                copies.append(pltpu.make_async_copy(b, buf.at[pl.ds(at, part)], sem.at[2 + p]))
            run(copies)

    other = jnp.logical_not
    rows = pl.ds(0, part), pl.ds(part, part)
    receive(same_y & same_x, near.at[rows[0]], near.at[rows[1]], gown.at[rows[0]], gown.at[rows[1]])
    receive(same_y & other(same_x), rx1, rx2, got.at[0], got.at[2])
    receive(same_x & other(same_y), ry2, ry1, got.at[3], got.at[1])
    receive(other(same_x) & other(same_y), ry2, rx2, got.at[3], got.at[2])

    @pl.when(comes)
    def _():
        put(jnp.where(here[0], dst[0], dst[1]) % slots)

    @pl.when(local)
    def _():
        for i in range(2):
            s = src[i] % slots
            copies = [pltpu.make_async_copy(wg.at[s], buf.at[pl.ds(0, depth)], sem.at[0]),
                      pltpu.make_async_copy(wu.at[s], buf.at[pl.ds(depth, depth)], sem.at[1])]
            for b in range(depth // width):
                copies.append(pltpu.make_async_copy(wd.at[s, :, pl.ds(width * b, width)],
                                                    buf.at[pl.ds(2 * depth + width * b, width)], sem.at[2 + b]))
            run(copies)
            put(dst[i] % slots)


def cost(flops, moved):
    return pl.CostEstimate(flops=flops, bytes_accessed=moved, transcendentals=0)


def solution(mesh):
    groups = mesh.shape['ep']

    def flip(bit):
        return [(d, d + bit - 2 * bit * ((d // bit) % 2)) for d in range(groups)]

    to_x, to_y = flip(2), flip(4)

    def local_step(x_loc, expert_ids, gate_val, w_gate, w_up, w_down, old_map, mig_src, mig_dst):
        tok, model = x_loc.shape
        slots, depth, width = w_gate.shape
        total = groups * tok
        per = groups * 8
        rows = slots * per
        later = (slots - HALF) * per
        half = 3 * depth // 2
        weights = (w_gate, w_up, w_down)
        shapes = tuple(jax.ShapeDtypeStruct(w.shape, BF16) for w in weights)
        dma = pltpu.SemaphoreType.DMA
        slot_bytes = 6 * depth * width

        send, own = pl.pallas_call(
            pack_kernel,
            out_shape=(jax.ShapeDtypeStruct((half, width), BF16),) * 2,
            in_specs=[SMEM, ANY, ANY, ANY], out_specs=(VMEM, VMEM),
            scratch_shapes=[dma((6,))],
            cost_estimate=cost(2_000_000_000, 2 * slot_bytes), name='pack',
        )(mig_src, *weights)

        meta = jnp.concatenate([expert_ids.astype(F32).T, gate_val.T], axis=0)
        meta = jnp.pad(meta, ((0, 0), (0, 128 - tok)))
        xall, mall, near = pl.pallas_call(
            dispatch_kernel,
            out_shape=(jax.ShapeDtypeStruct((groups, tok, model), BF16), jax.ShapeDtypeStruct((groups, 16, 128), F32),
                       jax.ShapeDtypeStruct((half, width), BF16)),
            in_specs=[VMEM, VMEM, ANY], out_specs=(VMEM, VMEM, ANY),
            scratch_shapes=[dma((15,)), dma((15,))],
            compiler_params=pltpu.CompilerParams(collective_id=0, has_side_effects=True),
            cost_estimate=cost(8_000_000_000, 2_000_000), name='dispatch',
        )(x_loc, meta, send)

        me = lax.axis_index('ep')
        owner = mig_src // slots
        i_own = (owner[0] == me) | (owner[1] == me)
        chip_own = (owner[0] // 2 == me // 2) | (owner[1] // 2 == me // 2)
        part = half // 2
        held0 = jnp.where(i_own, own[:part], near[:part])
        held1 = jnp.where(i_own, own[part:], near[part:])
        rx1 = lax.ppermute(held0, 'ep', to_x)
        ry1 = lax.ppermute(held1, 'ep', to_y)

        buf = [pltpu.VMEM((HALF, depth, width), BF16)] * 2 + [pltpu.VMEM((HALF, width, depth), BF16)]
        *new, xg, at, gr, c = pl.pallas_call(
            first_kernel,
            out_shape=shapes + (jax.ShapeDtypeStruct((later, model), BF16), jax.ShapeDtypeStruct((total, rows), BF16),
                                jax.ShapeDtypeStruct((later, 128), F32), jax.ShapeDtypeStruct((HALF * per, model), BF16)),
            in_specs=[SMEM] + [ANY] * 5, out_specs=(ANY,) * 7,
            scratch_shapes=buf + [
                pltpu.VMEM((total, model), BF16), pltpu.VMEM((groups, 16, 128), F32),
                pltpu.VMEM((rows, model), BF16), pltpu.VMEM((rows, total), BF16), pltpu.VMEM((total, rows), BF16),
                pltpu.VMEM((rows, 128), F32), pltpu.VMEM((HALF * per, model), BF16),
                pltpu.VMEM((slots, total), F32), pltpu.VMEM((slots, total), F32), pltpu.VMEM((16, total), F32),
                dma((3, HALF)), dma((3, HALF)), dma((4,))],
            compiler_params=pltpu.CompilerParams(vmem_limit_bytes=LIMIT),
            cost_estimate=cost(40_000_000_000, 2 * HALF * slot_bytes), name='first',
        )(old_map, xall.reshape(total, model), mall, *weights)

        rx1, ry1, xg = lax.optimization_barrier((rx1, ry1, xg))
        next_x = jnp.where(chip_own, held1, ry1)
        next_y = jnp.where(chip_own, held0, rx1)
        next_x, next_y, xg = lax.optimization_barrier((next_x, next_y, xg))
        rx2 = lax.ppermute(next_x, 'ep', to_x)
        ry2 = lax.ppermute(next_y, 'ep', to_y)

        *new, psum = pl.pallas_call(
            second_kernel,
            out_shape=shapes + (jax.ShapeDtypeStruct((total, model), F32),),
            in_specs=[ANY] * 10, out_specs=(ANY,) * 4,
            input_output_aliases={7: 0, 8: 1, 9: 2},
            scratch_shapes=buf + [
                pltpu.VMEM((later, model), BF16), pltpu.VMEM((total, rows), BF16), pltpu.VMEM((later, 128), F32),
                pltpu.VMEM((rows, model), BF16), pltpu.VMEM((total, model), F32),
                dma((3, HALF)), dma((3, HALF)), dma((4,))],
            compiler_params=pltpu.CompilerParams(vmem_limit_bytes=LIMIT),
            cost_estimate=cost(40_000_000_000, 2 * HALF * slot_bytes), name='second',
        )(xg, at, gr, c, *weights, *new)

        y_out, got, gown = pl.pallas_call(
            combine_kernel,
            out_shape=(jax.ShapeDtypeStruct((tok, model), BF16), jax.ShapeDtypeStruct((4, part, width), BF16),
                       jax.ShapeDtypeStruct((half, width), BF16)),
            in_specs=[ANY, VMEM] + [ANY] * 5, out_specs=(VMEM, ANY, ANY),
            scratch_shapes=[pltpu.VMEM((4, tok, model), F32), pltpu.VMEM((4, tok, model), F32),
                            pltpu.VMEM((4, tok, model), F32), pltpu.VMEM((3, tok, model), F32),
                            dma((4,)), dma((12,)), dma((12,))],
            compiler_params=pltpu.CompilerParams(collective_id=1, has_side_effects=True),
            cost_estimate=cost(16_000_000_000, 4_000_000), name='combine',
        )(psum.reshape(groups, tok, model), x_loc, rx1, ry1, rx2, ry2, own)

        new = pl.pallas_call(
            patch_kernel,
            out_shape=shapes,
            in_specs=[SMEM, SMEM] + [ANY] * 13, out_specs=(ANY, ANY, ANY),
            input_output_aliases={12: 0, 13: 1, 14: 2},
            scratch_shapes=[pltpu.VMEM((3 * depth, width), BF16), dma((5,))],
            cost_estimate=cost(3_000_000_000, 2 * slot_bytes), name='patch',
        )(mig_src, mig_dst, rx1, ry1, rx2, ry2, got, near, gown, *weights, *new)
        return (y_out, *new)

    row_spec = P(('dp', 'ep'), None)
    slot_spec = P('ep', None, None)
    return jax.shard_map(local_step, mesh=mesh, in_specs=(row_spec, row_spec, row_spec, slot_spec, slot_spec, slot_spec, P(), P(), P()), out_specs=(row_spec, slot_spec, slot_spec, slot_spec), check_vma=False)
```

time: 171 us -> 131 us (0.77)
  the two profiles are of different devices: /device:TPU:0 before, /device:TPU:3 now
where the time goes in v2:
time: 131 us
  Pallas kernels  109 us (83%)
  other arithmetic  9.61 us (7%)
  between operations  6.66 us (5%)
  starting transfers between devices  2.93 us (2%)
  local copies, waits for them, and re-layouts  2.37 us (2%)
    pallas_call x1, Pallas kernels, local_step(): pl.pallas_call(first_kernel, out_shape=shapes + (jax.ShapeDtypeStruct((la...  30.9 us
    pallas_call x1, Pallas kernels, local_step(): pl.pallas_call(combine_kernel, out_shape=(jax.ShapeDtypeStruct((tok, mode...  25.3 us
    pallas_call x1, Pallas kernels, local_step(): pl.pallas_call(second_kernel, out_shape=shapes + (jax.ShapeDtypeStruct((t...  25.2 us
    pallas_call x1, Pallas kernels, local_step(): pl.pallas_call(dispatch_kernel, out_shape=(jax.ShapeDtypeStruct((groups,...  16.9 us
    pallas_call x1, Pallas kernels, local_step(): pl.pallas_call(patch_kernel, out_shape=shapes, in_specs=[SMEM, SMEM] + [A...  5.43 us
    pallas_call x1, Pallas kernels, local_step(): pl.pallas_call(pack_kernel, out_shape=(jax.ShapeDtypeStruct((half, width)...  5.27 us
    select_n x1, other arithmetic, local_step(): next_y = jnp.where(chip_own, held0, rx1)  3.68 us
    select_n x1, other arithmetic, local_step(): held0 = jnp.where(i_own, own[:part], near[:part])  3.28 us
  transfers between devices with their start and end apart: 4, of which 0 were waited for; matrix products, arithmetic and copies ran while one was open for 0% of the time, Pallas kernels for 43%

profile of v2, /device:TPU:3, one launch (start us, length us, event | category | flops | bytes accessed | tf_op | source)
XLA Modules:
  0.0 130.7 jit_solution(9355487014247835237)
XLA Ops:
  0.6 0.7 and_select_fusion
  1.3 0.6 fusion
  3.1 0.7 convert_bitcast_fusion
  3.8 1.3 select_maximum_fusion.meta_ref
  5.1 5.3 %pack.1 = (bf16[2304,512]{1,0:T(8,128)(2,1)}, bf16[2304,512]{1,0:T(8,128)(2,1)}) custom-call(s32[2]{0:T(128)} %src.3, bf16[16,1536,512]{2,1,0:T(8,128)(2,1)} %wg.7, bf16[16,1536,512]{2,1,0:T(8,128)(2,1)} %wu.7, bf16[16,512,1536]{2,1,0:T(8,128)(2,1)} %wd.7), custom_call_target="tpu_custom_call" | custom-call | flops 2000000000 | bytes 9437184 | tf_op jit(solution)/shard_map/pack/pallas_call | solution.py:378
  10.3 0.0 copy-start.1
  10.3 16.9 %dispatch.1 = (bf16[8,64,1536]{2,1,0:T(8,128)(2,1)}, f32[8,16,128]{2,1,0:T(8,128)}, bf16[2304,512]{1,0:T(8,128)(2,1)}) custom-call(bf16[64,1536]{1,0:T(8,128)(2,1)} %x_ref.3, f32[16,128]{1,0:T(8,128)} %select_maximum_fusion.meta_ref, bf16[2304,512]{1,0:T(8,128)(2,1)} %get-tuple-element.33.slot_ref), custom_call_target="tpu_custom_call" | custom-call | flops 8000000000 | bytes 2000000 | tf_op jit(solution)/shard_map/dispatch/pallas_call | solution.py:388
  27.3 0.0 copy-done.1
  27.3 3.3 %slice_select_fusion = (bf16[1152,512]{1,0:T(8,128)(2,1)}, bf16[1152,512]{1,0:T(8,128)(2,1)}) fusion(bf16[2304,512]{1,0:T(8,128)(2,1)} %get-tuple-element.34.near, bf16[2304,512]{1,0:T(8,128)(2,1)S(1)} %copy-done.1, pred[]{:T(512)S(6)} %or.7), kind=kLoop, calls=%fused_computation | loop fusion | flops 1179648 | bytes 7077889 | tf_op jit(solution)/shard_map/jit(_where)/select_n | solution.py:403
  30.6 0.3 collective-permute-start
  30.8 0.7 collective-permute-start.1
  31.5 30.9 %first.1 = (bf16[16,1536,512]{2,1,0:T(8,128)(2,1)}, bf16[16,1536,512]{2,1,0:T(8,128)(2,1)}, bf16[16,512,1536]{2,1,0:T(8,128)(2,1)}, bf16[512,1536]{1,0:T(8,128)(...) custom-call(s32[128]{0:T(128)} %old_map.1, bf16[512,1536]{1,0:T(8,128)(2,1)} %bitcast.9, ...), custom_call_target="tpu_custom_call" | custom-call | flops 40000000000 | bytes 75497472 | tf_op jit(solution)/shard_map/first/pallas_call | solution.py:409
  67.1 0.0 collective-permute-done.rx1
  67.2 0.0 copy-start
  67.2 0.0 collective-permute-done.1.ry1
  67.2 3.7 %broadcast_select_fusion = (bf16[1152,512]{1,0:T(8,128)(2,1)}, bf16[1152,512]{1,0:T(8,128)(2,1)}) fusion(bf16[1152,512]{1,0:T(8,128)(2,1)} %get-tuple-element.60, bf16[1152,512]{1,0:T(8,128)(2,1)S(1)} %collective-permute-done.rx1, pred[]{:T(512)S(6)} %or.6, bf16[1152,512]{1,0:T(8,128)(2,1)} %get-tuple-element.61, bf16[1152,512]{1,0:T(8,128)(2,1)} %collective-permute-done.1.ry1), kind=kLoop, calls=%fused_computation.2 | loop fusion | flops 1179648 | bytes 7077889 | tf_op jit(solution)/shard_map/jit(_where)/select_n | solution.py:426
  70.9 0.0 copy-done
  70.9 0.4 collective-permute-start.2
  71.3 1.5 %collective-permute-start.3 = (bf16[1152,512]{1,0:T(8,128)(2,1)}, bf16[1152,512]{1,0:T(8,128)(2,1)}, u32[]{:S(2)}, u32[]{:S(2)}) collective-permute-start(bf16[1152,512]{1,0:T(8,128)(2,1)} %get-tuple-element.50), channel_id=1, source_target_pairs={{0,4},{1,5},{2,6},{3,7},{4,0},{5,1},{6,2},{7,3}} | collective-permute-start | bytes 3538952 | tf_op jit(solution)/shard_map/ppermute | solution.py:429
  72.8 25.2 %second.1 = (bf16[16,1536,512]{2,1,0:T(8,128)(2,1)}, bf16[16,1536,512]{2,1,0:T(8,128)(2,1)}, bf16[16,512,1536]{2,1,0:T(8,128)(2,1)}, f32[512,1536]{1,0:T(8,128)}) custom-call(bf16[512,1536]{1,0:T(8,128)(2,1)} %get-tuple-element.41.xg_hbm, bf16[512,1024]{1,0:T(8,128)(2,1)} %get-tuple-element.42.at_hbm, ...), custom_call_target="tpu_custom_call", output_to_operand_aliasing={{0}: (7, {}), {1}: (8, {}), {2}: (9, {})} | custom-call | flops 40000000000 | bytes 75497472 | tf_op jit(solution)/shard_map/second/pallas_call | solution.py:431
  98.1 0.0 collective-permute-done.2.rx2
  98.1 0.0 copy-start.2
  98.1 0.0 collective-permute-done.3.ry2
  98.1 1.1 copy-done.2
  99.2 25.3 %combine.1 = (bf16[64,1536]{1,0:T(8,128)(2,1)}, bf16[4,1152,512]{2,1,0:T(8,128)(2,1)}, bf16[2304,512]{1,0:T(8,128)(2,1)}) custom-call(f32[8,64,1536]{2,1,0:T(8,128)} %bitcast.8, bf16[64,1536]{1,0:T(8,128)(2,1)} %x_ref.3, bf16[1152,512]{1,0:T(8,128)(2,1)} %copy-done, bf16[1152,512]{1,0:T(8,128)(2,1)} %collective-permute-done.1.ry1, ...), custom_call_target="tpu_custom_call" | custom-call | flops 16000000000 | bytes 4000000 | tf_op jit(solution)/shard_map/combine/pallas_call | solution.py:444
  124.5 0.0 copy-start.3
  124.5 5.4 %patch.1 = (bf16[16,1536,512]{2,1,0:T(8,128)(2,1)}, bf16[16,1536,512]{2,1,0:T(8,128)(2,1)}, bf16[16,512,1536]{2,1,0:T(8,128)(2,1)}) custom-call(s32[2]{0:T(128)} %src.3, s32[2]{0:T(128)} %dst.1, bf16[1152,512]{1,0:T(8,128)(2,1)} %copy-done, ...), custom_call_target="tpu_custom_call", output_to_operand_aliasing={{0}: (12, {}), {1}: (13, {}), {2}: (14, {})} | custom-call | flops 3000000000 | bytes 9437184 | tf_op jit(solution)/shard_map/patch/pallas_call | solution.py:456
  130.0 0.0 copy-done.3
  130.0 0.7 copy.26
Async XLA Ops:
  10.3 16.9 %copy-start.1 = (bf16[2304,512]{1,0:T(8,128)(2,1)S(1)}, bf16[2304,512]{1,0:T(8,128)(2,1)}, u32[]{:S(2)}) copy-start(bf16[2304,512]{1,0:T(8,128)(2,1)} %get-tuple-element.32.own) | copy-start | bytes 7077892
  30.6 36.6 %collective-permute-start = (bf16[1152,512]{1,0:T(8,128)(2,1)}, bf16[1152,512]{1,0:T(8,128)(2,1)S(1)}, u32[]{:S(2)}, u32[]{:S(2)}) collective-permute-start(bf16[1152,512]{1,0:T(8,128)(2,1)} %get-tuple-element.60), channel_id=1, source_target_pairs={{0,2},{1,3},{2,0},{3,1},{4,6},{5,7},{6,4},{7,5}} | collective-permute-start | bytes 3538952 | tf_op jit(solution)/shard_map/ppermute | solution.py:405
  30.8 36.3 %collective-permute-start.1 = (bf16[1152,512]{1,0:T(8,128)(2,1)}, bf16[1152,512]{1,0:T(8,128)(2,1)}, u32[]{:S(2)}, u32[]{:S(2)}) collective-permute-start(bf16[1152,512]{1,0:T(8,128)(2,1)} %get-tuple-element.61), channel_id=1, source_target_pairs={{0,4},{1,5},{2,6},{3,7},{4,0},{5,1},{6,2},{7,3}} | collective-permute-start | bytes 3538952 | tf_op jit(solution)/shard_map/ppermute | solution.py:406
  67.2 3.7 %copy-start = (bf16[1152,512]{1,0:T(8,128)(2,1)}, bf16[1152,512]{1,0:T(8,128)(2,1)S(1)}, u32[]{:S(2)}) copy-start(bf16[1152,512]{1,0:T(8,128)(2,1)S(1)} %collective-permute-done.rx1) | copy-start | bytes 3538948
  70.9 27.2 %collective-permute-start.2 = (bf16[1152,512]{1,0:T(8,128)(2,1)}, bf16[1152,512]{1,0:T(8,128)(2,1)S(1)}, u32[]{:S(2)}, u32[]{:S(2)}) collective-permute-start(bf16[1152,512]{1,0:T(8,128)(2,1)} %get-tuple-element.49), channel_id=1, source_target_pairs={{0,2},{1,3},{2,0},{3,1},{4,6},{5,7},{6,4},{7,5}} | collective-permute-start | bytes 3538952 | tf_op jit(solution)/shard_map/ppermute | solution.py:428
  71.3 26.8 %collective-permute-start.3 = (bf16[1152,512]{1,0:T(8,128)(2,1)}, bf16[1152,512]{1,0:T(8,128)(2,1)}, u32[]{:S(2)}, u32[]{:S(2)}) collective-permute-start(bf16[1152,512]{1,0:T(8,128)(2,1)} %get-tuple-element.50), channel_id=1, source_target_pairs={{0,4},{1,5},{2,6},{3,7},{4,0},{5,1},{6,2},{7,3}} | collective-permute-start | bytes 3538952 | tf_op jit(solution)/shard_map/ppermute | solution.py:429
  98.1 1.1 copy-start.2
  124.5 5.5 %copy-start.3 = (bf16[64,1536]{1,0:T(8,128)(2,1)S(1)}, bf16[64,1536]{1,0:T(8,128)(2,1)}, u32[]{:S(2)}) copy-start(bf16[64,1536]{1,0:T(8,128)(2,1)} %get-tuple-element.70) | copy-start | bytes 589828

commit v3 on v2

--- a/solution.py
+++ b/solution.py
@@ -1,5 +1,3 @@
-import functools
-
 import jax
 import jax.numpy as jnp
 from jax import lax
@@ -12,7 +10,8 @@
 ANY = pl.BlockSpec(memory_space=pl.ANY)
 VMEM = pl.BlockSpec(memory_space=pltpu.VMEM)
 SMEM = pl.BlockSpec(memory_space=pltpu.SMEM)
-LIMIT = 62 * 1024 * 1024
+HBM = pl.BlockSpec(memory_space=pltpu.HBM)
+MIB = 1024 * 1024
 HALF = 8
 
 
@@ -36,9 +35,16 @@
     return pltpu.make_async_remote_copy(src, dst, send, recv, device_id={'ep': dev}, device_id_type=MESH)
 
 
-def pack_kernel(src, wg, wu, wd, send_ref, own_ref, sem):
+def pack_kernel(src, ids_ref, gate_ref, wg, wu, wd, meta_ref, flag_ref, send_ref, own_ref, sem):
     me = lax.axis_index('ep')
     slots, depth, width = wg.shape
+    owner = [src[i] // slots for i in range(2)]
+    flag_ref[0] = jnp.where((owner[0] == me) | (owner[1] == me), 1, 0)
+    flag_ref[1] = jnp.where((owner[0] // 2 == me // 2) | (owner[1] // 2 == me // 2), 1, 0)
+    tok = ids_ref.shape[1]
+    meta_ref[...] = jnp.zeros_like(meta_ref)
+    meta_ref[0:8, 0:tok] = ids_ref[...].astype(F32)
+    meta_ref[8:16, 0:tok] = gate_ref[...]
     half = 3 * depth // 2
     slot = jnp.where(src[0] // slots == me, src[0], src[1]) % slots
 
@@ -124,8 +130,8 @@
     return (o * gate).astype(BF16)
 
 
-def first_kernel(old_map, x_hbm, m_hbm, wg, wu, wd, wg_new, wu_new, wd_new, xg_out, at_out, gr_out, c_out,
-                 bg, bu, bd, x_ref, mall, xg, a_ref, at_ref, gr_ref, c_ref, pos, gsc, meta, sem_in, sem_out, sem):
+def first_kernel(old_map, x_ref, mall, wg, wu, wd, wg_new, wu_new, wd_new, xg_out, at_ref, gr_out, c_ref,
+                 bg, bu, bd, xg, a_ref, gr_ref, pos, gsc, meta, sem_in, sem_out):
     me = lax.axis_index('ep')
     slots, tok, cap = wg.shape[0], 64, 8
     total = x_ref.shape[0]
@@ -133,14 +139,10 @@
     rows = devs * cap
     bufs = (bg, bu, bd)
     load, drain = stream(0, HALF, (wg, wu, wd), (wg_new, wu_new, wd_new), bufs, sem_in, sem_out)
-    get_m = pltpu.make_async_copy(m_hbm, mall, sem.at[0])
-    get_x = pltpu.make_async_copy(x_hbm, x_ref, sem.at[1])
-    get_m.start()
-    get_x.start()
     for i in range(HALF):
         for copy in load(i):
             copy.start()
-    get_m.wait()
+    done = HALF * rows
 
     lane = lax.broadcasted_iota(jnp.int32, (16, 128), 1)
     for p in range(devs // 2):
@@ -169,21 +171,23 @@
 
     row_id = lax.broadcasted_iota(jnp.int32, (rows, total), 0).astype(F32)
 
-    @pl.loop(0, slots)
-    def _(j):
-        r0 = pl.multiple_of(j * rows, rows)
-        chosen = row_id == pos[pl.ds(j, 1), :]
-        a_ref[pl.ds(r0, rows), :] = jnp.where(chosen, 1.0, 0.0).astype(BF16)
-        g = jnp.sum(jnp.where(chosen, gsc[pl.ds(j, 1), :], 0.0), axis=1, keepdims=True)
-        gr_ref[pl.ds(r0, rows), :] = jnp.broadcast_to(g, (rows, 128))
-
-    get_x.wait()
-
-    @pl.loop(0, slots // 4)
-    def _(q):
-        r0 = pl.multiple_of(q * 4 * rows, 4 * rows)
-        picked = jnp.dot(a_ref[pl.ds(r0, 4 * rows), :], x_ref[...], preferred_element_type=F32)
-        xg[pl.ds(r0, 4 * rows), :] = picked.astype(BF16)
+    def choose(first, count, g_ref):
+        @pl.loop(0, count)
+        def _(j):
+            chosen = row_id == pos[pl.ds(first + j, 1), :]
+            a_ref[pl.ds(pl.multiple_of((first + j) * rows, rows), rows), :] = jnp.where(chosen, 1.0, 0.0).astype(BF16)
+            g = jnp.sum(jnp.where(chosen, gsc[pl.ds(first + j, 1), :], 0.0), axis=1, keepdims=True)
+            g_ref[pl.ds(pl.multiple_of(j * rows, rows), rows), :] = jnp.broadcast_to(g, (rows, 128))
+
+    def gather(first, count, to_ref):
+        @pl.loop(0, count // (4 * rows))
+        def _(q):
+            r0 = pl.multiple_of(q * 4 * rows, 4 * rows)
+            picked = jnp.dot(a_ref[pl.ds(first + r0, 4 * rows), :], x_ref[...], preferred_element_type=F32)
+            to_ref[pl.ds(r0, 4 * rows), :] = picked.astype(BF16)
+
+    choose(0, HALF, gr_ref)
+    gather(0, done, xg)
 
     @pl.loop(0, HALF)
     def _(i):
@@ -194,39 +198,23 @@
         r0 = pl.multiple_of(i * rows, rows)
         c_ref[pl.ds(r0, rows), :] = experts(i, xg[pl.ds(r0, rows), :], gr_ref[pl.ds(r0, rows), 0:1], bufs)
 
-    done = HALF * rows
-    puts = [pltpu.make_async_copy(xg.at[pl.ds(done, slots * rows - done)], xg_out, sem.at[0]),
-            pltpu.make_async_copy(at_ref, at_out, sem.at[1]),
-            pltpu.make_async_copy(gr_ref.at[pl.ds(done, slots * rows - done)], gr_out, sem.at[2]),
-            pltpu.make_async_copy(c_ref, c_out, sem.at[3])]
-    for copy in puts:
-        copy.start()
+    choose(HALF, slots - HALF, gr_out)
+    gather(done, (slots - HALF) * rows, xg_out)
     for i in range(HALF):
         for copy in drain(i):
             copy.wait()
-    for copy in puts:
-        copy.wait()
-
-
-def second_kernel(xg_hbm, at_hbm, gr_hbm, c_hbm, wg, wu, wd, wg_old, wu_old, wd_old, wg_new, wu_new, wd_new, out_hbm,
-                  bg, bu, bd, xg, at_ref, gr_ref, c_ref, out_ref, sem_in, sem_out, sem):
+
+
+def second_kernel(xg, at_ref, gr_ref, c_early, wg, wu, wd, wg_old, wu_old, wd_old, wg_new, wu_new, wd_new, out_ref,
+                  bg, bu, bd, c_ref, sem_in, sem_out):
     slots = wg.shape[0]
     count = slots - HALF
     rows = xg.shape[0] // count
     bufs = (bg, bu, bd)
     load, drain = stream(HALF, count, (wg, wu, wd), (wg_new, wu_new, wd_new), bufs, sem_in, sem_out)
-    done = HALF * rows
-    gets = [pltpu.make_async_copy(xg_hbm, xg, sem.at[0]), pltpu.make_async_copy(gr_hbm, gr_ref, sem.at[1]),
-            pltpu.make_async_copy(c_hbm, c_ref.at[pl.ds(0, done)], sem.at[2]), pltpu.make_async_copy(at_hbm, at_ref, sem.at[3])]
-    for copy in gets[:2]:
-        copy.start()
     for i in range(count):
         for copy in load(i):
             copy.start()
-    for copy in gets[2:]:
-        copy.start()
-    for copy in gets[:2]:
-        copy.wait()
 
     @pl.loop(0, count)
     def _(i):
@@ -235,33 +223,26 @@
         for copy in drain(i):
             copy.start()
         r0 = pl.multiple_of(i * rows, rows)
-        c = experts(i, xg[pl.ds(r0, rows), :], gr_ref[pl.ds(r0, rows), 0:1], bufs)
-        c_ref[pl.ds(pl.multiple_of(done + i * rows, rows), rows), :] = c
-
-    for copy in gets[2:]:
-        copy.wait()
+        c_ref[pl.ds(r0, rows), :] = experts(i, xg[pl.ds(r0, rows), :], gr_ref[pl.ds(r0, rows), 0:1], bufs)
+
     cols = 256
+    done = HALF * rows
 
     @pl.loop(0, out_ref.shape[1] // cols)
     def _(n):
-        c0 = pl.multiple_of(n * cols, cols)
-        out_ref[:, pl.ds(c0, cols)] = jnp.dot(at_ref[...], c_ref[:, pl.ds(c0, cols)], preferred_element_type=F32)
-
-    put = pltpu.make_async_copy(out_ref, out_hbm, sem.at[0])
-    put.start()
+        at = pl.ds(pl.multiple_of(n * cols, cols), cols)
+        out_ref[:, at] = (jnp.dot(at_ref[:, 0:done], c_early[:, at], preferred_element_type=F32)
+                          + jnp.dot(at_ref[:, done:], c_ref[:, at], preferred_element_type=F32))
+
     for i in range(count):
         for copy in drain(i):
             copy.wait()
-    put.wait()
-
-
-def combine_kernel(part, x_ref, rx1, ry1, rx2, ry2, own, y_ref, got, gown, here, near, summed, far, sem, send, recv):
+
+
+def combine_kernel(part, x_ref, rx1, ry1, rx2, ry2, own, y_ref, got, gown, near, summed, far, send, recv):
     me, core, chip, sib, chips = places()
     peers = [c * 2 + core for c in chips]
     order = list(chips) + [chip]
-    mine = [pltpu.make_async_copy(part.at[c * 2 + core], here.at[k], sem.at[k]) for k, c in enumerate(order)]
-    for copy in mine:
-        copy.start()
     enter(peers + [sib])
     across = [remote(part.at[c * 2 + 1 - core], near.at[k], send.at[k], recv.at[k], sib) for k, c in enumerate(order)]
     for copy in across:
@@ -272,9 +253,8 @@
     for copy in moved:
         copy.start()
     for k in range(4):
-        mine[k].wait()
         across[k].wait_recv()
-        summed[k] = here[k] + near[k]
+        summed[k] = part[order[k] * 2 + core] + near[k]
         if k >= 1:
             out[k - 1].start()
     acc = x_ref[...].astype(F32) + summed[3]
@@ -301,30 +281,30 @@
     comes = (here[0] | here[1]) & jnp.logical_not(local)
     same_x, same_y = chip[0] % 2 == chip[1] % 2, chip[0] // 2 == chip[1] // 2
 
-    def run(copies):
+    def quarters(slot):
+        rest = 2 * part - depth
+        return ([(0, part, wg_new, 0, None)],
+                [(0, depth - part, wg_new, part, None), (depth - part, rest, wu_new, 0, None)],
+                [(0, depth - rest, wu_new, rest, None), (depth - rest, part - depth + rest, wd_new, 0, 0)],
+                [(0, width - (part - depth + rest), wd_new, part - depth + rest, 0)]
+                + [(width - (part - depth + rest) + width * b, width, wd_new, 0, b + 1) for b in range(2)])
+
+    def put(refs, slot):
+        copies = []
+        for ref, pieces in zip(refs, quarters(slot)):
+            for r0, n, new, to, b in pieces:
+                where = new.at[slot, pl.ds(to, n)] if b is None else new.at[slot, pl.ds(to, n), pl.ds(width * b, width)]
+                copies.append(pltpu.make_async_copy(ref.at[pl.ds(r0, n)], where, sem.at[len(copies)]))
         for copy in copies:
             copy.start()
         for copy in copies:
             copy.wait()
 
-    def put(slot):
-        copies = [pltpu.make_async_copy(buf.at[pl.ds(0, depth)], wg_new.at[slot], sem.at[0]),
-                  pltpu.make_async_copy(buf.at[pl.ds(depth, depth)], wu_new.at[slot], sem.at[1])]
-        for b in range(depth // width):
-            copies.append(pltpu.make_async_copy(buf.at[pl.ds(2 * depth + width * b, width)],
-                                                wd_new.at[slot, :, pl.ds(width * b, width)], sem.at[2 + b]))
-        run(copies)
-
     def receive(case, a0, a1, b0, b1):
-        @pl.when(comes & case)
-        def _():
-            copies = []
-            for p, (a, b) in enumerate(((a0, b0), (a1, b1))):
-                at = pl.multiple_of(core * 2 * part + p * part, 128)
-                copies.append(pltpu.make_async_copy(a, buf.at[pl.ds(at, part)], sem.at[p]))
-                at = pl.multiple_of((1 - core) * 2 * part + p * part, 128)
-                copies.append(pltpu.make_async_copy(b, buf.at[pl.ds(at, part)], sem.at[2 + p]))
-            run(copies)
+        for c in range(2):
+            @pl.when(comes & case & (core == c))
+            def _(refs=(a0, a1, b0, b1) if c == 0 else (b0, b1, a0, a1)):
+                put(refs, jnp.where(here[0], dst[0], dst[1]) % slots)
 
     other = jnp.logical_not
     rows = pl.ds(0, part), pl.ds(part, part)
@@ -332,10 +312,6 @@
     receive(same_y & other(same_x), rx1, rx2, got.at[0], got.at[2])
     receive(same_x & other(same_y), ry2, ry1, got.at[3], got.at[1])
     receive(other(same_x) & other(same_y), ry2, rx2, got.at[3], got.at[2])
-
-    @pl.when(comes)
-    def _():
-        put(jnp.where(here[0], dst[0], dst[1]) % slots)
 
     @pl.when(local)
     def _():
@@ -346,8 +322,11 @@
             for b in range(depth // width):
                 copies.append(pltpu.make_async_copy(wd.at[s, :, pl.ds(width * b, width)],
                                                     buf.at[pl.ds(2 * depth + width * b, width)], sem.at[2 + b]))
-            run(copies)
-            put(dst[i] % slots)
+            for copy in copies:
+                copy.start()
+            for copy in copies:
+                copy.wait()
+            put([buf.at[pl.ds(part * k, part)] for k in range(4)], dst[i] % slots)
 
 
 def cost(flops, moved):
@@ -375,30 +354,27 @@
         dma = pltpu.SemaphoreType.DMA
         slot_bytes = 6 * depth * width
 
-        send, own = pl.pallas_call(
+        meta, flags, send, own = pl.pallas_call(
             pack_kernel,
-            out_shape=(jax.ShapeDtypeStruct((half, width), BF16),) * 2,
-            in_specs=[SMEM, ANY, ANY, ANY], out_specs=(VMEM, VMEM),
+            out_shape=(jax.ShapeDtypeStruct((16, 128), F32), jax.ShapeDtypeStruct((2,), jnp.int32))
+            + (jax.ShapeDtypeStruct((half, width), BF16),) * 2,
+            in_specs=[SMEM, VMEM, VMEM, HBM, HBM, HBM], out_specs=(VMEM, SMEM, VMEM, VMEM),
             scratch_shapes=[dma((6,))],
+            compiler_params=pltpu.CompilerParams(vmem_limit_bytes=42 * MIB),
             cost_estimate=cost(2_000_000_000, 2 * slot_bytes), name='pack',
-        )(mig_src, *weights)
-
-        meta = jnp.concatenate([expert_ids.astype(F32).T, gate_val.T], axis=0)
-        meta = jnp.pad(meta, ((0, 0), (0, 128 - tok)))
+        )(mig_src, expert_ids.T, gate_val.T, *weights)
+
         xall, mall, near = pl.pallas_call(
             dispatch_kernel,
             out_shape=(jax.ShapeDtypeStruct((groups, tok, model), BF16), jax.ShapeDtypeStruct((groups, 16, 128), F32),
                        jax.ShapeDtypeStruct((half, width), BF16)),
             in_specs=[VMEM, VMEM, ANY], out_specs=(VMEM, VMEM, ANY),
             scratch_shapes=[dma((15,)), dma((15,))],
-            compiler_params=pltpu.CompilerParams(collective_id=0, has_side_effects=True),
+            compiler_params=pltpu.CompilerParams(collective_id=0, has_side_effects=True, vmem_limit_bytes=8 * MIB),
             cost_estimate=cost(8_000_000_000, 2_000_000), name='dispatch',
         )(x_loc, meta, send)
 
-        me = lax.axis_index('ep')
-        owner = mig_src // slots
-        i_own = (owner[0] == me) | (owner[1] == me)
-        chip_own = (owner[0] // 2 == me // 2) | (owner[1] // 2 == me // 2)
+        i_own, chip_own = flags[0] > 0, flags[1] > 0
         part = half // 2
         held0 = jnp.where(i_own, own[:part], near[:part])
         held1 = jnp.where(i_own, own[part:], near[part:])
@@ -410,14 +386,12 @@
             first_kernel,
             out_shape=shapes + (jax.ShapeDtypeStruct((later, model), BF16), jax.ShapeDtypeStruct((total, rows), BF16),
                                 jax.ShapeDtypeStruct((later, 128), F32), jax.ShapeDtypeStruct((HALF * per, model), BF16)),
-            in_specs=[SMEM] + [ANY] * 5, out_specs=(ANY,) * 7,
+            in_specs=[SMEM, VMEM, VMEM, HBM, HBM, HBM], out_specs=(HBM,) * 3 + (VMEM,) * 4,
             scratch_shapes=buf + [
-                pltpu.VMEM((total, model), BF16), pltpu.VMEM((groups, 16, 128), F32),
-                pltpu.VMEM((rows, model), BF16), pltpu.VMEM((rows, total), BF16), pltpu.VMEM((total, rows), BF16),
-                pltpu.VMEM((rows, 128), F32), pltpu.VMEM((HALF * per, model), BF16),
+                pltpu.VMEM((HALF * per, model), BF16), pltpu.VMEM((rows, total), BF16), pltpu.VMEM((HALF * per, 128), F32),
                 pltpu.VMEM((slots, total), F32), pltpu.VMEM((slots, total), F32), pltpu.VMEM((16, total), F32),
-                dma((3, HALF)), dma((3, HALF)), dma((4,))],
-            compiler_params=pltpu.CompilerParams(vmem_limit_bytes=LIMIT),
+                dma((3, HALF)), dma((3, HALF))],
+            compiler_params=pltpu.CompilerParams(vmem_limit_bytes=42 * MIB),
             cost_estimate=cost(40_000_000_000, 2 * HALF * slot_bytes), name='first',
         )(old_map, xall.reshape(total, model), mall, *weights)
 
@@ -431,13 +405,11 @@
         *new, psum = pl.pallas_call(
             second_kernel,
             out_shape=shapes + (jax.ShapeDtypeStruct((total, model), F32),),
-            in_specs=[ANY] * 10, out_specs=(ANY,) * 4,
+            in_specs=[VMEM] * 4 + [HBM] * 6, out_specs=(HBM,) * 3 + (VMEM,),
             input_output_aliases={7: 0, 8: 1, 9: 2},
             scratch_shapes=buf + [
-                pltpu.VMEM((later, model), BF16), pltpu.VMEM((total, rows), BF16), pltpu.VMEM((later, 128), F32),
-                pltpu.VMEM((rows, model), BF16), pltpu.VMEM((total, model), F32),
-                dma((3, HALF)), dma((3, HALF)), dma((4,))],
-            compiler_params=pltpu.CompilerParams(vmem_limit_bytes=LIMIT),
+                pltpu.VMEM((later, model), BF16), dma((3, HALF)), dma((3, HALF))],
+            compiler_params=pltpu.CompilerParams(vmem_limit_bytes=42 * MIB),
             cost_estimate=cost(40_000_000_000, 2 * HALF * slot_bytes), name='second',
         )(xg, at, gr, c, *weights, *new)
 
@@ -445,20 +417,20 @@
             combine_kernel,
             out_shape=(jax.ShapeDtypeStruct((tok, model), BF16), jax.ShapeDtypeStruct((4, part, width), BF16),
                        jax.ShapeDtypeStruct((half, width), BF16)),
-            in_specs=[ANY, VMEM] + [ANY] * 5, out_specs=(VMEM, ANY, ANY),
+            in_specs=[VMEM, VMEM] + [ANY] * 5, out_specs=(VMEM, ANY, ANY),
             scratch_shapes=[pltpu.VMEM((4, tok, model), F32), pltpu.VMEM((4, tok, model), F32),
-                            pltpu.VMEM((4, tok, model), F32), pltpu.VMEM((3, tok, model), F32),
-                            dma((4,)), dma((12,)), dma((12,))],
-            compiler_params=pltpu.CompilerParams(collective_id=1, has_side_effects=True),
+                            pltpu.VMEM((3, tok, model), F32), dma((12,)), dma((12,))],
+            compiler_params=pltpu.CompilerParams(collective_id=1, has_side_effects=True, vmem_limit_bytes=24 * MIB),
             cost_estimate=cost(16_000_000_000, 4_000_000), name='combine',
         )(psum.reshape(groups, tok, model), x_loc, rx1, ry1, rx2, ry2, own)
 
         new = pl.pallas_call(
             patch_kernel,
             out_shape=shapes,
-            in_specs=[SMEM, SMEM] + [ANY] * 13, out_specs=(ANY, ANY, ANY),
+            in_specs=[SMEM, SMEM] + [VMEM] * 7 + [HBM] * 6, out_specs=(HBM,) * 3,
             input_output_aliases={12: 0, 13: 1, 14: 2},
-            scratch_shapes=[pltpu.VMEM((3 * depth, width), BF16), dma((5,))],
+            scratch_shapes=[pltpu.VMEM((3 * depth, width), BF16), dma((9,))],
+            compiler_params=pltpu.CompilerParams(vmem_limit_bytes=40 * MIB),
             cost_estimate=cost(3_000_000_000, 2 * slot_bytes), name='patch',
         )(mig_src, mig_dst, rx1, ry1, rx2, ry2, got, near, gown, *weights, *new)
         return (y_out, *new)

time: 131 us -> 109 us (0.83)
  the two profiles are of different devices: /device:TPU:3 before, /device:TPU:0 now
where the time goes in v3:
time: 109 us; the launch traced here: 108 us
  Pallas kernels  96.4 us (88%)
  starting transfers between devices  4.05 us (4%)
  local copies, waits for them, and re-layouts  3.31 us (3%)
  between operations  2.07 us (2%)
  other arithmetic  1.81 us (2%)
    pallas_call x1, Pallas kernels, local_step(): pl.pallas_call(first_kernel, out_shape=shapes + (jax.ShapeDtypeStruct((la...  26.7 us
    pallas_call x1, Pallas kernels, local_step(): pl.pallas_call(second_kernel, out_shape=shapes + (jax.ShapeDtypeStruct((t...  26.6 us
    pallas_call x1, Pallas kernels, local_step(): pl.pallas_call(combine_kernel, out_shape=(jax.ShapeDtypeStruct((tok, mode...  22.7 us
    pallas_call x1, Pallas kernels, local_step(): pl.pallas_call(dispatch_kernel, out_shape=(jax.ShapeDtypeStruct((groups,...  16 us
    pallas_call x1, Pallas kernels, local_step(): pl.pallas_call(pack_kernel, out_shape=(jax.ShapeDtypeStruct((16, 128), F3...  3.55 us
    unnamed x15, local copies, waits for them, and re-layouts  2.72 us
  transfers between devices with their start and end apart: 4, of which 0 were waited for; matrix products, arithmetic and copies ran while one was open for 0% of the time, Pallas kernels for 49%

profile of v3, /device:TPU:0, one launch (start us, length us, event | category | flops | bytes accessed | tf_op | source)
XLA Modules:
  0.0 107.7 jit_solution(3967370913068047619)
XLA Ops:
  0.6 0.0 copy-start
  0.6 0.7 copy-done
  1.3 0.0 copy-start.1
  1.3 0.7 copy-done.1
  2.0 0.0 copy-start.2
  2.0 0.7 copy-done.2
  2.7 0.0 copy-start.5
  2.7 3.5 %pack.1 = (f32[16,128]{1,0:T(8,128)S(1)}, s32[2]{0:T(128)S(1)}, bf16[2304,512]{1,0:T(8,128)(2,1)S(1)}, bf16[2304,512]{1,0:T(8,128)(2,1)S(1)}) custom-call(s32[2]{0:T(128)S(1)} %copy-done.2, s32[8,64]{1,0:T(8,128)S(1)} %bitcast.6, f32[8,64]{1,0:T(8,128)S(1)} %bitcast.7, bf16[16,1536,512]{2,1,0:T(8,128)(2,1)} %wg.7, bf16[16,1536,512]{2,1,0:T(8,128)(2,1)} %wu.7, ...), custom_call_target="tpu_custom_call" | custom-call | flops 2000000000 | bytes 9437184 | tf_op jit(solution)/shard_map/pack/pallas_call | solution.py:357
  6.2 0.6 fusion
  7.5 0.0 copy-done.5
  7.5 16.0 %dispatch.1 = (bf16[8,64,1536]{2,1,0:T(8,128)(2,1)S(1)}, f32[8,16,128]{2,1,0:T(8,128)S(1)}, bf16[2304,512]{1,0:T(8,128)(2,1)S(1)}) custom-call(bf16[64,1536]{1,0:T(8,128)(2,1)S(1)} %copy-done.5, f32[16,128]{1,0:T(8,128)S(1)} %get-tuple-element.36.meta_ref, bf16[2304,512]{1,0:T(8,128)(2,1)S(1)} %get-tuple-element.37.slot_ref), custom_call_target="tpu_custom_call" | custom-call | flops 8000000000 | bytes 2000000 | tf_op jit(solution)/shard_map/dispatch/pallas_call | solution.py:367
  23.5 0.0 copy-start.6
  23.5 0.4 slice_select_fusion
  24.0 1.5 %collective-permute-start = (bf16[1152,512]{1,0:T(8,128)(2,1)S(1)}, bf16[1152,512]{1,0:T(8,128)(2,1)S(1)}, u32[]{:S(2)}, u32[]{:S(2)}) collective-permute-start(bf16[1152,512]{1,0:T(8,128)(2,1)S(1)} %get-tuple-element.64), channel_id=1, source_target_pairs={{0,2},{1,3},{2,0},{3,1},{4,6},{5,7},{6,4},{7,5}} | collective-permute-start | bytes 3538952 | tf_op jit(solution)/shard_map/ppermute | solution.py:381
  25.4 0.6 collective-permute-start.1
  26.0 0.0 copy-done.6
  26.0 26.7 %first.1 = (bf16[16,1536,512]{2,1,0:T(8,128)(2,1)}, bf16[16,1536,512]{2,1,0:T(8,128)(2,1)}, bf16[16,512,1536]{2,1,0:T(8,128)(2,1)}, bf16[512,1536]{1,0:T(8,128)(...) custom-call(s32[128]{0:T(128)S(1)} %copy-done.6, ...), custom_call_target="tpu_custom_call" | custom-call | flops 40000000000 | bytes 75497472 | tf_op jit(solution)/shard_map/first/pallas_call | solution.py:385
  53.4 0.0 collective-permute-done.rx1
  53.4 0.0 collective-permute-done.1.ry1
  53.4 1.4 %broadcast_select_fusion = (bf16[1152,512]{1,0:T(8,128)(2,1)S(1)}, bf16[1152,512]{1,0:T(8,128)(2,1)}) fusion(bf16[1152,512]{1,0:T(8,128)(2,1)S(1)} %get-tuple-element.64, bf16[1152,512]{1,0:T(8,128)(2,1)S(1)} %collective-permute-done.rx1, pred[]{:T(512)} %bitcast.2, bf16[1152,512]{1,0:T(8,128)(2,1)S(1)} %get-tuple-element.65, ...), kind=kLoop, calls=%fused_computation.2 | loop fusion | flops 1179648 | bytes 7077889 | tf_op jit(solution)/shard_map/jit(_where)/select_n | solution.py:400
  54.8 1.0 collective-permute-start.2
  55.7 1.1 collective-permute-start.3
  56.8 26.6 %second.1 = (bf16[16,1536,512]{2,1,0:T(8,128)(2,1)}, bf16[16,1536,512]{2,1,0:T(8,128)(2,1)}, bf16[16,512,1536]{2,1,0:T(8,128)(2,1)}, f32[512,1536]{1,0:T(8,128)S(1)}) custom-call(bf16[512,1536]{1,0:T(8,128)(2,1)S(1)} %get-tuple-element.45.xg, ...), custom_call_target="tpu_custom_call", output_to_operand_aliasing={{0}: (7, {}), {1}: (8, {}), {2}: (9, {})} | custom-call | flops 40000000000 | bytes 75497472 | tf_op jit(solution)/shard_map/second/pallas_call | solution.py:405
  83.4 0.0 collective-permute-done.2.rx2
  83.4 0.0 collective-permute-done.3.ry2
  83.4 0.0 copy-start.3
  83.4 0.0 copy-start.4
  83.4 22.7 %combine.1 = (bf16[64,1536]{1,0:T(8,128)(2,1)S(1)}, bf16[4,1152,512]{2,1,0:T(8,128)(2,1)S(1)}, bf16[2304,512]{1,0:T(8,128)(2,1)S(1)}) custom-call(f32[8,64,1536]{2,1,0:T(8,128)S(1)} %bitcast.8, bf16[64,1536]{1,0:T(8,128)(2,1)S(1)} %copy-done.5, bf16[1152,512]{1,0:T(8,128)(2,1)S(1)} %collective-permute-done.rx1, ...), custom_call_target="tpu_custom_call" | custom-call | flops 16000000000 | bytes 4000000 | tf_op jit(solution)/shard_map/combine/pallas_call | solution.py:416
  106.1 0.0 copy-done.3
  106.1 0.0 copy-done.4
  106.1 0.9 patch.1
  107.0 0.7 copy.26
Async XLA Ops:
  0.6 0.7 copy-start
  1.3 0.7 copy-start.1
  2.0 0.7 copy-start.2
  2.7 4.8 %copy-start.5 = (bf16[64,1536]{1,0:T(8,128)(2,1)S(1)}, bf16[64,1536]{1,0:T(8,128)(2,1)}, u32[]{:S(2)}) copy-start(bf16[64,1536]{1,0:T(8,128)(2,1)} %x_ref.3) | copy-start | bytes 589828
  23.5 2.5 %copy-start.6 = (s32[128]{0:T(128)S(1)}, s32[128]{0:T(128)}, u32[]{:S(2)}) copy-start(s32[128]{0:T(128)} %old_map.1) | copy-start | bytes 1540
  24.0 29.4 %collective-permute-start = (bf16[1152,512]{1,0:T(8,128)(2,1)S(1)}, bf16[1152,512]{1,0:T(8,128)(2,1)S(1)}, u32[]{:S(2)}, u32[]{:S(2)}) collective-permute-start(bf16[1152,512]{1,0:T(8,128)(2,1)S(1)} %get-tuple-element.64), channel_id=1, source_target_pairs={{0,2},{1,3},{2,0},{3,1},{4,6},{5,7},{6,4},{7,5}} | collective-permute-start | bytes 3538952 | tf_op jit(solution)/shard_map/ppermute | solution.py:381
  25.4 28.0 %collective-permute-start.1 = (bf16[1152,512]{1,0:T(8,128)(2,1)S(1)}, bf16[1152,512]{1,0:T(8,128)(2,1)S(1)}, u32[]{:S(2)}, u32[]{:S(2)}) collective-permute-start(bf16[1152,512]{1,0:T(8,128)(2,1)S(1)} %get-tuple-element.65), channel_id=1, source_target_pairs={{0,4},{1,5},{2,6},{3,7},{4,0},{5,1},{6,2},{7,3}} | collective-permute-start | bytes 3538952 | tf_op jit(solution)/shard_map/ppermute | solution.py:382
  54.8 28.6 %collective-permute-start.2 = (bf16[1152,512]{1,0:T(8,128)(2,1)}, bf16[1152,512]{1,0:T(8,128)(2,1)S(1)}, u32[]{:S(2)}, u32[]{:S(2)}) collective-permute-start(bf16[1152,512]{1,0:T(8,128)(2,1)} %get-tuple-element.53), channel_id=1, source_target_pairs={{0,2},{1,3},{2,0},{3,1},{4,6},{5,7},{6,4},{7,5}} | collective-permute-start | bytes 3538952 | tf_op jit(solution)/shard_map/ppermute | solution.py:402
  55.7 27.7 %collective-permute-start.3 = (bf16[1152,512]{1,0:T(8,128)(2,1)S(1)}, bf16[1152,512]{1,0:T(8,128)(2,1)S(1)}, u32[]{:S(2)}, u32[]{:S(2)}) collective-permute-start(bf16[1152,512]{1,0:T(8,128)(2,1)S(1)} %get-tuple-element.54), channel_id=1, source_target_pairs={{0,4},{1,5},{2,6},{3,7},{4,0},{5,1},{6,2},{7,3}} | collective-permute-start | bytes 3538952 | tf_op jit(solution)/shard_map/ppermute | solution.py:403
  83.4 22.7 %copy-start.3 = (s32[2]{0:T(128)S(1)}, s32[2]{0:T(128)}, u32[]{:S(2)}) copy-start(s32[2]{0:T(128)} %src.3) | copy-start | bytes 28
  83.4 22.7 %copy-start.4 = (s32[2]{0:T(128)S(1)}, s32[2]{0:T(128)}, u32[]{:S(2)}) copy-start(s32[2]{0:T(128)} %dst.1) | copy-start | bytes 28

commit v4 on v3

v4 whole, which is shorter than its diff:
```python
import jax
import jax.numpy as jnp
from jax import lax
from jax.experimental import pallas as pl
from jax.experimental.pallas import tpu as pltpu
from jax.sharding import PartitionSpec as P

MESH = pl.DeviceIdType.MESH
BF16, F32 = jnp.bfloat16, jnp.float32
ANY = pl.BlockSpec(memory_space=pl.ANY)
VMEM = pl.BlockSpec(memory_space=pltpu.VMEM)
SMEM = pl.BlockSpec(memory_space=pltpu.SMEM)
HBM = pl.BlockSpec(memory_space=pltpu.HBM)
MIB = 1024 * 1024
HELD = 2
EARLY, SECOND, THIRD = 6, 4, 4
FIRST = EARLY + 2


def places():
    me = lax.axis_index('ep')
    core, chip = me % 2, me // 2
    x, y = chip % 2, chip // 2
    sib = chip * 2 + 1 - core
    chips = ((1 - y) * 2 + 1 - x, y * 2 + 1 - x, (1 - y) * 2 + x)
    return me, core, chip, sib, chips


def enter(partners):
    barrier = pltpu.get_barrier_semaphore()
    for dev in partners:
        pl.semaphore_signal(barrier, inc=1, device_id={'ep': dev}, device_id_type=MESH)
    pl.semaphore_wait(barrier, len(partners))


def remote(src, dst, send, recv, dev):
    return pltpu.make_async_remote_copy(src, dst, send, recv, device_id={'ep': dev}, device_id_type=MESH)


def pack_kernel(src, ids_ref, gate_ref, wg, wu, wd, meta_ref, mine_ref, chip_ref, send_ref, own_ref, sem):
    me = lax.axis_index('ep')
    slots, depth, width = wg.shape
    owner = [src[i] // slots for i in range(2)]
    mine_ref[0] = jnp.where((owner[0] == me) | (owner[1] == me), 1, 0)
    chip_ref[0] = jnp.where((owner[0] // 2 == me // 2) | (owner[1] // 2 == me // 2), 1, 0)
    tok = ids_ref.shape[1]
    meta_ref[...] = jnp.zeros_like(meta_ref)
    meta_ref[0:8, 0:tok] = ids_ref[...].astype(F32)
    meta_ref[8:16, 0:tok] = gate_ref[...]
    half = 3 * depth // 2
    slot = jnp.where(src[0] // slots == me, src[0], src[1]) % slots

    def first(ref, k):
        return [pltpu.make_async_copy(wg.at[slot], ref.at[pl.ds(0, depth)], sem.at[k]),
                pltpu.make_async_copy(wu.at[slot, pl.ds(0, half - depth)], ref.at[pl.ds(depth, half - depth)], sem.at[k + 1])]

    def second(ref, k):
        rest = 2 * depth - half
        copies = [pltpu.make_async_copy(wu.at[slot, pl.ds(half - depth, rest)], ref.at[pl.ds(0, rest)], sem.at[k])]
        for b in range(depth // width):
            copies.append(pltpu.make_async_copy(wd.at[slot, :, pl.ds(width * b, width)],
                                                ref.at[pl.ds(rest + width * b, width)], sem.at[k + 1 + b]))
        return copies

    def run(copies):
        for copy in copies:
            copy.start()
        for copy in copies:
            copy.wait()

    @pl.when(me % 2 == 0)
    def _():
        run(second(send_ref, 2) + first(own_ref, 0))

    @pl.when(me % 2 == 1)
    def _():
        run(first(send_ref, 0) + second(own_ref, 2))


def dispatch_kernel(mine_ref, x_ref, meta_ref, slot_ref, own, wg, wu, wd, xall, mall, near, h0, h1, h2, h3, *rest):
    me, core, chip, sib, chips = places()
    peers = [c * 2 + core for c in chips]
    bufs, (send, recv, sem) = rest[:-3], rest[-3:]
    per = len(bufs) // 3
    size = EARLY // per
    reads = [pltpu.make_async_copy(w.at[pl.ds(i * size, size)], bufs[k * per + i], sem.at[k * per + i])
             for i in range(per) for k, w in enumerate((wg, wu, wd))]
    for copy in reads:
        copy.start()
    enter(peers + [sib])

    def pair(k, src_x, src_m, block, dev):
        return (remote(src_x, xall.at[block], send.at[2 * k], recv.at[2 * k], dev),
                remote(src_m, mall.at[block], send.at[2 * k + 1], recv.at[2 * k + 1], dev))

    first = [pair(k, x_ref, meta_ref, me, peers[k]) for k in range(3)]
    first.append(pair(3, x_ref, meta_ref, me, sib))
    for group in first:
        for copy in group:
            copy.start()
    slot = remote(slot_ref, near, send.at[14], recv.at[14], sib)
    slot.start()
    xall[pl.ds(me, 1)] = x_ref[...][None]
    mall[pl.ds(me, 1)] = meta_ref[...][None]
    slot.wait_recv()
    part = h0.shape[0]
    for k, held in enumerate((h0, h1, h2, h3)):
        rows = pl.ds(k * part, part)
        held[...] = jnp.where(mine_ref[0] > 0, own[rows, :], near[rows, :])
    second = []
    for k in (1, 2, 0):
        for copy in first[k]:
            copy.wait_recv()
        fwd = pair(4 + k, xall.at[peers[k]], mall.at[peers[k]], peers[k], sib)
        for copy in fwd:
            copy.start()
        second.append(fwd)
    for copy in first[3]:
        copy.wait_recv()
    for group in first:
        for copy in group:
            copy.wait_send()
    for group in second:
        for copy in group:
            copy.wait()
    slot.wait_send()
    for copy in reads:
        copy.wait()


def stream(slots0, count, w, w_new, bufs, sem_in, sem_out):
    def load(i):
        return [pltpu.make_async_copy(w[k].at[slots0 + i], bufs[k].at[i], sem_in.at[k, i]) for k in range(3)]

    def drain(i):
        return [pltpu.make_async_copy(bufs[k].at[i], w_new[k].at[slots0 + i], sem_out.at[k, i]) for k in range(3)]

    return load, drain


def experts(i, xs, gate, bufs):
    act_g = jnp.dot(xs, bufs[0][i], preferred_element_type=F32)
    act_u = jnp.dot(xs, bufs[1][i], preferred_element_type=F32)
    z = (jax.nn.silu(act_g) * act_u).astype(BF16)
    o = jnp.dot(z, bufs[2][i], preferred_element_type=F32)
    return (o * gate).astype(BF16)


def first_kernel(old_map, x_ref, mall, *rest):
    bufs, rest = rest[:-22], rest[-22:]
    wg, wu, wd, wg_new, wu_new, wd_new, xg_out, at_ref, gr_out, c_ref, eg, eu, ed, xg, a_ref, gr_ref, pos, gsc, meta = rest[:19]
    more_in, more_out, sem_out = rest[19:]
    me = lax.axis_index('ep')
    slots, tok, cap = wg_new.shape[0], 64, 8
    total = x_ref.shape[0]
    devs = total // tok
    rows = devs * cap
    done = FIRST * rows
    more = (eg, eu, ed)
    load, drain = stream(EARLY, FIRST - EARLY, (wg, wu, wd), (wg_new, wu_new, wd_new), more, more_in, more_out)
    for i in range(FIRST - EARLY):
        for copy in load(i):
            copy.start()
    held = len(bufs) // 3
    size = EARLY // held
    drains = [pltpu.make_async_copy(bufs[k * held + i], new.at[pl.ds(i * size, size)], sem_out.at[k, i])
              for i in range(held) for k, new in enumerate((wg_new, wu_new, wd_new))]
    for copy in drains:
        copy.start()

    lane = lax.broadcasted_iota(jnp.int32, (16, 128), 1)
    for p in range(devs // 2):
        other = pltpu.roll(mall[2 * p + 1], 64, axis=1)
        meta[:, pl.ds(128 * p, 128)] = jnp.where(lane < 64, mall[2 * p], other)
    ids = meta[0:8, :]
    gates = meta[8:16, :]
    hits, gs = [], []
    for j in range(slots):
        same = ids == old_map[me * slots + j].astype(F32)
        hits.append(jnp.sum(jnp.where(same, 1.0, 0.0), axis=0, keepdims=True))
        gs.append(jnp.sum(jnp.where(same, gates, 0.0), axis=0, keepdims=True))
    hit = jnp.concatenate(hits, axis=0)
    gsc[...] = jnp.concatenate(gs, axis=0)
    t_row = lax.broadcasted_iota(jnp.int32, (total, total), 0)
    t_col = lax.broadcasted_iota(jnp.int32, (total, total), 1)
    before = jnp.where((t_row < t_col) & (t_row // tok == t_col // tok), 1.0, 0.0).astype(BF16)
    rank = jnp.dot(hit.astype(BF16), before, preferred_element_type=F32)
    owner = (lax.broadcasted_iota(jnp.int32, (slots, total), 1) // tok * cap).astype(F32)
    pos[...] = jnp.where(hit > 0.5, rank + owner, -1.0)
    post = jnp.transpose(jnp.concatenate([pos[...], jnp.full((128 - slots, total), -1.0, F32)], axis=0))
    wide = lax.broadcasted_iota(jnp.int32, (total, 128), 1)
    for p in range(slots // 2):
        want = jnp.where(wide < rows, post[:, 2 * p:2 * p + 1], post[:, 2 * p + 1:2 * p + 2])
        at_ref[:, pl.ds(128 * p, 128)] = jnp.where(want == (wide % rows).astype(F32), 1.0, 0.0).astype(BF16)

    row_id = lax.broadcasted_iota(jnp.int32, (rows, total), 0).astype(F32)

    def choose(first, count, g_ref):
        @pl.loop(0, count)
        def _(j):
            chosen = row_id == pos[pl.ds(first + j, 1), :]
            a_ref[pl.ds(pl.multiple_of((first + j) * rows, rows), rows), :] = jnp.where(chosen, 1.0, 0.0).astype(BF16)
            g = jnp.sum(jnp.where(chosen, gsc[pl.ds(first + j, 1), :], 0.0), axis=1, keepdims=True)
            g_ref[pl.ds(pl.multiple_of(j * rows, rows), rows), :] = jnp.broadcast_to(g, (rows, 128))

    def gather(first, count, to_ref):
        step = max(d for d in range(16, 257, 16) if count % d == 0)

        @pl.loop(0, count // step)
        def _(q):
            r0 = pl.multiple_of(q * step, step)
            picked = jnp.dot(a_ref[pl.ds(first + r0, step), :], x_ref[...], preferred_element_type=F32)
            to_ref[pl.ds(r0, step), :] = picked.astype(BF16)

    choose(0, FIRST, gr_ref)
    gather(0, done, xg)

    for n in range(held):
        @pl.loop(0, size)
        def _(i):
            at = pl.ds(pl.multiple_of((n * size + i) * rows, rows), rows)
            c_ref[at, :] = experts(i, xg[at, :], gr_ref[at, 0:1], bufs[n::held])

    @pl.loop(0, FIRST - EARLY)
    def _(i):
        for copy in load(i):
            copy.wait()
        for copy in drain(i):
            copy.start()
        at = pl.ds(pl.multiple_of((EARLY + i) * rows, rows), rows)
        c_ref[at, :] = experts(i, xg[at, :], gr_ref[at, 0:1], more)

    choose(FIRST, slots - FIRST, gr_out)
    gather(done, (slots - FIRST) * rows, xg_out)
    for copy in drains:
        copy.wait()
    for i in range(FIRST - EARLY):
        for copy in drain(i):
            copy.wait()


def later(first_slot, xg, gr_ref, w, w_new, c_ref, c_base, bufs, sem_in, sem_out, finish):
    count = bufs[0].shape[0]
    rows = gr_ref.shape[0] // (w[0].shape[0] - FIRST)
    load, drain = stream(first_slot, count, w, w_new, bufs, sem_in, sem_out)
    for i in range(count):
        for copy in load(i):
            copy.start()
    base = (first_slot - FIRST) * rows

    @pl.loop(0, count)
    def _(i):
        for copy in load(i):
            copy.wait()
        for copy in drain(i):
            copy.start()
        r0 = pl.multiple_of(i * rows, rows)
        at = pl.ds(pl.multiple_of(base + r0, rows), rows)
        c_ref[pl.ds(pl.multiple_of(c_base + r0, rows), rows), :] = experts(i, xg[at, :], gr_ref[at, 0:1], bufs)

    finish()
    for i in range(count):
        for copy in drain(i):
            copy.wait()


def second_kernel(xg, gr_ref, wg, wu, wd, wg_old, wu_old, wd_old, wg_new, wu_new, wd_new, c_ref,
                  bg, bu, bd, sem_in, sem_out):
    later(FIRST, xg, gr_ref, (wg, wu, wd), (wg_new, wu_new, wd_new), c_ref, 0, (bg, bu, bd), sem_in, sem_out,
          lambda: None)


def third_kernel(xg, gr_ref, at_ref, c0, c1, wg, wu, wd, wg_old, wu_old, wd_old, wg_new, wu_new, wd_new, out_ref,
                 bg, bu, bd, c_ref, sem_in, sem_out):
    cols = 256
    n0 = c0.shape[0]
    done = n0 + c1.shape[0]

    def finish():
        c_ref[0:n0, :] = c0[...]
        c_ref[n0:done, :] = c1[...]

        @pl.loop(0, out_ref.shape[1] // cols)
        def _(n):
            at = pl.ds(pl.multiple_of(n * cols, cols), cols)
            out_ref[:, at] = jnp.dot(at_ref[...], c_ref[:, at], preferred_element_type=F32)

    later(FIRST + SECOND, xg, gr_ref, (wg, wu, wd), (wg_new, wu_new, wd_new), c_ref, done, (bg, bu, bd), sem_in, sem_out,
          finish)


def combine_kernel(part, x_ref, rx1, rx2, rx3, ry1, ry2, ry3, own, y_ref, got, gown, near, summed, far, relay, last,
                   send, recv):
    me, core, chip, sib, chips = places()
    dev_x, dev_y = chips[1] * 2 + core, chips[2] * 2 + core
    order = list(chips) + [chip]
    enter([dev_x, dev_y, sib])
    across = [remote(part.at[c * 2 + 1 - core], near.at[k], send.at[k], recv.at[k], sib) for k, c in enumerate(order)]
    for copy in across:
        copy.start()
    moved = [remote(r, got.at[k], send.at[10 + k], recv.at[10 + k], sib) for k, r in enumerate((rx1, rx2, rx3, ry1, ry2, ry3))]
    moved.append(remote(own, gown, send.at[16], recv.at[16], sib))
    for copy in moved:
        copy.start()
    half = x_ref.shape[1] // 2
    cols = (pl.ds(0, half), pl.ds(half, half))
    towards = (dev_x, dev_y)
    diag = [remote(summed.at[0, :, cols[h]], far.at[0, :, cols[h]], send.at[4 + h], recv.at[4 + h], towards[h]) for h in range(2)]
    next_ = [remote(summed.at[1 + h, :, cols[h]], far.at[1, :, cols[h]], send.at[6 + h], recv.at[6 + h], towards[h]) for h in range(2)]
    onward = [remote(relay.at[h], last.at[h], send.at[8 + h], recv.at[8 + h], towards[1 - h]) for h in range(2)]
    for k in range(4):
        across[k].wait_recv()
        summed[k] = part[order[k] * 2 + core] + near[k]
        if k == 1:
            for copy in diag:
                copy.start()
        elif k == 2:
            next_[0].start()
        elif k == 3:
            next_[1].start()
    acc = x_ref[...].astype(F32) + summed[3]
    for h in range(2):
        diag[h].wait_recv()
        relay[h] = summed[2 - h, :, cols[h]] + far[0, :, cols[h]]
    for h in range(2):
        onward[h].start()
    for h in range(2):
        next_[h].wait_recv()
    acc = acc + far[1]
    for h in range(2):
        onward[h].wait_recv()
        y_ref[:, cols[h]] = (acc[:, h * half:(h + 1) * half] + last[h]).astype(BF16)
    for copy in moved:
        copy.wait_recv()
    for copy in across + diag + next_ + onward + moved:
        copy.wait_send()


def patch_kernel(src, dst, rx1, rx2, rx3, ry1, ry2, ry3, got, near, gown, wg, wu, wd, wg_old, wu_old, wd_old,
                 wg_new, wu_new, wd_new, buf, sem):
    me = lax.axis_index('ep')
    core = me % 2
    slots, depth, width = wg.shape
    part = rx1.shape[0]
    count = 3 * depth // part
    owner = [dst[i] // slots for i in range(2)]
    here = [owner[i] == me for i in range(2)]
    chip = [owner[i] // 2 for i in range(2)]
    local = here[0] & here[1]
    comes = (here[0] | here[1]) & jnp.logical_not(local)
    same_x, same_y = chip[0] % 2 == chip[1] % 2, chip[0] // 2 == chip[1] // 2

    def put(refs, slot):
        spans = [(0, depth, wg_new, None), (depth, 2 * depth, wu_new, None)]
        spans += [(2 * depth + width * b, 2 * depth + width * (b + 1), wd_new, b) for b in range(depth // width)]
        copies, at = [], 0
        for ref in refs:
            n = ref.shape[0]
            for lo, hi, new, b in spans:
                r0, r1 = max(at, lo), min(at + n, hi)
                if r0 < r1:
                    rows = pl.ds(r0 - lo, r1 - r0)
                    where = new.at[slot, rows] if b is None else new.at[slot, rows, pl.ds(width * b, width)]
                    copies.append(pltpu.make_async_copy(ref.at[pl.ds(r0 - at, r1 - r0)], where, sem.at[len(copies)]))
            at += n
        for copy in copies:
            copy.start()
        for copy in copies:
            copy.wait()

    def receive(case, mine, theirs):
        for c in range(2):
            @pl.when(comes & case & (core == c))
            def _(refs=mine + theirs if c == 0 else theirs + mine):
                put(refs, jnp.where(here[0], dst[0], dst[1]) % slots)

    no = jnp.logical_not
    came = (rx1, rx2, rx3, ry1, ry2, ry3)
    for case, order in ((same_y & no(same_x), (0, 1, 2, 5)), (same_x & no(same_y), (2, 5, 4, 3)),
                        (no(same_x) & no(same_y), (4, 5, 2, 1))):
        receive(case, [came[k] for k in order], [got.at[k] for k in order])
    receive(same_y & same_x, [near], [gown])

    @pl.when(local)
    def _():
        for i in range(2):
            s = src[i] % slots
            copies = [pltpu.make_async_copy(wg.at[s], buf.at[pl.ds(0, depth)], sem.at[0]),
                      pltpu.make_async_copy(wu.at[s], buf.at[pl.ds(depth, depth)], sem.at[1])]
            for b in range(depth // width):
                copies.append(pltpu.make_async_copy(wd.at[s, :, pl.ds(width * b, width)],
                                                    buf.at[pl.ds(2 * depth + width * b, width)], sem.at[2 + b]))
            for copy in copies:
                copy.start()
            for copy in copies:
                copy.wait()
            put([buf], dst[i] % slots)


def cost(flops, moved):
    return pl.CostEstimate(flops=flops, bytes_accessed=moved, transcendentals=0)


def solution(mesh):
    groups = mesh.shape['ep']

    def flip(bit):
        return [(d, d + bit - 2 * bit * ((d // bit) % 2)) for d in range(groups)]

    to_x, to_y = flip(2), flip(4)

    def local_step(x_loc, expert_ids, gate_val, w_gate, w_up, w_down, old_map, mig_src, mig_dst):
        tok, model = x_loc.shape
        slots, depth, width = w_gate.shape
        total = groups * tok
        per = groups * 8
        rows = slots * per
        late = (slots - FIRST) * per
        half = 3 * depth // 2
        weights = (w_gate, w_up, w_down)
        shapes = tuple(jax.ShapeDtypeStruct(w.shape, BF16) for w in weights)
        dma = pltpu.SemaphoreType.DMA
        slot_bytes = 6 * depth * width

        def params(mib, **kw):
            return pltpu.CompilerParams(vmem_limit_bytes=mib * MIB, **kw)

        def bf(*shape):
            return jax.ShapeDtypeStruct(shape, BF16)

        meta, i_own, chip_own, send, own = pl.pallas_call(
            pack_kernel,
            out_shape=(jax.ShapeDtypeStruct((16, 128), F32),) + (jax.ShapeDtypeStruct((1,), jnp.int32),) * 2 + (bf(half, width),) * 2,
            in_specs=[SMEM, VMEM, VMEM, HBM, HBM, HBM], out_specs=(VMEM, SMEM, SMEM, VMEM, VMEM),
            scratch_shapes=[dma((6,))], compiler_params=params(42),
            cost_estimate=cost(2_000_000_000, 2 * slot_bytes), name='pack',
        )(mig_src, expert_ids.T, gate_val.T, *weights)

        part = half // 4
        xall, mall, near, h0, h1, h2, h3, *bufs = pl.pallas_call(
            dispatch_kernel,
            out_shape=(bf(groups, tok, model), jax.ShapeDtypeStruct((groups, 16, 128), F32), bf(half, width))
            + (bf(part, width),) * 4 + tuple(bf(HELD, *w.shape[1:]) for w in weights for _ in range(EARLY // HELD)),
            in_specs=[SMEM, VMEM, VMEM, ANY, VMEM, HBM, HBM, HBM], out_specs=(VMEM,) * (7 + 3 * (EARLY // HELD)),
            scratch_shapes=[dma((15,)), dma((15,)), dma((3 * (EARLY // HELD),))],
            compiler_params=params(4, collective_id=0, has_side_effects=True),
            cost_estimate=cost(8_000_000_000, 2_000_000), name='dispatch',
        )(i_own, x_loc, meta, send, own, *weights)

        chip_own = chip_own[0] > 0
        held = (h0, h1, h2, h3)

        def hop(to_x_rows, to_y_rows):
            return lax.ppermute(to_x_rows, 'ep', to_x), lax.ppermute(to_y_rows, 'ep', to_y)

        def onward(k_x, k_y, from_x, from_y, ready):
            from_x, from_y, *ready = lax.optimization_barrier((from_x, from_y, *ready))
            rows_x, rows_y = jnp.where(chip_own, held[k_x], from_y), jnp.where(chip_own, held[k_y], from_x)
            rows_x, rows_y, *ready = lax.optimization_barrier((rows_x, rows_y, *ready))
            return from_x, from_y, *hop(rows_x, rows_y), ready

        rx1, ry1 = hop(held[0], held[3])

        def room(count):
            return [pltpu.VMEM((count,) + w.shape[1:], BF16) for w in weights]

        *new, xg, at, gr, c0 = pl.pallas_call(
            first_kernel,
            out_shape=shapes + (bf(late, model), bf(total, rows), jax.ShapeDtypeStruct((late, 128), F32), bf(FIRST * per, model)),
            in_specs=[SMEM] + [VMEM] * (2 + 3 * (EARLY // HELD)) + [HBM] * 3, out_specs=(HBM,) * 3 + (VMEM,) * 4,
            scratch_shapes=room(FIRST - EARLY) + [
                pltpu.VMEM((FIRST * per, model), BF16), pltpu.VMEM((rows, total), BF16), pltpu.VMEM((FIRST * per, 128), F32),
                pltpu.VMEM((slots, total), F32), pltpu.VMEM((slots, total), F32), pltpu.VMEM((16, total), F32),
                dma((3, FIRST - EARLY)), dma((3, FIRST - EARLY)), dma((3, EARLY // HELD))],
            compiler_params=params(16), cost_estimate=cost(30_000_000_000, (2 * FIRST - EARLY) * slot_bytes), name='first',
        )(old_map, xall.reshape(total, model), mall, *bufs, *weights)

        rx1, ry1, rx2, ry2, (xg, c0) = onward(1, 2, rx1, ry1, (xg, c0))
        *new, c1 = pl.pallas_call(
            second_kernel,
            out_shape=shapes + (bf(SECOND * per, model),),
            in_specs=[VMEM] * 2 + [HBM] * 6, out_specs=(HBM,) * 3 + (VMEM,),
            input_output_aliases={5: 0, 6: 1, 7: 2},
            scratch_shapes=room(SECOND) + [dma((3, SECOND))] * 2,
            compiler_params=params(40), cost_estimate=cost(30_000_000_000, 2 * SECOND * slot_bytes), name='second',
        )(xg, gr, *weights, *new)

        rx2, ry2, rx3, ry3, (xg, c1) = onward(2, 1, rx2, ry2, (xg, c1))
        *new, psum = pl.pallas_call(
            third_kernel,
            out_shape=shapes + (jax.ShapeDtypeStruct((total, model), F32),),
            in_specs=[VMEM] * 5 + [HBM] * 6, out_specs=(HBM,) * 3 + (VMEM,),
            input_output_aliases={8: 0, 9: 1, 10: 2},
            scratch_shapes=room(THIRD) + [pltpu.VMEM((rows, model), BF16)] + [dma((3, THIRD))] * 2,
            compiler_params=params(40), cost_estimate=cost(30_000_000_000, 2 * THIRD * slot_bytes), name='third',
        )(xg, gr, at, c0, c1, *weights, *new)

        came = (rx1, rx2, rx3, ry1, ry2, ry3)
        y_out, got, gown = pl.pallas_call(
            combine_kernel,
            out_shape=(bf(tok, model), bf(6, part, width), bf(half, width)),
            in_specs=[VMEM, VMEM] + [ANY] * 7, out_specs=(VMEM, ANY, ANY),
            scratch_shapes=[pltpu.VMEM((4, tok, model), F32), pltpu.VMEM((4, tok, model), F32),
                            pltpu.VMEM((2, tok, model), F32), pltpu.VMEM((2, tok, model // 2), F32),
                            pltpu.VMEM((2, tok, model // 2), F32), dma((17,)), dma((17,))],
            compiler_params=params(24, collective_id=1, has_side_effects=True),
            cost_estimate=cost(16_000_000_000, 4_000_000), name='combine',
        )(psum.reshape(groups, tok, model), x_loc, *came, own)

        new = pl.pallas_call(
            patch_kernel,
            out_shape=shapes,
            in_specs=[SMEM, SMEM] + [VMEM] * 9 + [HBM] * 6, out_specs=(HBM,) * 3,
            input_output_aliases={14: 0, 15: 1, 16: 2},
            scratch_shapes=[pltpu.VMEM((3 * depth, width), BF16), dma((13,))],
            compiler_params=params(40), cost_estimate=cost(3_000_000_000, 2 * slot_bytes), name='patch',
        )(mig_src, mig_dst, *came, got, near, gown, *weights, *new)
        return (y_out, *new)

    row_spec = P(('dp', 'ep'), None)
    slot_spec = P('ep', None, None)
    return jax.shard_map(local_step, mesh=mesh, in_specs=(row_spec, row_spec, row_spec, slot_spec, slot_spec, slot_spec, P(), P(), P()), out_specs=(row_spec, slot_spec, slot_spec, slot_spec), check_vma=False)
```

time: 109 us -> 95.2 us (0.87); the launches traced: 108 us -> 95 us
  Pallas kernels: 96.4 us -> 83.2 us
  starting transfers between devices: 4.05 us -> 6.63 us
  other arithmetic: 1.81 us -> 0.39 us
    pallas_call x4 -> x5, Pallas kernels: 92 us -> 76.7 us  [the longest x1 16.8 us: local_step(): pl.pallas_call(dispatch_kernel, out_shape=(bf(groups, tok, model), jax.Sh...]
    ppermute x4 -> x6, starting transfers between devices: 4.05 us -> 6.63 us  [the longest x3 3.54 us: hop(): lax.ppermute(to_x_rows, 'ep', to_x)]
    pallas_call x1, Pallas kernels: 0.88 us -> 3.02 us  [local_step(): pl.pallas_call(patch_kernel, out_shape=shapes, in_specs=[SMEM, SMEM] + [V...]
    select_n x2 -> x3, other arithmetic: 1.81 us -> 0.39 us  [the longest x2 0.3 us: onward(): jnp.where(chip_own, held[k_y], from_x)]
  transfers between devices with their start and end apart: 4 -> 6, of which waited for: 0 -> 2; matrix products, arithmetic and copies ran while one was open for 0% -> 0% of each run, Pallas kernels for 49% -> 45%
where the time goes in v4:
time: 95.2 us; the launch traced here: 95 us
  Pallas kernels  83.2 us (87%)
  starting transfers between devices  6.63 us (7%)
  local copies, waits for them, and re-layouts  2.72 us (3%)
  between operations  1.34 us (1%)
    pallas_call x1, Pallas kernels, local_step(): pl.pallas_call(dispatch_kernel, out_shape=(bf(groups, tok, model), jax.Sh...  16.8 us
    pallas_call x1, Pallas kernels, local_step(): pl.pallas_call(combine_kernel, out_shape=(bf(tok, model), bf(6, part, wid...  16.7 us
    pallas_call x1, Pallas kernels, local_step(): pl.pallas_call(first_kernel, out_shape=shapes + (bf(late, model), bf(tota...  15.7 us
    pallas_call x1, Pallas kernels, local_step(): pl.pallas_call(third_kernel, out_shape=shapes + (jax.ShapeDtypeStruct((to...  14.6 us
    pallas_call x1, Pallas kernels, local_step(): pl.pallas_call(second_kernel, out_shape=shapes + (bf(SECOND * per, model)...  13 us
    ppermute x3, starting transfers between devices, hop(): lax.ppermute(to_x_rows, 'ep', to_x)  3.54 us
    pallas_call x1, Pallas kernels, local_step(): pl.pallas_call(pack_kernel, out_shape=(jax.ShapeDtypeStruct((16, 128), F3...  3.48 us
    ppermute x3, starting transfers between devices, hop(): lax.ppermute(to_y_rows, 'ep', to_y)  3.09 us
  transfers between devices with their start and end apart: 6, of which 2 were waited for; matrix products, arithmetic and copies ran while one was open for 0% of the time, Pallas kernels for 45%

profile of v4, /device:TPU:0, one launch (start us, length us, event | category | flops | bytes accessed | tf_op | source)
XLA Modules:
  0.0 95.0 jit_solution(3117754504933504555)
XLA Ops:
  0.6 0.0 copy-start.1
  0.6 0.7 copy-done.1
  1.3 0.0 copy-start.2
  1.3 0.7 copy-done.2
  2.0 0.0 copy-start.3
  2.0 0.7 copy-done.3
  2.7 0.0 copy-start
  2.7 3.5 %pack.1 = (f32[16,128]{1,0:T(8,128)S(1)}, s32[1]{0:T(128)}, s32[1]{0:T(128)}, bf16[2304,512]{1,0:T(8,128)(2,1)S(1)}, bf16[2304,512]{1,0:T(8,128)(2,1)S(1)}) custom-call(s32[2]{0:T(128)S(1)} %copy-done.3, s32[8,64]{1,0:T(8,128)S(1)} %bitcast.5, f32[8,64]{1,0:T(8,128)S(1)} %bitcast.6, bf16[16,1536,512]{2,1,0:T(8,128)(2,1)} %wg.9, bf16[16,1536,512]{2,1,0:T(8,128)(2,1)} %wu.9, ...), custom_call_target="tpu_custom_call" | custom-call | flops 2000000000 | bytes 9437184 | tf_op jit(solution)/shard_map/pack/pallas_call | solution.py:431
  6.2 0.0 copy-done
  6.2 0.0 copy-start.6
  6.2 16.8 %dispatch.1 = (bf16[8,64,1536]{2,1,0:T(8,128)(2,1)S(1)}, f32[8,16,128]{2,1,0:T(8,128)S(1)}, bf16[2304,512]{1,0:T(8,128)(2,1)S(1)}, bf16[576,512]{1,0:T(8,128)(2,...) custom-call(s32[1]{0:T(128)} %get-tuple-element.63.mine_ref, ...), custom_call_target="tpu_custom_call" | custom-call | flops 8000000000 | bytes 2000000 | tf_op jit(solution)/shard_map/dispatch/pallas_call | solution.py:440
  23.0 1.5 %collective-permute-start = (bf16[576,512]{1,0:T(8,128)(2,1)S(1)}, bf16[576,512]{1,0:T(8,128)(2,1)S(1)}, u32[]{:S(2)}, u32[]{:S(2)}) collective-permute-start(bf16[576,512]{1,0:T(8,128)(2,1)S(1)} %get-tuple-element.69), channel_id=1, source_target_pairs={{0,2},{1,3},{2,0},{3,1},{4,6},{5,7},{6,4},{7,5}} | collective-permute-start | bytes 1769480 | tf_op jit(solution)/shard_map/ppermute | solution.py:454
  24.4 0.6 collective-permute-start.1
  25.0 0.0 copy-done.6
  25.0 15.7 %first.1 = (bf16[16,1536,512]{2,1,0:T(8,128)(2,1)}, bf16[16,1536,512]{2,1,0:T(8,128)(2,1)}, bf16[16,512,1536]{2,1,0:T(8,128)(2,1)}, bf16[512,1536]{1,0:T(8,128)(...) custom-call(s32[128]{0:T(128)S(1)} %copy-done.6, ...), custom_call_target="tpu_custom_call" | custom-call | flops 30000001024 | bytes 47185920 | tf_op jit(solution)/shard_map/first/pallas_call | solution.py:467
  41.2 0.0 collective-permute-done.rx1
  41.2 0.0 collective-permute-done.1.ry1
  41.3 0.1 broadcast_select_fusion.3
  41.3 0.1 broadcast_select_fusion.2
  41.4 1.0 %collective-permute-start.2 = (bf16[576,512]{1,0:T(8,128)(2,1)S(1)}, bf16[576,512]{1,0:T(8,128)(2,1)S(1)}, u32[]{:S(2)}, u32[]{:S(2)}) collective-permute-start(bf16[576,512]{1,0:T(8,128)(2,1)S(1)} %broadcast_select_fusion.3), channel_id=1, source_target_pairs={{0,2},{1,3},{2,0},{3,1},{4,6},{5,7},{6,4},{7,5}} | collective-permute-start | bytes 1769480 | tf_op jit(solution)/shard_map/ppermute | solution.py:454
  42.4 1.1 %collective-permute-start.3 = (bf16[576,512]{1,0:T(8,128)(2,1)S(1)}, bf16[576,512]{1,0:T(8,128)(2,1)S(1)}, u32[]{:S(2)}, u32[]{:S(2)}) collective-permute-start(bf16[576,512]{1,0:T(8,128)(2,1)S(1)} %broadcast_select_fusion.2), channel_id=1, source_target_pairs={{0,4},{1,5},{2,6},{3,7},{4,0},{5,1},{6,2},{7,3}} | collective-permute-start | bytes 1769480 | tf_op jit(solution)/shard_map/ppermute | solution.py:454
  43.5 13.0 %second.1 = (bf16[16,1536,512]{2,1,0:T(8,128)(2,1)}, bf16[16,1536,512]{2,1,0:T(8,128)(2,1)}, bf16[16,512,1536]{2,1,0:T(8,128)(2,1)}, bf16[256,1536]{1,0:T(8,128)(2,1)S(1)}) custom-call(bf16[512,1536]{1,0:T(8,128)(2,1)S(1)} %get-tuple-element.100.xg, ...), custom_call_target="tpu_custom_call", output_to_operand_aliasing={{0}: (5, {}), {1}: (6, {}), {2}: (7, {})} | custom-call | flops 30000001024 | bytes 37748736 | tf_op jit(solution)/shard_map/second/pallas_call | solution.py:479
  56.4 0.1 collective-permute-done.2.rx2
  56.5 0.7 collective-permute-done.3.ry2
  57.2 0.2 broadcast_select_fusion
  57.4 1.1 %collective-permute-start.4 = (bf16[576,512]{1,0:T(8,128)(2,1)S(1)}, bf16[576,512]{1,0:T(8,128)(2,1)S(1)}, u32[]{:S(2)}, u32[]{:S(2)}) collective-permute-start(bf16[576,512]{1,0:T(8,128)(2,1)S(1)} %get-tuple-element.108), channel_id=1, source_target_pairs={{0,2},{1,3},{2,0},{3,1},{4,6},{5,7},{6,4},{7,5}} | collective-permute-start | bytes 1769480 | tf_op jit(solution)/shard_map/ppermute | solution.py:454
  58.5 1.5 %collective-permute-start.5 = (bf16[576,512]{1,0:T(8,128)(2,1)S(1)}, bf16[576,512]{1,0:T(8,128)(2,1)S(1)}, u32[]{:S(2)}, u32[]{:S(2)}) collective-permute-start(bf16[576,512]{1,0:T(8,128)(2,1)S(1)} %get-tuple-element.109), channel_id=1, source_target_pairs={{0,4},{1,5},{2,6},{3,7},{4,0},{5,1},{6,2},{7,3}} | collective-permute-start | bytes 1769480 | tf_op jit(solution)/shard_map/ppermute | solution.py:454
  59.9 14.6 %third.1 = (bf16[16,1536,512]{2,1,0:T(8,128)(2,1)}, bf16[16,1536,512]{2,1,0:T(8,128)(2,1)}, bf16[16,512,1536]{2,1,0:T(8,128)(2,1)}, f32[512,1536]{1,0:T(8,128)S(1)}) custom-call(bf16[512,1536]{1,0:T(8,128)(2,1)S(1)} %get-tuple-element.100.xg, f32[512,128]{1,0:T(8,128)S(1)} %get-tuple-element.91.gr_ref, ...), custom_call_target="tpu_custom_call", output_to_operand_aliasing={{0}: (8, {}), {1}: (9, {}), {2}: (10, {})} | custom-call | flops 30000001024 | bytes 37748736 | tf_op jit(solution)/shard_map/third/pallas_call | solution.py:489
  74.5 0.0 collective-permute-done.4.rx3
  74.5 0.0 collective-permute-done.5.ry3
  74.5 0.0 copy-start.4
  74.5 0.0 copy-start.5
  74.5 16.7 %combine.1 = (bf16[64,1536]{1,0:T(8,128)(2,1)S(1)}, bf16[6,576,512]{2,1,0:T(8,128)(2,1)S(1)}, bf16[2304,512]{1,0:T(8,128)(2,1)S(1)}) custom-call(f32[8,64,1536]{2,1,0:T(8,128)S(1)} %bitcast.7, bf16[64,1536]{1,0:T(8,128)(2,1)S(1)} %copy-done, bf16[576,512]{1,0:T(8,128)(2,1)S(1)} %collective-permute-done.rx1, bf16[576,512]{1,0:T(8,128)(2,1)S(1)} %collective-permute-done.2.rx2, ...), custom_call_target="tpu_custom_call" | custom-call | flops 16000000000 | bytes 4000000 | tf_op jit(solution)/shard_map/combine/pallas_call | solution.py:499
  91.3 0.0 copy-done.4
  91.3 0.0 copy-done.5
  91.3 3.0 %patch.1 = (bf16[16,1536,512]{2,1,0:T(8,128)(2,1)}, bf16[16,1536,512]{2,1,0:T(8,128)(2,1)}, bf16[16,512,1536]{2,1,0:T(8,128)(2,1)}) custom-call(s32[2]{0:T(128)S(1)} %copy-done.4, s32[2]{0:T(128)S(1)} %copy-done.5, bf16[576,512]{1,0:T(8,128)(2,1)S(1)} %collective-permute-done.rx1, ...), custom_call_target="tpu_custom_call", output_to_operand_aliasing={{0}: (14, {}), {1}: (15, {}), {2}: (16, {})} | custom-call | flops 3000000000 | bytes 9437184 | tf_op jit(solution)/shard_map/patch/pallas_call | solution.py:510
  94.3 0.7 copy.32
Async XLA Ops:
  0.6 0.7 copy-start.1
  1.3 0.7 copy-start.2
  2.0 0.7 copy-start.3
  2.7 3.5 %copy-start = (bf16[64,1536]{1,0:T(8,128)(2,1)S(1)}, bf16[64,1536]{1,0:T(8,128)(2,1)}, u32[]{:S(2)}) copy-start(bf16[64,1536]{1,0:T(8,128)(2,1)} %x_ref.3) | copy-start | bytes 589828
  6.2 18.8 %copy-start.6 = (s32[128]{0:T(128)S(1)}, s32[128]{0:T(128)}, u32[]{:S(2)}) copy-start(s32[128]{0:T(128)} %old_map.1) | copy-start | bytes 1540
  23.0 18.3 %collective-permute-start = (bf16[576,512]{1,0:T(8,128)(2,1)S(1)}, bf16[576,512]{1,0:T(8,128)(2,1)S(1)}, u32[]{:S(2)}, u32[]{:S(2)}) collective-permute-start(bf16[576,512]{1,0:T(8,128)(2,1)S(1)} %get-tuple-element.69), channel_id=1, source_target_pairs={{0,2},{1,3},{2,0},{3,1},{4,6},{5,7},{6,4},{7,5}} | collective-permute-start | bytes 1769480 | tf_op jit(solution)/shard_map/ppermute | solution.py:454
  24.4 16.8 %collective-permute-start.1 = (bf16[576,512]{1,0:T(8,128)(2,1)S(1)}, bf16[576,512]{1,0:T(8,128)(2,1)S(1)}, u32[]{:S(2)}, u32[]{:S(2)}) collective-permute-start(bf16[576,512]{1,0:T(8,128)(2,1)S(1)} %get-tuple-element.70), channel_id=1, source_target_pairs={{0,4},{1,5},{2,6},{3,7},{4,0},{5,1},{6,2},{7,3}} | collective-permute-start | bytes 1769480 | tf_op jit(solution)/shard_map/ppermute | solution.py:454
  41.4 15.1 %collective-permute-start.2 = (bf16[576,512]{1,0:T(8,128)(2,1)S(1)}, bf16[576,512]{1,0:T(8,128)(2,1)S(1)}, u32[]{:S(2)}, u32[]{:S(2)}) collective-permute-start(bf16[576,512]{1,0:T(8,128)(2,1)S(1)} %broadcast_select_fusion.3), channel_id=1, source_target_pairs={{0,2},{1,3},{2,0},{3,1},{4,6},{5,7},{6,4},{7,5}} | collective-permute-start | bytes 1769480 | tf_op jit(solution)/shard_map/ppermute | solution.py:454
  42.4 14.8 %collective-permute-start.3 = (bf16[576,512]{1,0:T(8,128)(2,1)S(1)}, bf16[576,512]{1,0:T(8,128)(2,1)S(1)}, u32[]{:S(2)}, u32[]{:S(2)}) collective-permute-start(bf16[576,512]{1,0:T(8,128)(2,1)S(1)} %broadcast_select_fusion.2), channel_id=1, source_target_pairs={{0,4},{1,5},{2,6},{3,7},{4,0},{5,1},{6,2},{7,3}} | collective-permute-start | bytes 1769480 | tf_op jit(solution)/shard_map/ppermute | solution.py:454
  57.4 17.1 %collective-permute-start.4 = (bf16[576,512]{1,0:T(8,128)(2,1)S(1)}, bf16[576,512]{1,0:T(8,128)(2,1)S(1)}, u32[]{:S(2)}, u32[]{:S(2)}) collective-permute-start(bf16[576,512]{1,0:T(8,128)(2,1)S(1)} %get-tuple-element.108), channel_id=1, source_target_pairs={{0,2},{1,3},{2,0},{3,1},{4,6},{5,7},{6,4},{7,5}} | collective-permute-start | bytes 1769480 | tf_op jit(solution)/shard_map/ppermute | solution.py:454
  58.5 16.0 %collective-permute-start.5 = (bf16[576,512]{1,0:T(8,128)(2,1)S(1)}, bf16[576,512]{1,0:T(8,128)(2,1)S(1)}, u32[]{:S(2)}, u32[]{:S(2)}) collective-permute-start(bf16[576,512]{1,0:T(8,128)(2,1)S(1)} %get-tuple-element.109), channel_id=1, source_target_pairs={{0,4},{1,5},{2,6},{3,7},{4,0},{5,1},{6,2},{7,3}} | collective-permute-start | bytes 1769480 | tf_op jit(solution)/shard_map/ppermute | solution.py:454
  74.5 16.8 %copy-start.4 = (s32[2]{0:T(128)S(1)}, s32[2]{0:T(128)}, u32[]{:S(2)}) copy-start(s32[2]{0:T(128)} %src.3) | copy-start | bytes 28
  74.5 16.8 %copy-start.5 = (s32[2]{0:T(128)S(1)}, s32[2]{0:T(128)}, u32[]{:S(2)}) copy-start(s32[2]{0:T(128)} %dst.1) | copy-start | bytes 28

commit v5 on v4

--- a/solution.py
+++ b/solution.py
@@ -12,9 +12,9 @@
 SMEM = pl.BlockSpec(memory_space=pltpu.SMEM)
 HBM = pl.BlockSpec(memory_space=pltpu.HBM)
 MIB = 1024 * 1024
-HELD = 2
-EARLY, SECOND, THIRD = 6, 4, 4
-FIRST = EARLY + 2
+HELD = 1
+EARLY, SECOND, THIRD = 7, 4, 4
+FIRST = EARLY + 1
 
 
 def places():
@@ -37,16 +37,12 @@
     return pltpu.make_async_remote_copy(src, dst, send, recv, device_id={'ep': dev}, device_id_type=MESH)
 
 
-def pack_kernel(src, ids_ref, gate_ref, wg, wu, wd, meta_ref, mine_ref, chip_ref, send_ref, own_ref, sem):
+def pack_kernel(src, wg, wu, wd, mine_ref, chip_ref, send_ref, own_ref, sem):
     me = lax.axis_index('ep')
     slots, depth, width = wg.shape
     owner = [src[i] // slots for i in range(2)]
     mine_ref[0] = jnp.where((owner[0] == me) | (owner[1] == me), 1, 0)
     chip_ref[0] = jnp.where((owner[0] // 2 == me // 2) | (owner[1] // 2 == me // 2), 1, 0)
-    tok = ids_ref.shape[1]
-    meta_ref[...] = jnp.zeros_like(meta_ref)
-    meta_ref[0:8, 0:tok] = ids_ref[...].astype(F32)
-    meta_ref[8:16, 0:tok] = gate_ref[...]
     half = 3 * depth // 2
     slot = jnp.where(src[0] // slots == me, src[0], src[1]) % slots
 
@@ -77,7 +73,7 @@
         run(first(send_ref, 0) + second(own_ref, 2))
 
 
-def dispatch_kernel(mine_ref, x_ref, meta_ref, slot_ref, own, wg, wu, wd, xall, mall, near, h0, h1, h2, h3, *rest):
+def dispatch_kernel(mine_ref, x_ref, ids_ref, gate_ref, slot_ref, own, wg, wu, wd, xall, iall, gall, near, h0, h1, h2, h3, *rest):
     me, core, chip, sib, chips = places()
     peers = [c * 2 + core for c in chips]
     bufs, (send, recv, sem) = rest[:-3], rest[-3:]
@@ -89,19 +85,21 @@
         copy.start()
     enter(peers + [sib])
 
-    def pair(k, src_x, src_m, block, dev):
-        return (remote(src_x, xall.at[block], send.at[2 * k], recv.at[2 * k], dev),
-                remote(src_m, mall.at[block], send.at[2 * k + 1], recv.at[2 * k + 1], dev))
-
-    first = [pair(k, x_ref, meta_ref, me, peers[k]) for k in range(3)]
-    first.append(pair(3, x_ref, meta_ref, me, sib))
-    for group in first:
-        for copy in group:
-            copy.start()
-    slot = remote(slot_ref, near, send.at[14], recv.at[14], sib)
+    alls = (xall, iall, gall)
+
+    def group(k, refs, block, dev):
+        return [remote(ref, to.at[block], send.at[3 * k + n], recv.at[3 * k + n], dev)
+                for n, (ref, to) in enumerate(zip(refs, alls))]
+
+    mine = (x_ref, ids_ref, gate_ref)
+    first = [group(k, mine, me, dev) for k, dev in enumerate(peers + [sib])]
+    for copies in first:
+        for copy in copies:
+            copy.start()
+    slot = remote(slot_ref, near, send.at[21], recv.at[21], sib)
     slot.start()
-    xall[pl.ds(me, 1)] = x_ref[...][None]
-    mall[pl.ds(me, 1)] = meta_ref[...][None]
+    for ref, to in zip(mine, alls):
+        to[pl.ds(me, 1)] = ref[...][None]
     slot.wait_recv()
     part = h0.shape[0]
     for k, held in enumerate((h0, h1, h2, h3)):
@@ -111,29 +109,38 @@
     for k in (1, 2, 0):
         for copy in first[k]:
             copy.wait_recv()
-        fwd = pair(4 + k, xall.at[peers[k]], mall.at[peers[k]], peers[k], sib)
+        fwd = group(4 + k, [to.at[peers[k]] for to in alls], peers[k], sib)
         for copy in fwd:
             copy.start()
         second.append(fwd)
     for copy in first[3]:
         copy.wait_recv()
-    for group in first:
-        for copy in group:
+    for copies in first:
+        for copy in copies:
             copy.wait_send()
-    for group in second:
-        for copy in group:
+    for copies in second:
+        for copy in copies:
             copy.wait()
     slot.wait_send()
     for copy in reads:
         copy.wait()
 
 
-def stream(slots0, count, w, w_new, bufs, sem_in, sem_out):
+def lands(src, dst, slot, slots):
+    me = lax.axis_index('ep')
+    local = (src[0] // slots == me) & (src[1] // slots == me)
+    for i in range(2):
+        slot = jnp.where(local & (slot == src[i] % slots), dst[i] % slots + slots, slot)
+    return slot % slots
+
+
+def stream(src, dst, slots0, w, w_new, bufs, sem_in, sem_out):
     def load(i):
         return [pltpu.make_async_copy(w[k].at[slots0 + i], bufs[k].at[i], sem_in.at[k, i]) for k in range(3)]
 
     def drain(i):
-        return [pltpu.make_async_copy(bufs[k].at[i], w_new[k].at[slots0 + i], sem_out.at[k, i]) for k in range(3)]
+        to = lands(src, dst, slots0 + i, w[0].shape[0])
+        return [pltpu.make_async_copy(bufs[k].at[i], w_new[k].at[to], sem_out.at[k, i]) for k in range(3)]
 
     return load, drain
 
@@ -146,10 +153,10 @@
     return (o * gate).astype(BF16)
 
 
-def first_kernel(old_map, x_ref, mall, *rest):
-    bufs, rest = rest[:-22], rest[-22:]
-    wg, wu, wd, wg_new, wu_new, wd_new, xg_out, at_ref, gr_out, c_ref, eg, eu, ed, xg, a_ref, gr_ref, pos, gsc, meta = rest[:19]
-    more_in, more_out, sem_out = rest[19:]
+def first_kernel(src, dst, old_map, x_ref, iall, gall, *rest):
+    bufs, rest = rest[:-21], rest[-21:]
+    wg, wu, wd, wg_new, wu_new, wd_new, xg_out, at_ref, gr_out, c_ref, eg, eu, ed, xg, a_ref, gr_ref, pos, gsc = rest[:18]
+    more_in, more_out, sem_out = rest[18:]
     me = lax.axis_index('ep')
     slots, tok, cap = wg_new.shape[0], 64, 8
     total = x_ref.shape[0]
@@ -157,23 +164,19 @@
     rows = devs * cap
     done = FIRST * rows
     more = (eg, eu, ed)
-    load, drain = stream(EARLY, FIRST - EARLY, (wg, wu, wd), (wg_new, wu_new, wd_new), more, more_in, more_out)
+    load, drain = stream(src, dst, EARLY, (wg, wu, wd), (wg_new, wu_new, wd_new), more, more_in, more_out)
     for i in range(FIRST - EARLY):
         for copy in load(i):
             copy.start()
     held = len(bufs) // 3
     size = EARLY // held
-    drains = [pltpu.make_async_copy(bufs[k * held + i], new.at[pl.ds(i * size, size)], sem_out.at[k, i])
+    drains = [pltpu.make_async_copy(bufs[k * held + i].at[0], new.at[lands(src, dst, i, slots)], sem_out.at[k, i])
               for i in range(held) for k, new in enumerate((wg_new, wu_new, wd_new))]
     for copy in drains:
         copy.start()
 
-    lane = lax.broadcasted_iota(jnp.int32, (16, 128), 1)
-    for p in range(devs // 2):
-        other = pltpu.roll(mall[2 * p + 1], 64, axis=1)
-        meta[:, pl.ds(128 * p, 128)] = jnp.where(lane < 64, mall[2 * p], other)
-    ids = meta[0:8, :]
-    gates = meta[8:16, :]
+    ids = jnp.concatenate([iall[d].astype(F32) for d in range(devs)], axis=1)
+    gates = jnp.concatenate([gall[d] for d in range(devs)], axis=1)
     hits, gs = [], []
     for j in range(slots):
         same = ids == old_map[me * slots + j].astype(F32)
@@ -239,14 +242,15 @@
             copy.wait()
 
 
-def later(first_slot, xg, gr_ref, w, w_new, c_ref, c_base, bufs, sem_in, sem_out, finish):
+def later(src, dst, first_slot, xg, gr_ref, w, w_new, c_ref, c_base, bufs, sem_in, sem_out, begin, finish):
     count = bufs[0].shape[0]
     rows = gr_ref.shape[0] // (w[0].shape[0] - FIRST)
-    load, drain = stream(first_slot, count, w, w_new, bufs, sem_in, sem_out)
+    load, drain = stream(src, dst, first_slot, w, w_new, bufs, sem_in, sem_out)
     for i in range(count):
         for copy in load(i):
             copy.start()
     base = (first_slot - FIRST) * rows
+    begin()
 
     @pl.loop(0, count)
     def _(i):
@@ -264,29 +268,33 @@
             copy.wait()
 
 
-def second_kernel(xg, gr_ref, wg, wu, wd, wg_old, wu_old, wd_old, wg_new, wu_new, wd_new, c_ref,
+def second_kernel(src, dst, xg, gr_ref, wg, wu, wd, wg_old, wu_old, wd_old, wg_new, wu_new, wd_new, c_ref,
                   bg, bu, bd, sem_in, sem_out):
-    later(FIRST, xg, gr_ref, (wg, wu, wd), (wg_new, wu_new, wd_new), c_ref, 0, (bg, bu, bd), sem_in, sem_out,
-          lambda: None)
-
-
-def third_kernel(xg, gr_ref, at_ref, c0, c1, wg, wu, wd, wg_old, wu_old, wd_old, wg_new, wu_new, wd_new, out_ref,
+    later(src, dst, FIRST, xg, gr_ref, (wg, wu, wd), (wg_new, wu_new, wd_new), c_ref, 0, (bg, bu, bd), sem_in, sem_out,
+          lambda: None, lambda: None)
+
+
+def third_kernel(src, dst, xg, gr_ref, at_ref, c0, c1, wg, wu, wd, wg_old, wu_old, wd_old, wg_new, wu_new, wd_new, out_ref,
                  bg, bu, bd, c_ref, sem_in, sem_out):
     cols = 256
     n0 = c0.shape[0]
     done = n0 + c1.shape[0]
 
-    def finish():
-        c_ref[0:n0, :] = c0[...]
-        c_ref[n0:done, :] = c1[...]
-
+    def over_columns(sums):
         @pl.loop(0, out_ref.shape[1] // cols)
         def _(n):
             at = pl.ds(pl.multiple_of(n * cols, cols), cols)
-            out_ref[:, at] = jnp.dot(at_ref[...], c_ref[:, at], preferred_element_type=F32)
-
-    later(FIRST + SECOND, xg, gr_ref, (wg, wu, wd), (wg_new, wu_new, wd_new), c_ref, done, (bg, bu, bd), sem_in, sem_out,
-          finish)
+            out_ref[:, at] = sums(at)
+
+    def begin():
+        over_columns(lambda at: jnp.dot(at_ref[:, 0:n0], c0[:, at], preferred_element_type=F32)
+                     + jnp.dot(at_ref[:, n0:done], c1[:, at], preferred_element_type=F32))
+
+    def finish():
+        over_columns(lambda at: out_ref[:, at] + jnp.dot(at_ref[:, done:], c_ref[:, at], preferred_element_type=F32))
+
+    later(src, dst, FIRST + SECOND, xg, gr_ref, (wg, wu, wd), (wg_new, wu_new, wd_new), c_ref, 0, (bg, bu, bd), sem_in, sem_out,
+          begin, finish)
 
 
 def combine_kernel(part, x_ref, rx1, rx2, rx3, ry1, ry2, ry3, own, y_ref, got, gown, near, summed, far, relay, last,
@@ -336,11 +344,13 @@
         copy.wait_send()
 
 
-def patch_kernel(src, dst, rx1, rx2, rx3, ry1, ry2, ry3, got, near, gown, wg, wu, wd, wg_old, wu_old, wd_old,
-                 wg_new, wu_new, wd_new, buf, sem):
+def patch_kernel(dst, y_ref, rx1, rx2, rx3, ry1, ry2, ry3, got, near, gown, wg_old, wu_old, wd_old,
+                 wg_new, wu_new, wd_new, y_out, sem):
+    put_y = pltpu.make_async_copy(y_ref, y_out, sem.at[13])
+    put_y.start()
     me = lax.axis_index('ep')
     core = me % 2
-    slots, depth, width = wg.shape
+    slots, depth, width = wg_new.shape
     part = rx1.shape[0]
     count = 3 * depth // part
     owner = [dst[i] // slots for i in range(2)]
@@ -381,20 +391,7 @@
         receive(case, [came[k] for k in order], [got.at[k] for k in order])
     receive(same_y & same_x, [near], [gown])
 
-    @pl.when(local)
-    def _():
-        for i in range(2):
-            s = src[i] % slots
-            copies = [pltpu.make_async_copy(wg.at[s], buf.at[pl.ds(0, depth)], sem.at[0]),
-                      pltpu.make_async_copy(wu.at[s], buf.at[pl.ds(depth, depth)], sem.at[1])]
-            for b in range(depth // width):
-                copies.append(pltpu.make_async_copy(wd.at[s, :, pl.ds(width * b, width)],
-                                                    buf.at[pl.ds(2 * depth + width * b, width)], sem.at[2 + b]))
-            for copy in copies:
-                copy.start()
-            for copy in copies:
-                copy.wait()
-            put([buf], dst[i] % slots)
+    put_y.wait()
 
 
 def cost(flops, moved):
@@ -411,6 +408,7 @@
 
     def local_step(x_loc, expert_ids, gate_val, w_gate, w_up, w_down, old_map, mig_src, mig_dst):
         tok, model = x_loc.shape
+        top = expert_ids.shape[1]
         slots, depth, width = w_gate.shape
         total = groups * tok
         per = groups * 8
@@ -428,24 +426,25 @@
         def bf(*shape):
             return jax.ShapeDtypeStruct(shape, BF16)
 
-        meta, i_own, chip_own, send, own = pl.pallas_call(
+        i_own, chip_own, send, own = pl.pallas_call(
             pack_kernel,
-            out_shape=(jax.ShapeDtypeStruct((16, 128), F32),) + (jax.ShapeDtypeStruct((1,), jnp.int32),) * 2 + (bf(half, width),) * 2,
-            in_specs=[SMEM, VMEM, VMEM, HBM, HBM, HBM], out_specs=(VMEM, SMEM, SMEM, VMEM, VMEM),
+            out_shape=(jax.ShapeDtypeStruct((1,), jnp.int32),) * 2 + (bf(half, width),) * 2,
+            in_specs=[SMEM, HBM, HBM, HBM], out_specs=(SMEM, SMEM, VMEM, VMEM),
             scratch_shapes=[dma((6,))], compiler_params=params(42),
             cost_estimate=cost(2_000_000_000, 2 * slot_bytes), name='pack',
-        )(mig_src, expert_ids.T, gate_val.T, *weights)
+        )(mig_src, *weights)
 
         part = half // 4
-        xall, mall, near, h0, h1, h2, h3, *bufs = pl.pallas_call(
+        xall, iall, gall, near, h0, h1, h2, h3, *bufs = pl.pallas_call(
             dispatch_kernel,
-            out_shape=(bf(groups, tok, model), jax.ShapeDtypeStruct((groups, 16, 128), F32), bf(half, width))
+            out_shape=(bf(groups, tok, model), jax.ShapeDtypeStruct((groups, top, tok), jnp.int32),
+                       jax.ShapeDtypeStruct((groups, top, tok), F32), bf(half, width))
             + (bf(part, width),) * 4 + tuple(bf(HELD, *w.shape[1:]) for w in weights for _ in range(EARLY // HELD)),
-            in_specs=[SMEM, VMEM, VMEM, ANY, VMEM, HBM, HBM, HBM], out_specs=(VMEM,) * (7 + 3 * (EARLY // HELD)),
-            scratch_shapes=[dma((15,)), dma((15,)), dma((3 * (EARLY // HELD),))],
+            in_specs=[SMEM, VMEM, VMEM, VMEM, ANY, VMEM, HBM, HBM, HBM], out_specs=(VMEM,) * (8 + 3 * (EARLY // HELD)),
+            scratch_shapes=[dma((22,)), dma((22,)), dma((3 * (EARLY // HELD),))],
             compiler_params=params(4, collective_id=0, has_side_effects=True),
             cost_estimate=cost(8_000_000_000, 2_000_000), name='dispatch',
-        )(i_own, x_loc, meta, send, own, *weights)
+        )(i_own, x_loc, expert_ids.T, gate_val.T, send, own, *weights)
 
         chip_own = chip_own[0] > 0
         held = (h0, h1, h2, h3)
@@ -467,33 +466,33 @@
         *new, xg, at, gr, c0 = pl.pallas_call(
             first_kernel,
             out_shape=shapes + (bf(late, model), bf(total, rows), jax.ShapeDtypeStruct((late, 128), F32), bf(FIRST * per, model)),
-            in_specs=[SMEM] + [VMEM] * (2 + 3 * (EARLY // HELD)) + [HBM] * 3, out_specs=(HBM,) * 3 + (VMEM,) * 4,
+            in_specs=[SMEM] * 3 + [VMEM] * (3 + 3 * (EARLY // HELD)) + [HBM] * 3, out_specs=(HBM,) * 3 + (VMEM,) * 4,
             scratch_shapes=room(FIRST - EARLY) + [
                 pltpu.VMEM((FIRST * per, model), BF16), pltpu.VMEM((rows, total), BF16), pltpu.VMEM((FIRST * per, 128), F32),
-                pltpu.VMEM((slots, total), F32), pltpu.VMEM((slots, total), F32), pltpu.VMEM((16, total), F32),
+                pltpu.VMEM((slots, total), F32), pltpu.VMEM((slots, total), F32),
                 dma((3, FIRST - EARLY)), dma((3, FIRST - EARLY)), dma((3, EARLY // HELD))],
-            compiler_params=params(16), cost_estimate=cost(30_000_000_000, (2 * FIRST - EARLY) * slot_bytes), name='first',
-        )(old_map, xall.reshape(total, model), mall, *bufs, *weights)
+            compiler_params=params(11), cost_estimate=cost(30_000_000_000, (2 * FIRST - EARLY) * slot_bytes), name='first',
+        )(mig_src, mig_dst, old_map, xall.reshape(total, model), iall, gall, *bufs, *weights)
 
         rx1, ry1, rx2, ry2, (xg, c0) = onward(1, 2, rx1, ry1, (xg, c0))
         *new, c1 = pl.pallas_call(
             second_kernel,
             out_shape=shapes + (bf(SECOND * per, model),),
-            in_specs=[VMEM] * 2 + [HBM] * 6, out_specs=(HBM,) * 3 + (VMEM,),
-            input_output_aliases={5: 0, 6: 1, 7: 2},
+            in_specs=[SMEM] * 2 + [VMEM] * 2 + [HBM] * 6, out_specs=(HBM,) * 3 + (VMEM,),
+            input_output_aliases={7: 0, 8: 1, 9: 2},
             scratch_shapes=room(SECOND) + [dma((3, SECOND))] * 2,
             compiler_params=params(40), cost_estimate=cost(30_000_000_000, 2 * SECOND * slot_bytes), name='second',
-        )(xg, gr, *weights, *new)
+        )(mig_src, mig_dst, xg, gr, *weights, *new)
 
         rx2, ry2, rx3, ry3, (xg, c1) = onward(2, 1, rx2, ry2, (xg, c1))
         *new, psum = pl.pallas_call(
             third_kernel,
             out_shape=shapes + (jax.ShapeDtypeStruct((total, model), F32),),
-            in_specs=[VMEM] * 5 + [HBM] * 6, out_specs=(HBM,) * 3 + (VMEM,),
-            input_output_aliases={8: 0, 9: 1, 10: 2},
-            scratch_shapes=room(THIRD) + [pltpu.VMEM((rows, model), BF16)] + [dma((3, THIRD))] * 2,
+            in_specs=[SMEM] * 2 + [VMEM] * 5 + [HBM] * 6, out_specs=(HBM,) * 3 + (VMEM,),
+            input_output_aliases={10: 0, 11: 1, 12: 2},
+            scratch_shapes=room(THIRD) + [pltpu.VMEM((THIRD * per, model), BF16)] + [dma((3, THIRD))] * 2,
             compiler_params=params(40), cost_estimate=cost(30_000_000_000, 2 * THIRD * slot_bytes), name='third',
-        )(xg, gr, at, c0, c1, *weights, *new)
+        )(mig_src, mig_dst, xg, gr, at, c0, c1, *weights, *new)
 
         came = (rx1, rx2, rx3, ry1, ry2, ry3)
         y_out, got, gown = pl.pallas_call(
@@ -507,14 +506,14 @@
             cost_estimate=cost(16_000_000_000, 4_000_000), name='combine',
         )(psum.reshape(groups, tok, model), x_loc, *came, own)
 
-        new = pl.pallas_call(
+        *new, y_out = pl.pallas_call(
             patch_kernel,
-            out_shape=shapes,
-            in_specs=[SMEM, SMEM] + [VMEM] * 9 + [HBM] * 6, out_specs=(HBM,) * 3,
-            input_output_aliases={14: 0, 15: 1, 16: 2},
-            scratch_shapes=[pltpu.VMEM((3 * depth, width), BF16), dma((13,))],
+            out_shape=shapes + (bf(tok, model),),
+            in_specs=[SMEM] + [VMEM] * 10 + [HBM] * 3, out_specs=(HBM,) * 4,
+            input_output_aliases={11: 0, 12: 1, 13: 2},
+            scratch_shapes=[dma((14,))],
             compiler_params=params(40), cost_estimate=cost(3_000_000_000, 2 * slot_bytes), name='patch',
-        )(mig_src, mig_dst, *came, got, near, gown, *weights, *new)
+        )(mig_dst, y_out, *came, got, near, gown, *new)
         return (y_out, *new)
 
     row_spec = P(('dp', 'ep'), None)

time: 95.2 us -> 92.3 us (0.970)
  local copies, waits for them, and re-layouts: 2.72 us -> 0.72 us
    unnamed x15 -> x14, local copies, waits for them, and re-layouts: 2.72 us -> 0.72 us
    pallas_call x2, Pallas kernels: 6.5 us -> 4.84 us  [the longest x1 3.48 us: local_step(): pl.pallas_call(pack_kernel, out_shape=(jax.ShapeDtypeStruct((1,), jnp.int...]
    pallas_call x1, Pallas kernels: 16.7 us -> 18.2 us  [local_step(): pl.pallas_call(combine_kernel, out_shape=(bf(tok, model), bf(6, part, wid...]
    pallas_call x1, Pallas kernels: 15.7 us -> 14.2 us  [local_step(): pl.pallas_call(first_kernel, out_shape=shapes + (bf(late, model), bf(tota...]
    pallas_call x1, Pallas kernels: 13 us -> 14.2 us  [local_step(): pl.pallas_call(second_kernel, out_shape=shapes + (bf(SECOND * per, model)...]
  transfers between devices with their start and end apart: 6 -> 6, of which waited for: 2 -> 0; matrix products, arithmetic and copies ran while one was open for 0% -> 0% of each run, Pallas kernels for 45% -> 47%
where the time goes in v5:
time: 92.3 us; the launch traced here: 91.4 us
  Pallas kernels  82.9 us (90%)
  starting transfers between devices  6.14 us (7%)
  between operations  1.38 us (1%)
    pallas_call x1, Pallas kernels, local_step(): pl.pallas_call(combine_kernel, out_shape=(bf(tok, model), bf(6, part, wid...  18.2 us
    pallas_call x1, Pallas kernels, local_step(): pl.pallas_call(dispatch_kernel, out_shape=(bf(groups, tok, model), jax.Sh...  17.1 us
    pallas_call x1, Pallas kernels, local_step(): pl.pallas_call(third_kernel, out_shape=shapes + (jax.ShapeDtypeStruct((to...  14.3 us
    pallas_call x1, Pallas kernels, local_step(): pl.pallas_call(second_kernel, out_shape=shapes + (bf(SECOND * per, model)...  14.2 us
    pallas_call x1, Pallas kernels, local_step(): pl.pallas_call(first_kernel, out_shape=shapes + (bf(late, model), bf(tota...  14.2 us
    ppermute x3, starting transfers between devices, hop(): lax.ppermute(to_x_rows, 'ep', to_x)  3.95 us
    pallas_call x1, Pallas kernels, local_step(): pl.pallas_call(pack_kernel, out_shape=(jax.ShapeDtypeStruct((1,), jnp.int...  3.48 us
    ppermute x3, starting transfers between devices, hop(): lax.ppermute(to_y_rows, 'ep', to_y)  2.19 us
  transfers between devices with their start and end apart: 6, of which 0 were waited for; matrix products, arithmetic and copies ran while one was open for 0% of the time, Pallas kernels for 47%

profile of v5, /device:TPU:0, one launch (start us, length us, event | category | flops | bytes accessed | tf_op | source)
XLA Modules:
  0.0 91.4 jit_solution(15411212887631123097)
XLA Ops:
  0.6 0.0 copy-start
  0.6 0.0 copy-start.1
  0.7 0.7 copy-done.1
  1.3 0.0 copy-start.4
  1.3 0.0 copy-start.5
  1.3 3.5 %pack.1 = (s32[1]{0:T(128)}, s32[1]{0:T(128)}, bf16[2304,512]{1,0:T(8,128)(2,1)S(1)}, bf16[2304,512]{1,0:T(8,128)(2,1)S(1)}) custom-call(s32[2]{0:T(128)S(1)} %copy-done.1, bf16[16,1536,512]{2,1,0:T(8,128)(2,1)} %wg.7, bf16[16,1536,512]{2,1,0:T(8,128)(2,1)} %wu.7, bf16[16,512,1536]{2,1,0:T(8,128)(2,1)} %wd.7), custom_call_target="tpu_custom_call" | custom-call | flops 2000000000 | bytes 9437184 | tf_op jit(solution)/shard_map/pack/pallas_call | solution.py:429
  4.8 0.0 copy-done
  4.8 0.0 copy-done.4
  4.9 0.0 copy-done.5
  4.9 0.0 copy-start.2
  4.9 0.0 copy-start.3
  4.9 0.0 copy-start.6
  4.9 17.1 %dispatch.1 = (bf16[8,64,1536]{2,1,0:T(8,128)(2,1)S(1)}, s32[8,8,64]{2,1,0:T(8,128)S(1)}, f32[8,8,64]{2,1,0:T(8,128)S(1)}, bf16[2304,512]{1,0:T(8,128)(2,1)S(1)}...) custom-call(s32[1]{0:T(128)} %get-tuple-element.76.mine_ref, ...), custom_call_target="tpu_custom_call" | custom-call | flops 8000000000 | bytes 2000000 | tf_op jit(solution)/shard_map/dispatch/pallas_call | solution.py:438
  22.0 1.5 %collective-permute-start = (bf16[576,512]{1,0:T(8,128)(2,1)S(1)}, bf16[576,512]{1,0:T(8,128)(2,1)S(1)}, u32[]{:S(2)}, u32[]{:S(2)}) collective-permute-start(bf16[576,512]{1,0:T(8,128)(2,1)S(1)} %get-tuple-element.81), channel_id=1, source_target_pairs={{0,2},{1,3},{2,0},{3,1},{4,6},{5,7},{6,4},{7,5}} | collective-permute-start | bytes 1769480 | tf_op jit(solution)/shard_map/ppermute | solution.py:453
  23.4 0.6 collective-permute-start.1
  24.0 0.0 copy-done.2
  24.0 0.0 copy-done.3
  24.0 0.0 copy-done.6
  24.0 14.2 %first.1 = (bf16[16,1536,512]{2,1,0:T(8,128)(2,1)}, bf16[16,1536,512]{2,1,0:T(8,128)(2,1)}, bf16[16,512,1536]{2,1,0:T(8,128)(2,1)}, bf16[512,1536]{1,0:T(8,128)(...) custom-call(s32[2]{0:T(128)S(1)} %copy-done.2, s32[2]{0:T(128)S(1)} %copy-done.3, ...), custom_call_target="tpu_custom_call" | custom-call | flops 30000001024 | bytes 42467328 | tf_op jit(solution)/shard_map/first/pallas_call | solution.py:466
  38.8 0.0 collective-permute-done.rx1
  38.8 0.0 collective-permute-done.1.ry1
  38.8 0.1 broadcast_select_fusion.3
  38.9 0.1 broadcast_select_fusion.2
  38.9 1.0 %collective-permute-start.2 = (bf16[576,512]{1,0:T(8,128)(2,1)S(1)}, bf16[576,512]{1,0:T(8,128)(2,1)S(1)}, u32[]{:S(2)}, u32[]{:S(2)}) collective-permute-start(bf16[576,512]{1,0:T(8,128)(2,1)S(1)} %broadcast_select_fusion.3), channel_id=1, source_target_pairs={{0,2},{1,3},{2,0},{3,1},{4,6},{5,7},{6,4},{7,5}} | collective-permute-start | bytes 1769480 | tf_op jit(solution)/shard_map/ppermute | solution.py:453
  39.9 1.1 %collective-permute-start.3 = (bf16[576,512]{1,0:T(8,128)(2,1)S(1)}, bf16[576,512]{1,0:T(8,128)(2,1)S(1)}, u32[]{:S(2)}, u32[]{:S(2)}) collective-permute-start(bf16[576,512]{1,0:T(8,128)(2,1)S(1)} %broadcast_select_fusion.2), channel_id=1, source_target_pairs={{0,4},{1,5},{2,6},{3,7},{4,0},{5,1},{6,2},{7,3}} | collective-permute-start | bytes 1769480 | tf_op jit(solution)/shard_map/ppermute | solution.py:453
  41.0 14.2 %second.1 = (bf16[16,1536,512]{2,1,0:T(8,128)(2,1)}, bf16[16,1536,512]{2,1,0:T(8,128)(2,1)}, bf16[16,512,1536]{2,1,0:T(8,128)(2,1)}, bf16[256,1536]{1,0:T(8,128)(2,1)S(1)}) custom-call(s32[2]{0:T(128)S(1)} %copy-done.2, s32[2]{0:T(128)S(1)} %copy-done.3, ...), custom_call_target="tpu_custom_call", output_to_operand_aliasing={{0}: (7, {}), {1}: (8, {}), {2}: (9, {})} | custom-call | flops 30000001024 | bytes 37748736 | tf_op jit(solution)/shard_map/second/pallas_call | solution.py:478
  55.2 0.0 collective-permute-done.2.rx2
  55.2 0.0 collective-permute-done.3.ry2
  55.2 0.1 broadcast_select_fusion
  55.4 1.5 %collective-permute-start.4 = (bf16[576,512]{1,0:T(8,128)(2,1)S(1)}, bf16[576,512]{1,0:T(8,128)(2,1)S(1)}, u32[]{:S(2)}, u32[]{:S(2)}) collective-permute-start(bf16[576,512]{1,0:T(8,128)(2,1)S(1)} %get-tuple-element.133), channel_id=1, source_target_pairs={{0,2},{1,3},{2,0},{3,1},{4,6},{5,7},{6,4},{7,5}} | collective-permute-start | bytes 1769480 | tf_op jit(solution)/shard_map/ppermute | solution.py:453
  56.9 0.6 collective-permute-start.5
  57.4 14.3 %third.1 = (bf16[16,1536,512]{2,1,0:T(8,128)(2,1)}, bf16[16,1536,512]{2,1,0:T(8,128)(2,1)}, bf16[16,512,1536]{2,1,0:T(8,128)(2,1)}, f32[512,1536]{1,0:T(8,128)S(1)}) custom-call(s32[2]{0:T(128)S(1)} %copy-done.2, s32[2]{0:T(128)S(1)} %copy-done.3, ...), custom_call_target="tpu_custom_call", output_to_operand_aliasing={{0}: (10, {}), {1}: (11, {}), {2}: (12, {})} | custom-call | flops 30000001024 | bytes 37748736 | tf_op jit(solution)/shard_map/third/pallas_call | solution.py:488
  71.7 0.0 collective-permute-done.4.rx3
  71.7 0.0 collective-permute-done.5.ry3
  71.7 18.2 %combine.1 = (bf16[64,1536]{1,0:T(8,128)(2,1)S(1)}, bf16[6,576,512]{2,1,0:T(8,128)(2,1)S(1)}, bf16[2304,512]{1,0:T(8,128)(2,1)S(1)}) custom-call(f32[8,64,1536]{2,1,0:T(8,128)S(1)} %bitcast.7, bf16[64,1536]{1,0:T(8,128)(2,1)S(1)} %copy-done, bf16[576,512]{1,0:T(8,128)(2,1)S(1)} %collective-permute-done.rx1, bf16[576,512]{1,0:T(8,128)(2,1)S(1)} %collective-permute-done.2.rx2, ...), custom_call_target="tpu_custom_call" | custom-call | flops 16000000000 | bytes 4000000 | tf_op jit(solution)/shard_map/combine/pallas_call | solution.py:498
  90.0 1.4 %patch.1 = (bf16[16,1536,512]{2,1,0:T(8,128)(2,1)}, bf16[16,1536,512]{2,1,0:T(8,128)(2,1)}, bf16[16,512,1536]{2,1,0:T(8,128)(2,1)}, bf16[64,1536]{1,0:T(8,128)(2,1)}) custom-call(s32[2]{0:T(128)S(1)} %copy-done.3, bf16[64,1536]{1,0:T(8,128)(2,1)S(1)} %get-tuple-element.135.y_ref, ...), custom_call_target="tpu_custom_call", output_to_operand_aliasing={{0}: (11, {}), {1}: (12, {}), {2}: (13, {})} | custom-call | flops 3000000000 | bytes 9437184 | tf_op jit(solution)/shard_map/patch/pallas_call | solution.py:509
Async XLA Ops:
  0.6 4.2 %copy-start = (bf16[64,1536]{1,0:T(8,128)(2,1)S(1)}, bf16[64,1536]{1,0:T(8,128)(2,1)}, u32[]{:S(2)}) copy-start(bf16[64,1536]{1,0:T(8,128)(2,1)} %x_ref.3) | copy-start | bytes 589828
  0.6 0.7 copy-start.1
  1.3 3.5 %copy-start.4 = (s32[64,8]{0,1:T(8,128)S(1)}, s32[64,8]{0,1:T(8,128)}, u32[]{:S(2)}) copy-start(s32[64,8]{0,1:T(8,128)} %param.10) | copy-start | bytes 6148
  1.3 3.5 %copy-start.5 = (f32[64,8]{0,1:T(8,128)S(1)}, f32[64,8]{0,1:T(8,128)}, u32[]{:S(2)}) copy-start(f32[64,8]{0,1:T(8,128)} %param.11) | copy-start | bytes 6148
  4.9 19.2 %copy-start.2 = (s32[2]{0:T(128)S(1)}, s32[2]{0:T(128)}, u32[]{:S(2)}) copy-start(s32[2]{0:T(128)} %src.7) | copy-start | bytes 28
  4.9 19.1 %copy-start.3 = (s32[2]{0:T(128)S(1)}, s32[2]{0:T(128)}, u32[]{:S(2)}) copy-start(s32[2]{0:T(128)} %dst.7) | copy-start | bytes 28
  4.9 19.1 %copy-start.6 = (s32[128]{0:T(128)S(1)}, s32[128]{0:T(128)}, u32[]{:S(2)}) copy-start(s32[128]{0:T(128)} %old_map.1) | copy-start | bytes 1540
  22.0 16.8 %collective-permute-start = (bf16[576,512]{1,0:T(8,128)(2,1)S(1)}, bf16[576,512]{1,0:T(8,128)(2,1)S(1)}, u32[]{:S(2)}, u32[]{:S(2)}) collective-permute-start(bf16[576,512]{1,0:T(8,128)(2,1)S(1)} %get-tuple-element.81), channel_id=1, source_target_pairs={{0,2},{1,3},{2,0},{3,1},{4,6},{5,7},{6,4},{7,5}} | collective-permute-start | bytes 1769480 | tf_op jit(solution)/shard_map/ppermute | solution.py:453
  23.4 15.3 %collective-permute-start.1 = (bf16[576,512]{1,0:T(8,128)(2,1)S(1)}, bf16[576,512]{1,0:T(8,128)(2,1)S(1)}, u32[]{:S(2)}, u32[]{:S(2)}) collective-permute-start(bf16[576,512]{1,0:T(8,128)(2,1)S(1)} %get-tuple-element.82), channel_id=1, source_target_pairs={{0,4},{1,5},{2,6},{3,7},{4,0},{5,1},{6,2},{7,3}} | collective-permute-start | bytes 1769480 | tf_op jit(solution)/shard_map/ppermute | solution.py:453
  38.9 16.3 %collective-permute-start.2 = (bf16[576,512]{1,0:T(8,128)(2,1)S(1)}, bf16[576,512]{1,0:T(8,128)(2,1)S(1)}, u32[]{:S(2)}, u32[]{:S(2)}) collective-permute-start(bf16[576,512]{1,0:T(8,128)(2,1)S(1)} %broadcast_select_fusion.3), channel_id=1, source_target_pairs={{0,2},{1,3},{2,0},{3,1},{4,6},{5,7},{6,4},{7,5}} | collective-permute-start | bytes 1769480 | tf_op jit(solution)/shard_map/ppermute | solution.py:453
  39.9 15.3 %collective-permute-start.3 = (bf16[576,512]{1,0:T(8,128)(2,1)S(1)}, bf16[576,512]{1,0:T(8,128)(2,1)S(1)}, u32[]{:S(2)}, u32[]{:S(2)}) collective-permute-start(bf16[576,512]{1,0:T(8,128)(2,1)S(1)} %broadcast_select_fusion.2), channel_id=1, source_target_pairs={{0,4},{1,5},{2,6},{3,7},{4,0},{5,1},{6,2},{7,3}} | collective-permute-start | bytes 1769480 | tf_op jit(solution)/shard_map/ppermute | solution.py:453
  55.4 16.3 %collective-permute-start.4 = (bf16[576,512]{1,0:T(8,128)(2,1)S(1)}, bf16[576,512]{1,0:T(8,128)(2,1)S(1)}, u32[]{:S(2)}, u32[]{:S(2)}) collective-permute-start(bf16[576,512]{1,0:T(8,128)(2,1)S(1)} %get-tuple-element.133), channel_id=1, source_target_pairs={{0,2},{1,3},{2,0},{3,1},{4,6},{5,7},{6,4},{7,5}} | collective-permute-start | bytes 1769480 | tf_op jit(solution)/shard_map/ppermute | solution.py:453
  56.9 14.9 %collective-permute-start.5 = (bf16[576,512]{1,0:T(8,128)(2,1)S(1)}, bf16[576,512]{1,0:T(8,128)(2,1)S(1)}, u32[]{:S(2)}, u32[]{:S(2)}) collective-permute-start(bf16[576,512]{1,0:T(8,128)(2,1)S(1)} %get-tuple-element.134), channel_id=1, source_target_pairs={{0,4},{1,5},{2,6},{3,7},{4,0},{5,1},{6,2},{7,3}} | collective-permute-start | bytes 1769480 | tf_op jit(solution)/shard_map/ppermute | solution.py:453

commit v6 on v5

--- a/solution.py
+++ b/solution.py
@@ -85,42 +85,69 @@
         copy.start()
     enter(peers + [sib])
 
-    alls = (xall, iall, gall)
-
-    def group(k, refs, block, dev):
-        return [remote(ref, to.at[block], send.at[3 * k + n], recv.at[3 * k + n], dev)
-                for n, (ref, to) in enumerate(zip(refs, alls))]
-
-    mine = (x_ref, ids_ref, gate_ref)
-    first = [group(k, mine, me, dev) for k, dev in enumerate(peers + [sib])]
-    for copies in first:
+    (dev_d, dev_x, dev_y), half = peers, x_ref.shape[0] // 2
+    low, high = pl.ds(0, half), pl.ds(half, half)
+
+    def rows(k, block, part, dev, ref=None):
+        to = xall.at[block, part]
+        return remote(to if ref is None else ref.at[part], to, send.at[k], recv.at[k], dev)
+
+    def table(k, block, dev, refs):
+        return [remote(ref, to.at[block], send.at[k + n], recv.at[k + n], dev) for n, (ref, to) in enumerate(zip(refs, (iall, gall)))]
+
+    own_rows = {key: rows(k, me, part, dev, x_ref) for k, (key, part, dev) in enumerate((
+        ('xh', high, dev_x), ('yl', low, dev_y), ('xl', low, dev_x), ('yh', high, dev_y), ('sl', low, sib), ('sh', high, sib)))}
+    own_tables = [table(6 + 2 * k, me, dev, (ids_ref, gate_ref)) for k, dev in enumerate(peers + [sib])]
+    slot = remote(slot_ref, near, send.at[14], recv.at[14], sib)
+    for key in ('xh', 'yl'):
+        own_rows[key].start()
+    for copies in own_tables:
         for copy in copies:
             copy.start()
-    slot = remote(slot_ref, near, send.at[21], recv.at[21], sib)
+    for key in ('xl', 'yh', 'sl', 'sh'):
+        own_rows[key].start()
     slot.start()
+    mine, alls = (x_ref, ids_ref, gate_ref), (xall, iall, gall)
     for ref, to in zip(mine, alls):
         to[pl.ds(me, 1)] = ref[...][None]
+    sent = []
+
+    def forward(*copies):
+        for copy in copies:
+            copy.start()
+            sent.append(copy)
+
+    own_rows['xh'].wait_recv()
+    forward(rows(15, dev_x, high, dev_y), rows(17, dev_x, high, sib))
+    own_rows['yl'].wait_recv()
+    forward(rows(16, dev_y, low, dev_x), rows(18, dev_y, low, sib))
     slot.wait_recv()
     part = h0.shape[0]
     for k, held in enumerate((h0, h1, h2, h3)):
-        rows = pl.ds(k * part, part)
-        held[...] = jnp.where(mine_ref[0] > 0, own[rows, :], near[rows, :])
-    second = []
-    for k in (1, 2, 0):
-        for copy in first[k]:
+        span = pl.ds(k * part, part)
+        held[...] = jnp.where(mine_ref[0] > 0, own[span, :], near[span, :])
+    for k, dev in enumerate(peers):
+        for copy in own_tables[k]:
             copy.wait_recv()
-        fwd = group(4 + k, [to.at[peers[k]] for to in alls], peers[k], sib)
-        for copy in fwd:
-            copy.start()
-        second.append(fwd)
-    for copy in first[3]:
+        forward(*table(23 + 2 * k, dev, sib, (iall.at[dev], gall.at[dev])))
+    own_rows['xl'].wait_recv()
+    forward(rows(19, dev_x, low, sib))
+    own_rows['yh'].wait_recv()
+    forward(rows(20, dev_y, high, sib))
+    sent[0].wait_recv()
+    forward(rows(21, dev_d, high, sib))
+    sent[2].wait_recv()
+    forward(rows(22, dev_d, low, sib))
+    for copy in own_tables[3]:
         copy.wait_recv()
-    for copies in first:
-        for copy in copies:
-            copy.wait_send()
-    for copies in second:
-        for copy in copies:
-            copy.wait()
+    for key in ('sl', 'sh'):
+        own_rows[key].wait_recv()
+    for k, copy in enumerate(sent):
+        if k not in (0, 2):
+            copy.wait_recv()
+        copy.wait_send()
+    for copy in list(own_rows.values()) + [copy for copies in own_tables for copy in copies]:
+        copy.wait_send()
     slot.wait_send()
     for copy in reads:
         copy.wait()
@@ -441,7 +468,7 @@
                        jax.ShapeDtypeStruct((groups, top, tok), F32), bf(half, width))
             + (bf(part, width),) * 4 + tuple(bf(HELD, *w.shape[1:]) for w in weights for _ in range(EARLY // HELD)),
             in_specs=[SMEM, VMEM, VMEM, VMEM, ANY, VMEM, HBM, HBM, HBM], out_specs=(VMEM,) * (8 + 3 * (EARLY // HELD)),
-            scratch_shapes=[dma((22,)), dma((22,)), dma((3 * (EARLY // HELD),))],
+            scratch_shapes=[dma((29,)), dma((29,)), dma((3 * (EARLY // HELD),))],
             compiler_params=params(4, collective_id=0, has_side_effects=True),
             cost_estimate=cost(8_000_000_000, 2_000_000), name='dispatch',
         )(i_own, x_loc, expert_ids.T, gate_val.T, send, own, *weights)

time: 92.3 us -> 88.7 us (0.961)
  Pallas kernels: 82.9 us -> 79.9 us
    pallas_call x1, Pallas kernels: 17.1 us -> 15 us  [local_step(): pl.pallas_call(dispatch_kernel, out_shape=(bf(groups, tok, model), jax.Sh...]
    ppermute x3, starting transfers between devices: 2.19 us -> 3.7 us  [hop(): lax.ppermute(to_y_rows, 'ep', to_y)]
    ppermute x3, starting transfers between devices: 3.95 us -> 2.56 us  [hop(): lax.ppermute(to_x_rows, 'ep', to_x)]
  transfers between devices with their start and end apart: 6 -> 6, of which waited for: 0 -> 0; matrix products, arithmetic and copies ran while one was open for 0% -> 0% of each run, Pallas kernels for 47% -> 48%
where the time goes in v6:
time: 88.7 us; the launch traced here: 88.5 us
  Pallas kernels  79.9 us (90%)
  starting transfers between devices  6.26 us (7%)
  between operations  1.38 us (2%)
    pallas_call x1, Pallas kernels, local_step(): pl.pallas_call(combine_kernel, out_shape=(bf(tok, model), bf(6, part, wid...  17.3 us
    pallas_call x1, Pallas kernels, local_step(): pl.pallas_call(dispatch_kernel, out_shape=(bf(groups, tok, model), jax.Sh...  15 us
    pallas_call x1, Pallas kernels, local_step(): pl.pallas_call(third_kernel, out_shape=shapes + (jax.ShapeDtypeStruct((to...  14.3 us
    pallas_call x1, Pallas kernels, local_step(): pl.pallas_call(second_kernel, out_shape=shapes + (bf(SECOND * per, model)...  14.2 us
    pallas_call x1, Pallas kernels, local_step(): pl.pallas_call(first_kernel, out_shape=shapes + (bf(late, model), bf(tota...  14.2 us
    ppermute x3, starting transfers between devices, hop(): lax.ppermute(to_y_rows, 'ep', to_y)  3.7 us
    pallas_call x1, Pallas kernels, local_step(): pl.pallas_call(pack_kernel, out_shape=(jax.ShapeDtypeStruct((1,), jnp.int...  3.48 us
    ppermute x3, starting transfers between devices, hop(): lax.ppermute(to_x_rows, 'ep', to_x)  2.56 us
  transfers between devices with their start and end apart: 6, of which 0 were waited for; matrix products, arithmetic and copies ran while one was open for 0% of the time, Pallas kernels for 48%

profile of v6, /device:TPU:0, one launch (start us, length us, event | category | flops | bytes accessed | tf_op | source)
XLA Modules:
  0.0 88.5 jit_solution(10717591962368184917)
XLA Ops:
  0.6 0.0 copy-start
  0.6 0.0 copy-start.1
  0.7 0.7 copy-done.1
  1.3 0.0 copy-start.4
  1.3 0.0 copy-start.5
  1.3 3.5 %pack.1 = (s32[1]{0:T(128)}, s32[1]{0:T(128)}, bf16[2304,512]{1,0:T(8,128)(2,1)S(1)}, bf16[2304,512]{1,0:T(8,128)(2,1)S(1)}) custom-call(s32[2]{0:T(128)S(1)} %copy-done.1, bf16[16,1536,512]{2,1,0:T(8,128)(2,1)} %wg.7, bf16[16,1536,512]{2,1,0:T(8,128)(2,1)} %wu.7, bf16[16,512,1536]{2,1,0:T(8,128)(2,1)} %wd.7), custom_call_target="tpu_custom_call" | custom-call | flops 2000000000 | bytes 9437184 | tf_op jit(solution)/shard_map/pack/pallas_call | solution.py:456
  4.8 0.0 copy-done
  4.8 0.0 copy-done.4
  4.9 0.0 copy-done.5
  4.9 0.0 copy-start.2
  4.9 0.0 copy-start.3
  4.9 0.0 copy-start.6
  4.9 15.0 %dispatch.1 = (bf16[8,64,1536]{2,1,0:T(8,128)(2,1)S(1)}, s32[8,8,64]{2,1,0:T(8,128)S(1)}, f32[8,8,64]{2,1,0:T(8,128)S(1)}, bf16[2304,512]{1,0:T(8,128)(2,1)S(1)}...) custom-call(s32[1]{0:T(128)} %get-tuple-element.76.mine_ref, ...), custom_call_target="tpu_custom_call" | custom-call | flops 8000000000 | bytes 2000000 | tf_op jit(solution)/shard_map/dispatch/pallas_call | solution.py:465
  19.9 0.9 collective-permute-start
  20.8 1.3 %collective-permute-start.1 = (bf16[576,512]{1,0:T(8,128)(2,1)S(1)}, bf16[576,512]{1,0:T(8,128)(2,1)S(1)}, u32[]{:S(2)}, u32[]{:S(2)}) collective-permute-start(bf16[576,512]{1,0:T(8,128)(2,1)S(1)} %get-tuple-element.82), channel_id=1, source_target_pairs={{0,4},{1,5},{2,6},{3,7},{4,0},{5,1},{6,2},{7,3}} | collective-permute-start | bytes 1769480 | tf_op jit(solution)/shard_map/ppermute | solution.py:480
  22.1 0.0 copy-done.2
  22.1 0.0 copy-done.3
  22.1 0.0 copy-done.6
  22.1 14.2 %first.1 = (bf16[16,1536,512]{2,1,0:T(8,128)(2,1)}, bf16[16,1536,512]{2,1,0:T(8,128)(2,1)}, bf16[16,512,1536]{2,1,0:T(8,128)(2,1)}, bf16[512,1536]{1,0:T(8,128)(...) custom-call(s32[2]{0:T(128)S(1)} %copy-done.2, s32[2]{0:T(128)S(1)} %copy-done.3, ...), custom_call_target="tpu_custom_call" | custom-call | flops 30000001024 | bytes 42467328 | tf_op jit(solution)/shard_map/first/pallas_call | solution.py:493
  36.8 0.0 collective-permute-done.rx1
  36.8 0.0 collective-permute-done.1.ry1
  36.8 0.1 broadcast_select_fusion.3
  36.9 0.1 broadcast_select_fusion.2
  37.0 0.9 collective-permute-start.2
  37.8 1.1 %collective-permute-start.3 = (bf16[576,512]{1,0:T(8,128)(2,1)S(1)}, bf16[576,512]{1,0:T(8,128)(2,1)S(1)}, u32[]{:S(2)}, u32[]{:S(2)}) collective-permute-start(bf16[576,512]{1,0:T(8,128)(2,1)S(1)} %broadcast_select_fusion.2), channel_id=1, source_target_pairs={{0,4},{1,5},{2,6},{3,7},{4,0},{5,1},{6,2},{7,3}} | collective-permute-start | bytes 1769480 | tf_op jit(solution)/shard_map/ppermute | solution.py:480
  38.9 14.2 %second.1 = (bf16[16,1536,512]{2,1,0:T(8,128)(2,1)}, bf16[16,1536,512]{2,1,0:T(8,128)(2,1)}, bf16[16,512,1536]{2,1,0:T(8,128)(2,1)}, bf16[256,1536]{1,0:T(8,128)(2,1)S(1)}) custom-call(s32[2]{0:T(128)S(1)} %copy-done.2, s32[2]{0:T(128)S(1)} %copy-done.3, ...), custom_call_target="tpu_custom_call", output_to_operand_aliasing={{0}: (7, {}), {1}: (8, {}), {2}: (9, {})} | custom-call | flops 30000001024 | bytes 37748736 | tf_op jit(solution)/shard_map/second/pallas_call | solution.py:505
  53.2 0.0 collective-permute-done.2.rx2
  53.2 0.0 collective-permute-done.3.ry2
  53.2 0.1 broadcast_select_fusion
  53.3 0.9 collective-permute-start.4
  54.2 1.3 %collective-permute-start.5 = (bf16[576,512]{1,0:T(8,128)(2,1)S(1)}, bf16[576,512]{1,0:T(8,128)(2,1)S(1)}, u32[]{:S(2)}, u32[]{:S(2)}) collective-permute-start(bf16[576,512]{1,0:T(8,128)(2,1)S(1)} %get-tuple-element.134), channel_id=1, source_target_pairs={{0,4},{1,5},{2,6},{3,7},{4,0},{5,1},{6,2},{7,3}} | collective-permute-start | bytes 1769480 | tf_op jit(solution)/shard_map/ppermute | solution.py:480
  55.5 14.3 %third.1 = (bf16[16,1536,512]{2,1,0:T(8,128)(2,1)}, bf16[16,1536,512]{2,1,0:T(8,128)(2,1)}, bf16[16,512,1536]{2,1,0:T(8,128)(2,1)}, f32[512,1536]{1,0:T(8,128)S(1)}) custom-call(s32[2]{0:T(128)S(1)} %copy-done.2, s32[2]{0:T(128)S(1)} %copy-done.3, ...), custom_call_target="tpu_custom_call", output_to_operand_aliasing={{0}: (10, {}), {1}: (11, {}), {2}: (12, {})} | custom-call | flops 30000001024 | bytes 37748736 | tf_op jit(solution)/shard_map/third/pallas_call | solution.py:515
  69.8 0.0 collective-permute-done.4.rx3
  69.8 0.0 collective-permute-done.5.ry3
  69.8 17.3 %combine.1 = (bf16[64,1536]{1,0:T(8,128)(2,1)S(1)}, bf16[6,576,512]{2,1,0:T(8,128)(2,1)S(1)}, bf16[2304,512]{1,0:T(8,128)(2,1)S(1)}) custom-call(f32[8,64,1536]{2,1,0:T(8,128)S(1)} %bitcast.7, bf16[64,1536]{1,0:T(8,128)(2,1)S(1)} %copy-done, bf16[576,512]{1,0:T(8,128)(2,1)S(1)} %collective-permute-done.rx1, bf16[576,512]{1,0:T(8,128)(2,1)S(1)} %collective-permute-done.2.rx2, ...), custom_call_target="tpu_custom_call" | custom-call | flops 16000000000 | bytes 4000000 | tf_op jit(solution)/shard_map/combine/pallas_call | solution.py:525
  87.1 1.4 %patch.1 = (bf16[16,1536,512]{2,1,0:T(8,128)(2,1)}, bf16[16,1536,512]{2,1,0:T(8,128)(2,1)}, bf16[16,512,1536]{2,1,0:T(8,128)(2,1)}, bf16[64,1536]{1,0:T(8,128)(2,1)}) custom-call(s32[2]{0:T(128)S(1)} %copy-done.3, bf16[64,1536]{1,0:T(8,128)(2,1)S(1)} %get-tuple-element.135.y_ref, ...), custom_call_target="tpu_custom_call", output_to_operand_aliasing={{0}: (11, {}), {1}: (12, {}), {2}: (13, {})} | custom-call | flops 3000000000 | bytes 9437184 | tf_op jit(solution)/shard_map/patch/pallas_call | solution.py:536
Async XLA Ops:
  0.6 4.2 %copy-start = (bf16[64,1536]{1,0:T(8,128)(2,1)S(1)}, bf16[64,1536]{1,0:T(8,128)(2,1)}, u32[]{:S(2)}) copy-start(bf16[64,1536]{1,0:T(8,128)(2,1)} %x_ref.3) | copy-start | bytes 589828
  0.6 0.7 copy-start.1
  1.3 3.5 %copy-start.4 = (s32[64,8]{0,1:T(8,128)S(1)}, s32[64,8]{0,1:T(8,128)}, u32[]{:S(2)}) copy-start(s32[64,8]{0,1:T(8,128)} %param.10) | copy-start | bytes 6148
  1.3 3.5 %copy-start.5 = (f32[64,8]{0,1:T(8,128)S(1)}, f32[64,8]{0,1:T(8,128)}, u32[]{:S(2)}) copy-start(f32[64,8]{0,1:T(8,128)} %param.11) | copy-start | bytes 6148
  4.9 17.2 %copy-start.2 = (s32[2]{0:T(128)S(1)}, s32[2]{0:T(128)}, u32[]{:S(2)}) copy-start(s32[2]{0:T(128)} %src.7) | copy-start | bytes 28
  4.9 17.2 %copy-start.3 = (s32[2]{0:T(128)S(1)}, s32[2]{0:T(128)}, u32[]{:S(2)}) copy-start(s32[2]{0:T(128)} %dst.7) | copy-start | bytes 28
  4.9 17.2 %copy-start.6 = (s32[128]{0:T(128)S(1)}, s32[128]{0:T(128)}, u32[]{:S(2)}) copy-start(s32[128]{0:T(128)} %old_map.1) | copy-start | bytes 1540
  19.9 16.9 %collective-permute-start = (bf16[576,512]{1,0:T(8,128)(2,1)S(1)}, bf16[576,512]{1,0:T(8,128)(2,1)S(1)}, u32[]{:S(2)}, u32[]{:S(2)}) collective-permute-start(bf16[576,512]{1,0:T(8,128)(2,1)S(1)} %get-tuple-element.81), channel_id=1, source_target_pairs={{0,2},{1,3},{2,0},{3,1},{4,6},{5,7},{6,4},{7,5}} | collective-permute-start | bytes 1769480 | tf_op jit(solution)/shard_map/ppermute | solution.py:480
  20.8 16.1 %collective-permute-start.1 = (bf16[576,512]{1,0:T(8,128)(2,1)S(1)}, bf16[576,512]{1,0:T(8,128)(2,1)S(1)}, u32[]{:S(2)}, u32[]{:S(2)}) collective-permute-start(bf16[576,512]{1,0:T(8,128)(2,1)S(1)} %get-tuple-element.82), channel_id=1, source_target_pairs={{0,4},{1,5},{2,6},{3,7},{4,0},{5,1},{6,2},{7,3}} | collective-permute-start | bytes 1769480 | tf_op jit(solution)/shard_map/ppermute | solution.py:480
  37.0 16.2 %collective-permute-start.2 = (bf16[576,512]{1,0:T(8,128)(2,1)S(1)}, bf16[576,512]{1,0:T(8,128)(2,1)S(1)}, u32[]{:S(2)}, u32[]{:S(2)}) collective-permute-start(bf16[576,512]{1,0:T(8,128)(2,1)S(1)} %broadcast_select_fusion.3), channel_id=1, source_target_pairs={{0,2},{1,3},{2,0},{3,1},{4,6},{5,7},{6,4},{7,5}} | collective-permute-start | bytes 1769480 | tf_op jit(solution)/shard_map/ppermute | solution.py:480
  37.8 15.3 %collective-permute-start.3 = (bf16[576,512]{1,0:T(8,128)(2,1)S(1)}, bf16[576,512]{1,0:T(8,128)(2,1)S(1)}, u32[]{:S(2)}, u32[]{:S(2)}) collective-permute-start(bf16[576,512]{1,0:T(8,128)(2,1)S(1)} %broadcast_select_fusion.2), channel_id=1, source_target_pairs={{0,4},{1,5},{2,6},{3,7},{4,0},{5,1},{6,2},{7,3}} | collective-permute-start | bytes 1769480 | tf_op jit(solution)/shard_map/ppermute | solution.py:480
  53.3 16.5 %collective-permute-start.4 = (bf16[576,512]{1,0:T(8,128)(2,1)S(1)}, bf16[576,512]{1,0:T(8,128)(2,1)S(1)}, u32[]{:S(2)}, u32[]{:S(2)}) collective-permute-start(bf16[576,512]{1,0:T(8,128)(2,1)S(1)} %get-tuple-element.133), channel_id=1, source_target_pairs={{0,2},{1,3},{2,0},{3,1},{4,6},{5,7},{6,4},{7,5}} | collective-permute-start | bytes 1769480 | tf_op jit(solution)/shard_map/ppermute | solution.py:480
  54.2 15.6 %collective-permute-start.5 = (bf16[576,512]{1,0:T(8,128)(2,1)S(1)}, bf16[576,512]{1,0:T(8,128)(2,1)S(1)}, u32[]{:S(2)}, u32[]{:S(2)}) collective-permute-start(bf16[576,512]{1,0:T(8,128)(2,1)S(1)} %get-tuple-element.134), channel_id=1, source_target_pairs={{0,4},{1,5},{2,6},{3,7},{4,0},{5,1},{6,2},{7,3}} | collective-permute-start | bytes 1769480 | tf_op jit(solution)/shard_map/ppermute | solution.py:480

commit v7 on v6

--- a/solution.py
+++ b/solution.py
@@ -330,29 +330,30 @@
     dev_x, dev_y = chips[1] * 2 + core, chips[2] * 2 + core
     order = list(chips) + [chip]
     enter([dev_x, dev_y, sib])
-    across = [remote(part.at[c * 2 + 1 - core], near.at[k], send.at[k], recv.at[k], sib) for k, c in enumerate(order)]
+    half = x_ref.shape[1] // 2
+    cols = (pl.ds(0, half), pl.ds(half, half))
+    early = [remote(part.at[order[0] * 2 + 1 - core, :, at], near.at[0, :, at], send.at[k], recv.at[k], sib)
+             for k, at in zip((0, 17), cols)]
+    across = early + [remote(part.at[order[k] * 2 + 1 - core], near.at[k], send.at[k], recv.at[k], sib) for k in range(1, 4)]
     for copy in across:
         copy.start()
     moved = [remote(r, got.at[k], send.at[10 + k], recv.at[10 + k], sib) for k, r in enumerate((rx1, rx2, rx3, ry1, ry2, ry3))]
     moved.append(remote(own, gown, send.at[16], recv.at[16], sib))
     for copy in moved:
         copy.start()
-    half = x_ref.shape[1] // 2
-    cols = (pl.ds(0, half), pl.ds(half, half))
     towards = (dev_x, dev_y)
     diag = [remote(summed.at[0, :, cols[h]], far.at[0, :, cols[h]], send.at[4 + h], recv.at[4 + h], towards[h]) for h in range(2)]
     next_ = [remote(summed.at[1 + h, :, cols[h]], far.at[1, :, cols[h]], send.at[6 + h], recv.at[6 + h], towards[h]) for h in range(2)]
     onward = [remote(relay.at[h], last.at[h], send.at[8 + h], recv.at[8 + h], towards[1 - h]) for h in range(2)]
-    for k in range(4):
-        across[k].wait_recv()
+    for h in range(2):
+        early[h].wait_recv()
+        summed[0, :, cols[h]] = part[order[0] * 2 + core, :, cols[h]] + near[0, :, cols[h]]
+        diag[h].start()
+    for k in range(1, 4):
+        across[k + 1].wait_recv()
         summed[k] = part[order[k] * 2 + core] + near[k]
-        if k == 1:
-            for copy in diag:
-                copy.start()
-        elif k == 2:
-            next_[0].start()
-        elif k == 3:
-            next_[1].start()
+        if k < 3:
+            next_[k - 1].start()
     acc = x_ref[...].astype(F32) + summed[3]
     for h in range(2):
         diag[h].wait_recv()
@@ -528,7 +529,7 @@
             in_specs=[VMEM, VMEM] + [ANY] * 7, out_specs=(VMEM, ANY, ANY),
             scratch_shapes=[pltpu.VMEM((4, tok, model), F32), pltpu.VMEM((4, tok, model), F32),
                             pltpu.VMEM((2, tok, model), F32), pltpu.VMEM((2, tok, model // 2), F32),
-                            pltpu.VMEM((2, tok, model // 2), F32), dma((17,)), dma((17,))],
+                            pltpu.VMEM((2, tok, model // 2), F32), dma((18,)), dma((18,))],
             compiler_params=params(24, collective_id=1, has_side_effects=True),
             cost_estimate=cost(16_000_000_000, 4_000_000), name='combine',
         )(psum.reshape(groups, tok, model), x_loc, *came, own)

time: 88.7 us -> 87.8 us (0.990)
  Pallas kernels: 79.9 us -> 79 us
  transfers between devices with their start and end apart: 6 -> 6, of which waited for: 0 -> 0; matrix products, arithmetic and copies ran while one was open for 0% -> 0% of each run, Pallas kernels for 48% -> 49%
where the time goes in v7:
time: 87.8 us; the launch traced here: 87.7 us
  Pallas kernels  79 us (90%)
  starting transfers between devices  6.26 us (7%)
  between operations  1.38 us (2%)
    pallas_call x1, Pallas kernels, local_step(): pl.pallas_call(combine_kernel, out_shape=(bf(tok, model), bf(6, part, wid...  16.5 us
    pallas_call x1, Pallas kernels, local_step(): pl.pallas_call(dispatch_kernel, out_shape=(bf(groups, tok, model), jax.Sh...  15 us
    pallas_call x1, Pallas kernels, local_step(): pl.pallas_call(third_kernel, out_shape=shapes + (jax.ShapeDtypeStruct((to...  14.3 us
    pallas_call x1, Pallas kernels, local_step(): pl.pallas_call(second_kernel, out_shape=shapes + (bf(SECOND * per, model)...  14.2 us
    pallas_call x1, Pallas kernels, local_step(): pl.pallas_call(first_kernel, out_shape=shapes + (bf(late, model), bf(tota...  14.2 us
    ppermute x3, starting transfers between devices, hop(): lax.ppermute(to_y_rows, 'ep', to_y)  3.7 us
    pallas_call x1, Pallas kernels, local_step(): pl.pallas_call(pack_kernel, out_shape=(jax.ShapeDtypeStruct((1,), jnp.int...  3.48 us
    ppermute x3, starting transfers between devices, hop(): lax.ppermute(to_x_rows, 'ep', to_x)  2.56 us
  transfers between devices with their start and end apart: 6, of which 0 were waited for; matrix products, arithmetic and copies ran while one was open for 0% of the time, Pallas kernels for 49%

profile of v7, /device:TPU:0, one launch (start us, length us, event | category | flops | bytes accessed | tf_op | source)
XLA Modules:
  0.0 87.7 jit_solution(4901827558324323153)
XLA Ops:
  0.6 0.0 copy-start
  0.6 0.0 copy-start.1
  0.7 0.7 copy-done.1
  1.3 0.0 copy-start.4
  1.3 0.0 copy-start.5
  1.3 3.5 %pack.1 = (s32[1]{0:T(128)}, s32[1]{0:T(128)}, bf16[2304,512]{1,0:T(8,128)(2,1)S(1)}, bf16[2304,512]{1,0:T(8,128)(2,1)S(1)}) custom-call(s32[2]{0:T(128)S(1)} %copy-done.1, bf16[16,1536,512]{2,1,0:T(8,128)(2,1)} %wg.7, bf16[16,1536,512]{2,1,0:T(8,128)(2,1)} %wu.7, bf16[16,512,1536]{2,1,0:T(8,128)(2,1)} %wd.7), custom_call_target="tpu_custom_call" | custom-call | flops 2000000000 | bytes 9437184 | tf_op jit(solution)/shard_map/pack/pallas_call | solution.py:457
  4.8 0.0 copy-done
  4.8 0.0 copy-done.4
  4.9 0.0 copy-done.5
  4.9 0.0 copy-start.2
  4.9 0.0 copy-start.3
  4.9 0.0 copy-start.6
  4.9 15.0 %dispatch.1 = (bf16[8,64,1536]{2,1,0:T(8,128)(2,1)S(1)}, s32[8,8,64]{2,1,0:T(8,128)S(1)}, f32[8,8,64]{2,1,0:T(8,128)S(1)}, bf16[2304,512]{1,0:T(8,128)(2,1)S(1)}...) custom-call(s32[1]{0:T(128)} %get-tuple-element.76.mine_ref, ...), custom_call_target="tpu_custom_call" | custom-call | flops 8000000000 | bytes 2000000 | tf_op jit(solution)/shard_map/dispatch/pallas_call | solution.py:466
  19.9 0.9 collective-permute-start
  20.8 1.3 %collective-permute-start.1 = (bf16[576,512]{1,0:T(8,128)(2,1)S(1)}, bf16[576,512]{1,0:T(8,128)(2,1)S(1)}, u32[]{:S(2)}, u32[]{:S(2)}) collective-permute-start(bf16[576,512]{1,0:T(8,128)(2,1)S(1)} %get-tuple-element.82), channel_id=1, source_target_pairs={{0,4},{1,5},{2,6},{3,7},{4,0},{5,1},{6,2},{7,3}} | collective-permute-start | bytes 1769480 | tf_op jit(solution)/shard_map/ppermute | solution.py:481
  22.1 0.0 copy-done.2
  22.1 0.0 copy-done.3
  22.1 0.0 copy-done.6
  22.1 14.2 %first.1 = (bf16[16,1536,512]{2,1,0:T(8,128)(2,1)}, bf16[16,1536,512]{2,1,0:T(8,128)(2,1)}, bf16[16,512,1536]{2,1,0:T(8,128)(2,1)}, bf16[512,1536]{1,0:T(8,128)(...) custom-call(s32[2]{0:T(128)S(1)} %copy-done.2, s32[2]{0:T(128)S(1)} %copy-done.3, ...), custom_call_target="tpu_custom_call" | custom-call | flops 30000001024 | bytes 42467328 | tf_op jit(solution)/shard_map/first/pallas_call | solution.py:494
  36.8 0.0 collective-permute-done.rx1
  36.8 0.0 collective-permute-done.1.ry1
  36.8 0.1 broadcast_select_fusion.3
  36.9 0.1 broadcast_select_fusion.2
  37.0 0.9 collective-permute-start.2
  37.8 1.1 %collective-permute-start.3 = (bf16[576,512]{1,0:T(8,128)(2,1)S(1)}, bf16[576,512]{1,0:T(8,128)(2,1)S(1)}, u32[]{:S(2)}, u32[]{:S(2)}) collective-permute-start(bf16[576,512]{1,0:T(8,128)(2,1)S(1)} %broadcast_select_fusion.2), channel_id=1, source_target_pairs={{0,4},{1,5},{2,6},{3,7},{4,0},{5,1},{6,2},{7,3}} | collective-permute-start | bytes 1769480 | tf_op jit(solution)/shard_map/ppermute | solution.py:481
  38.9 14.2 %second.1 = (bf16[16,1536,512]{2,1,0:T(8,128)(2,1)}, bf16[16,1536,512]{2,1,0:T(8,128)(2,1)}, bf16[16,512,1536]{2,1,0:T(8,128)(2,1)}, bf16[256,1536]{1,0:T(8,128)(2,1)S(1)}) custom-call(s32[2]{0:T(128)S(1)} %copy-done.2, s32[2]{0:T(128)S(1)} %copy-done.3, ...), custom_call_target="tpu_custom_call", output_to_operand_aliasing={{0}: (7, {}), {1}: (8, {}), {2}: (9, {})} | custom-call | flops 30000001024 | bytes 37748736 | tf_op jit(solution)/shard_map/second/pallas_call | solution.py:506
  53.2 0.0 collective-permute-done.2.rx2
  53.2 0.0 collective-permute-done.3.ry2
  53.2 0.1 broadcast_select_fusion
  53.3 0.9 collective-permute-start.4
  54.2 1.3 %collective-permute-start.5 = (bf16[576,512]{1,0:T(8,128)(2,1)S(1)}, bf16[576,512]{1,0:T(8,128)(2,1)S(1)}, u32[]{:S(2)}, u32[]{:S(2)}) collective-permute-start(bf16[576,512]{1,0:T(8,128)(2,1)S(1)} %get-tuple-element.134), channel_id=1, source_target_pairs={{0,4},{1,5},{2,6},{3,7},{4,0},{5,1},{6,2},{7,3}} | collective-permute-start | bytes 1769480 | tf_op jit(solution)/shard_map/ppermute | solution.py:481
  55.5 14.3 %third.1 = (bf16[16,1536,512]{2,1,0:T(8,128)(2,1)}, bf16[16,1536,512]{2,1,0:T(8,128)(2,1)}, bf16[16,512,1536]{2,1,0:T(8,128)(2,1)}, f32[512,1536]{1,0:T(8,128)S(1)}) custom-call(s32[2]{0:T(128)S(1)} %copy-done.2, s32[2]{0:T(128)S(1)} %copy-done.3, ...), custom_call_target="tpu_custom_call", output_to_operand_aliasing={{0}: (10, {}), {1}: (11, {}), {2}: (12, {})} | custom-call | flops 30000001024 | bytes 37748736 | tf_op jit(solution)/shard_map/third/pallas_call | solution.py:516
  69.8 0.0 collective-permute-done.4.rx3
  69.8 0.0 collective-permute-done.5.ry3
  69.8 16.5 %combine.1 = (bf16[64,1536]{1,0:T(8,128)(2,1)S(1)}, bf16[6,576,512]{2,1,0:T(8,128)(2,1)S(1)}, bf16[2304,512]{1,0:T(8,128)(2,1)S(1)}) custom-call(f32[8,64,1536]{2,1,0:T(8,128)S(1)} %bitcast.7, bf16[64,1536]{1,0:T(8,128)(2,1)S(1)} %copy-done, bf16[576,512]{1,0:T(8,128)(2,1)S(1)} %collective-permute-done.rx1, bf16[576,512]{1,0:T(8,128)(2,1)S(1)} %collective-permute-done.2.rx2, ...), custom_call_target="tpu_custom_call" | custom-call | flops 16000000000 | bytes 4000000 | tf_op jit(solution)/shard_map/combine/pallas_call | solution.py:526
  86.3 1.4 %patch.1 = (bf16[16,1536,512]{2,1,0:T(8,128)(2,1)}, bf16[16,1536,512]{2,1,0:T(8,128)(2,1)}, bf16[16,512,1536]{2,1,0:T(8,128)(2,1)}, bf16[64,1536]{1,0:T(8,128)(2,1)}) custom-call(s32[2]{0:T(128)S(1)} %copy-done.3, bf16[64,1536]{1,0:T(8,128)(2,1)S(1)} %get-tuple-element.135.y_ref, ...), custom_call_target="tpu_custom_call", output_to_operand_aliasing={{0}: (11, {}), {1}: (12, {}), {2}: (13, {})} | custom-call | flops 3000000000 | bytes 9437184 | tf_op jit(solution)/shard_map/patch/pallas_call | solution.py:537
Async XLA Ops:
  0.6 4.2 %copy-start = (bf16[64,1536]{1,0:T(8,128)(2,1)S(1)}, bf16[64,1536]{1,0:T(8,128)(2,1)}, u32[]{:S(2)}) copy-start(bf16[64,1536]{1,0:T(8,128)(2,1)} %x_ref.3) | copy-start | bytes 589828
  0.6 0.7 copy-start.1
  1.3 3.5 %copy-start.4 = (s32[64,8]{0,1:T(8,128)S(1)}, s32[64,8]{0,1:T(8,128)}, u32[]{:S(2)}) copy-start(s32[64,8]{0,1:T(8,128)} %param.10) | copy-start | bytes 6148
  1.3 3.5 %copy-start.5 = (f32[64,8]{0,1:T(8,128)S(1)}, f32[64,8]{0,1:T(8,128)}, u32[]{:S(2)}) copy-start(f32[64,8]{0,1:T(8,128)} %param.11) | copy-start | bytes 6148
  4.9 17.2 %copy-start.2 = (s32[2]{0:T(128)S(1)}, s32[2]{0:T(128)}, u32[]{:S(2)}) copy-start(s32[2]{0:T(128)} %src.7) | copy-start | bytes 28
  4.9 17.2 %copy-start.3 = (s32[2]{0:T(128)S(1)}, s32[2]{0:T(128)}, u32[]{:S(2)}) copy-start(s32[2]{0:T(128)} %dst.7) | copy-start | bytes 28
  4.9 17.2 %copy-start.6 = (s32[128]{0:T(128)S(1)}, s32[128]{0:T(128)}, u32[]{:S(2)}) copy-start(s32[128]{0:T(128)} %old_map.1) | copy-start | bytes 1540
  19.9 16.9 %collective-permute-start = (bf16[576,512]{1,0:T(8,128)(2,1)S(1)}, bf16[576,512]{1,0:T(8,128)(2,1)S(1)}, u32[]{:S(2)}, u32[]{:S(2)}) collective-permute-start(bf16[576,512]{1,0:T(8,128)(2,1)S(1)} %get-tuple-element.81), channel_id=1, source_target_pairs={{0,2},{1,3},{2,0},{3,1},{4,6},{5,7},{6,4},{7,5}} | collective-permute-start | bytes 1769480 | tf_op jit(solution)/shard_map/ppermute | solution.py:481
  20.8 16.1 %collective-permute-start.1 = (bf16[576,512]{1,0:T(8,128)(2,1)S(1)}, bf16[576,512]{1,0:T(8,128)(2,1)S(1)}, u32[]{:S(2)}, u32[]{:S(2)}) collective-permute-start(bf16[576,512]{1,0:T(8,128)(2,1)S(1)} %get-tuple-element.82), channel_id=1, source_target_pairs={{0,4},{1,5},{2,6},{3,7},{4,0},{5,1},{6,2},{7,3}} | collective-permute-start | bytes 1769480 | tf_op jit(solution)/shard_map/ppermute | solution.py:481
  37.0 16.2 %collective-permute-start.2 = (bf16[576,512]{1,0:T(8,128)(2,1)S(1)}, bf16[576,512]{1,0:T(8,128)(2,1)S(1)}, u32[]{:S(2)}, u32[]{:S(2)}) collective-permute-start(bf16[576,512]{1,0:T(8,128)(2,1)S(1)} %broadcast_select_fusion.3), channel_id=1, source_target_pairs={{0,2},{1,3},{2,0},{3,1},{4,6},{5,7},{6,4},{7,5}} | collective-permute-start | bytes 1769480 | tf_op jit(solution)/shard_map/ppermute | solution.py:481
  37.8 15.3 %collective-permute-start.3 = (bf16[576,512]{1,0:T(8,128)(2,1)S(1)}, bf16[576,512]{1,0:T(8,128)(2,1)S(1)}, u32[]{:S(2)}, u32[]{:S(2)}) collective-permute-start(bf16[576,512]{1,0:T(8,128)(2,1)S(1)} %broadcast_select_fusion.2), channel_id=1, source_target_pairs={{0,4},{1,5},{2,6},{3,7},{4,0},{5,1},{6,2},{7,3}} | collective-permute-start | bytes 1769480 | tf_op jit(solution)/shard_map/ppermute | solution.py:481
  53.3 16.5 %collective-permute-start.4 = (bf16[576,512]{1,0:T(8,128)(2,1)S(1)}, bf16[576,512]{1,0:T(8,128)(2,1)S(1)}, u32[]{:S(2)}, u32[]{:S(2)}) collective-permute-start(bf16[576,512]{1,0:T(8,128)(2,1)S(1)} %get-tuple-element.133), channel_id=1, source_target_pairs={{0,2},{1,3},{2,0},{3,1},{4,6},{5,7},{6,4},{7,5}} | collective-permute-start | bytes 1769480 | tf_op jit(solution)/shard_map/ppermute | solution.py:481
  54.2 15.6 %collective-permute-start.5 = (bf16[576,512]{1,0:T(8,128)(2,1)S(1)}, bf16[576,512]{1,0:T(8,128)(2,1)S(1)}, u32[]{:S(2)}, u32[]{:S(2)}) collective-permute-start(bf16[576,512]{1,0:T(8,128)(2,1)S(1)} %get-tuple-element.134), channel_id=1, source_target_pairs={{0,4},{1,5},{2,6},{3,7},{4,0},{5,1},{6,2},{7,3}} | collective-permute-start | bytes 1769480 | tf_op jit(solution)/shard_map/ppermute | solution.py:481
